TPU v7x, 256 devices: a 8x8x2 block of a 8x8x16 slice. The times are simulated.
256 devices in a mesh: rep: 2 (over z), grp: 8 (over x), tp: 16 (over y, core).
Axes of the slice: x: 8, y: 8, z: 2, core: 2. Of those that a mesh axis runs over, the one named last changes fastest.
The devices are a block of a 8x8x16 slice.
Arguments:
- queries: bfloat16 [1024, 8192], P(('rep', 'grp'), 'tp'), parts along dimension 0, may hold values from -256 to 256
- newest_key_value: bfloat16 [1024, 2, 1024], P(('rep', 'grp')), parts along dimension 0, may hold values from -6 to 6
- kv_pages: bfloat16 [1024, 2, 128, 1024], P(('rep', 'grp', 'tp')), parts along dimension 0, may hold values from -8 to 8
- fetch_slots: int32 [16, 128, 2], P('rep', ('grp', 'tp')), parts along dimension 0, may hold values from -1 to 3, as said below
- block_table: int32 [1024, 8], P(('rep', 'grp')), parts along dimension 0, may hold values from 0 to 255, as said below
- prefix_len: int32 [1024], P(('rep', 'grp')), parts along dimension 0, may hold values from 2 to 1024
- out_weight: bfloat16 [8192, 8192], P('tp'), may hold values from -0.09375 to 0.09375
Outputs:
- attended: bfloat16 [1024, 8192], P(('rep', 'grp'), 'tp'), parts along dimension 0
There are 2 independent parts, one for each index of `rep`. A program takes and returns all parts, laid end to end along the dimension named above; an argument that names none is the same for every part. Nothing has to cross between parts.
Inputs may be any that keep to these rules, and one draw needn't show every extreme that they name: `fetch_slots`: entries of one (group, owner device) are distinct pages of that device's storage; each group takes at most 2 pages from one device, and in every draw some group takes exactly 2 from some device; -1 marks an unused entry, and used entries come first. `block_table`: every entry names a used entry of its group's fetch_slots; requests of a group share their first pages to a varying depth.
All inputs are finite; a program needn't handle non-finite values.
Results may differ from a plain program's by a relative error of at most 0.0057.
Values may be sent and summed in bfloat16 or wider, within the bound.
No kernel may reach another device: no remote copies, remote signals or barrier semaphores. Data moves between devices by JAX's collectives and lax.ppermute only.
A program may use at most 128 MiB of HBM per device.

v0:
```python
import math

import jax
import jax.numpy as jnp
from jax import lax
from jax.experimental import pallas as pl
from jax.experimental.pallas import tpu as pltpu
from jax.sharding import PartitionSpec as P

HEAD_SIZE = 128
PAGE_TOKENS = 128
META_ROWS = 16
LOW = -1e30
CHUNKS = ((0, 1, 7), (2, 6), (3, 5), (4,))
INTERPRET = False


def split3(x):
    hi = x.astype(jnp.bfloat16)
    rest = x - hi.astype(jnp.float32)
    mid = rest.astype(jnp.bfloat16)
    low = (rest - mid.astype(jnp.float32)).astype(jnp.bfloat16)
    return [part.astype(jnp.float32) for part in (hi, mid, low)]


def attend_chunk(stored, named, place, bufs, queries_t, state, shifts, y_count, group_count, pages_dev, per_batch, first, last):
    n_buf = len(bufs)
    rows, cols = queries_t[0].shape
    limit = 2 * n_buf
    factor = math.log2(math.e) / math.sqrt(HEAD_SIZE)

    def kernel(stored_ref, named_ref, place_ref, *refs):
        buf_refs = refs[:n_buf]
        q_refs = refs[n_buf : n_buf + group_count]
        rest = list(refs[n_buf + group_count :])
        if not first:
            acc_in, ml_in = rest[:2]
            rest = rest[2:]
        if last:
            out_refs = rest[:group_count]
            rest = rest[group_count:]
        else:
            acc_out, ml_out = rest[:2]
            rest = rest[2:]
        acc, ml, store, query_all, out_all, item_page, item_slot, sem_store, sem_query, sem_acc, sem_ml, sem_out = rest
        tp_rank = place_ref[0]
        row = place_ref[1]
        core = lax.rem(tp_rank, 2)

        query_copies = [pltpu.make_async_copy(q_refs[g], query_all.at[g], sem_query.at[g]) for g in range(group_count)]
        store_copies = [pltpu.make_async_copy(buf_refs[b], store.at[b], sem_store.at[b]) for b in range(n_buf)]
        if not first:
            ml_copy = pltpu.make_async_copy(ml_in, ml, sem_ml)
            acc_copies = [pltpu.make_async_copy(acc_in.at[g], acc.at[g], sem_acc.at[g]) for g in range(group_count)]
            ml_copy.start()
        for one in store_copies + query_copies:
            one.start()
        if first:
            acc[...] = jnp.zeros(acc.shape, jnp.float32)
            ml[...] = jnp.where(lax.broadcasted_iota(jnp.int32, ml.shape, 1) == 0, LOW, 0.0)
        else:
            for one in acc_copies:
                one.start()
            ml_copy.wait()
            for one in acc_copies:
                one.wait()
        for one in query_copies + store_copies:
            one.wait()

        entry = lax.broadcasted_iota(jnp.int32, (8, cols), 0).astype(jnp.float32)
        token = lax.broadcasted_iota(jnp.int32, (PAGE_TOKENS, cols), 0).astype(jnp.float32)

        def group(g, _):
            number = lax.rem(row + group_count - g, group_count)
            count = jnp.int32(0)
            for b in range(n_buf):
                source_y = lax.rem(lax.div(tp_rank, 2) + y_count - shifts[b // 2], y_count)
                owner = 2 * source_y + (core if b % 2 == 0 else 1 - core)
                for column in range(2):
                    page = stored_ref[(owner * group_count + number) * 2 + column]
                    slot = (row * 2 * y_count + owner) * 2 + column
                    item_page[count] = b * pages_dev + page
                    item_slot[count] = slot
                    used = named_ref[g * (4 * y_count * group_count) + slot]
                    count = count + jnp.where((page >= 0) & (used > 0), 1, 0)
            for pad in range(per_batch):
                item_page[count + pad] = 0
                item_slot[count + pad] = -1

            table = query_all[g, HEAD_SIZE : HEAD_SIZE + 16].astype(jnp.float32)
            length = table[8:9] * 8.0 + table[9:10]
            table = table[0:8]
            live = jnp.clip(length - PAGE_TOKENS * entry, 0.0, 1.0 * PAGE_TOKENS)
            whole = live == PAGE_TOKENS

            def batch(i, _):
                query = query_all[g, 0:HEAD_SIZE]
                old = ml[g, 0:1]
                top = old
                scores, counts = [], []
                for j in range(per_batch):
                    page = item_page[i * per_batch + j]
                    slot = item_slot[i * per_batch + j].astype(jnp.float32)
                    key = store[lax.div(page, pages_dev), lax.rem(page, pages_dev), 0]
                    score = jnp.dot(key, query, preferred_element_type=jnp.float32) * factor
                    match = table == slot
                    full = jnp.sum(jnp.where(match & whole, 1.0, 0.0), axis=0, keepdims=True)
                    part = jnp.max(jnp.where(match & ~whole, live, 0.0), axis=0, keepdims=True)
                    reach = jnp.where(full > 0.0, 1.0 * PAGE_TOKENS, part)
                    score = jnp.where(token < reach, score, LOW)
                    top = jnp.maximum(top, jnp.max(score, axis=0, keepdims=True))
                    scores.append(score)
                    counts.append((full, part))
                shrink = jnp.exp2(old - top)
                total = ml[g, 1:2] * shrink
                update = acc[g] * shrink
                for j in range(per_batch):
                    page = item_page[i * per_batch + j]
                    full, part = counts[j]
                    weight = jnp.exp2(scores[j] - top) * jnp.where(token < part, full + 1.0, full)
                    total = total + jnp.sum(weight, axis=0, keepdims=True)
                    value = store[lax.div(page, pages_dev), lax.rem(page, pages_dev), 1]
                    update = update + lax.dot_general(
                        value, weight.astype(jnp.bfloat16), (((0,), (0,)), ((), ())), preferred_element_type=jnp.float32
                    )
                acc[g] = update
                ml[g, 0:1] = top
                ml[g, 1:2] = total
                return 0

            lax.fori_loop(0, lax.div(count + per_batch - 1, per_batch), batch, 0)

            if last:
                top = ml[g, 0:1]
                total = ml[g, 1:2]
                inverse = jnp.where(total > 0.0, 1.0 / jnp.where(total > 0.0, total, 1.0), 0.0)
                out_all[g, 0:HEAD_SIZE] = (acc[g] * inverse).astype(jnp.bfloat16)
                sub = lax.broadcasted_iota(jnp.int32, (META_ROWS, cols), 0)
                packed = jnp.zeros((META_ROWS, cols), jnp.float32)
                for n, part in enumerate(split3(top) + split3(total)):
                    packed = jnp.where(sub == n, part, packed)
                out_all[g, HEAD_SIZE:] = packed.astype(jnp.bfloat16)
            return 0

        lax.fori_loop(0, group_count, group, 0)
        if last:
            out_copies = [pltpu.make_async_copy(out_all.at[g], out_refs[g], sem_out.at[g]) for g in range(group_count)]
        else:
            out_copies = [pltpu.make_async_copy(acc.at[g], acc_out.at[g], sem_out.at[g]) for g in range(group_count)]
            out_copies.append(pltpu.make_async_copy(ml, ml_out, sem_ml))
        for one in out_copies:
            one.start()
        for one in out_copies:
            one.wait()

    if last:
        out_shape = [jax.ShapeDtypeStruct((HEAD_SIZE + META_ROWS, cols), jnp.bfloat16)] * group_count
        aliases = {}
    else:
        out_shape = [
            jax.ShapeDtypeStruct((group_count, HEAD_SIZE, cols), jnp.float32),
            jax.ShapeDtypeStruct((group_count, 8, cols), jnp.float32),
        ]
        aliases = {} if first else {3 + n_buf + group_count: 0, 3 + n_buf + group_count + 1: 1}
    n_out_slots = group_count if last else 1
    scratch = [
        pltpu.VMEM((group_count, HEAD_SIZE, cols), jnp.float32),
        pltpu.VMEM((group_count, 8, cols), jnp.float32),
        pltpu.VMEM((n_buf, pages_dev, 2, PAGE_TOKENS, HEAD_SIZE), jnp.bfloat16),
        pltpu.VMEM((group_count, rows, cols), jnp.bfloat16),
        pltpu.VMEM((n_out_slots, HEAD_SIZE + META_ROWS, cols), jnp.bfloat16),
        pltpu.SMEM((limit + per_batch,), jnp.int32),
        pltpu.SMEM((limit + per_batch,), jnp.int32),
        pltpu.SemaphoreType.DMA((n_buf,)),
        pltpu.SemaphoreType.DMA((group_count,)),
        pltpu.SemaphoreType.DMA((group_count,)),
        pltpu.SemaphoreType.DMA,
        pltpu.SemaphoreType.DMA((group_count,)),
    ]
    anywhere = pl.BlockSpec(memory_space=pltpu.MemorySpace.HBM)
    n_in = n_buf + group_count + (0 if first else 2)
    return pl.pallas_call(
        kernel,
        out_shape=out_shape,
        grid_spec=pltpu.PrefetchScalarGridSpec(
            num_scalar_prefetch=3,
            grid=(),
            in_specs=[anywhere] * n_in,
            out_specs=[anywhere] * len(out_shape),
            scratch_shapes=scratch,
        ),
        input_output_aliases=aliases,
        interpret=INTERPRET,
    )(stored, named, place, *bufs, *queries_t, *(() if first else state))


def combine(arrived, query_t, newest_t, heads_dev):
    parts = len(arrived)
    cols = arrived[0].shape[1]
    req_rows = cols // heads_dev
    factor = math.log2(math.e) / math.sqrt(HEAD_SIZE)

    def kernel(*refs):
        in_refs = refs[:parts]
        q_ref, new_ref, out_ref = refs[parts:]
        query = q_ref[0:HEAD_SIZE].astype(jnp.float32)
        own = jnp.sum(query * new_ref[0].astype(jnp.float32), axis=0, keepdims=True) * factor
        top = own
        tops, totals = [], []
        for n in range(parts):
            packed = in_refs[n][HEAD_SIZE:].astype(jnp.float32)
            tops.append(packed[0:1] + packed[1:2] + packed[2:3])
            totals.append(packed[3:4] + packed[4:5] + packed[5:6])
            top = jnp.maximum(top, tops[-1])
        own_weight = jnp.exp2(own - top)
        denominator = own_weight
        scales = []
        for n in range(parts):
            scales.append(totals[n] * jnp.exp2(tops[n] - top))
            denominator = denominator + scales[-1]
        inverse = 1.0 / denominator
        mix = new_ref[1].astype(jnp.float32) * (own_weight * inverse)
        for n in range(parts):
            mix = mix + in_refs[n][0:HEAD_SIZE].astype(jnp.float32) * (scales[n] * inverse)
        for h in range(heads_dev):
            one = mix[:, h * req_rows : (h + 1) * req_rows]
            out_ref[:, h * HEAD_SIZE : (h + 1) * HEAD_SIZE] = one.T.astype(jnp.bfloat16)

    return pl.pallas_call(
        kernel,
        out_shape=jax.ShapeDtypeStruct((req_rows, heads_dev * HEAD_SIZE), jnp.bfloat16),
        interpret=INTERPRET,
        name="combine",
    )(*arrived, query_t, newest_t)


def project(place, mix_own, mix_partner, weight_own, weight_partner, y_count):
    width = weight_own.shape[1] // (2 * y_count)
    req_rows, depth = mix_own.shape

    def kernel(place_ref, own_ref, partner_ref, w_own_ref, w_partner_ref, *out_refs):
        total = jnp.dot(own_ref[...], w_own_ref[...], preferred_element_type=jnp.float32)
        total = total + jnp.dot(partner_ref[...], w_partner_ref[...], preferred_element_type=jnp.float32)
        total = total.astype(jnp.bfloat16)
        for n in range(y_count):

            @pl.when(pl.program_id(0) == n)
            def _():
                out_refs[n][...] = total

    def column(n, place):
        rank = place[0]
        return (0, 2 * lax.rem(lax.div(rank, 2) + n, y_count) + lax.rem(rank, 2))

    mix_spec = pl.BlockSpec((req_rows, depth), lambda n, place: (0, 0))
    return pl.pallas_call(
        kernel,
        out_shape=[jax.ShapeDtypeStruct((req_rows, width), jnp.bfloat16)] * y_count,
        grid_spec=pltpu.PrefetchScalarGridSpec(
            num_scalar_prefetch=1,
            grid=(y_count,),
            in_specs=[mix_spec, mix_spec, pl.BlockSpec((depth, width), column), pl.BlockSpec((depth, width), column)],
            out_specs=[pl.BlockSpec((req_rows, width), lambda n, place: (0, 0))] * y_count,
        ),
        interpret=INTERPRET,
        name="project",
    )(place, mix_own, mix_partner, weight_own, weight_partner)


def per_device_inner(
    queries, newest_key_value, kv_pages, fetch_slots, block_table, prefix_len, out_weight
):
    tp_count = lax.axis_size("tp")
    group_count = lax.axis_size("grp")
    y_count = tp_count // 2
    tp_rank = lax.axis_index("tp").astype(jnp.int32)
    row = lax.axis_index("grp").astype(jnp.int32)
    y = lax.div(tp_rank, 2)
    req_rows = queries.shape[0]
    heads_dev = queries.shape[1] // HEAD_SIZE
    pages_dev = kv_pages.shape[0]
    list_length = block_table.shape[1]
    cols = heads_dev * req_rows
    slots = 2 * tp_count * group_count
    swap = [(i, i ^ 1) for i in range(tp_count)]

    def along_y(x, shift):
        return lax.ppermute(x, "tp", [(i, (i + 2 * shift) % tp_count) for i in range(tp_count)])

    def along_x(x, shift):
        return lax.ppermute(x, "grp", [(i, (i + shift) % group_count) for i in range(group_count)])

    def to_other_core(x):
        return lax.ppermute(x, "tp", swap)

    own, partner = {}, {}
    for shift in [s for chunk in CHUNKS for s in chunk]:
        head = lax.rem(y + shift, y_count)
        piece = lax.dynamic_slice_in_dim(kv_pages, head * HEAD_SIZE, HEAD_SIZE, 3)
        own[shift] = along_y(piece, shift) if shift else piece

    query_t = jnp.transpose(queries.reshape(req_rows, heads_dev, HEAD_SIZE), (2, 1, 0)).reshape(HEAD_SIZE, cols)
    table_t = block_table.T
    live = PAGE_TOKENS * jnp.arange(list_length)[:, None] < prefix_len[None, :]
    alive = jnp.where(live, table_t, -1)
    named = jnp.any(alive[:, :, None] == jnp.arange(slots)[None, None, :], axis=(0, 1)).astype(jnp.bfloat16)
    named = jnp.pad(named, (0, cols - slots))[None]
    meta = jnp.concatenate([table_t, (prefix_len // 8)[None], (prefix_len % 8)[None]], axis=0)
    meta = jnp.tile(meta.astype(jnp.bfloat16), (1, heads_dev))
    fill = jnp.zeros((META_ROWS - list_length - 3, cols), jnp.bfloat16)
    query_t = jnp.concatenate([query_t, meta, named, fill], axis=0)
    queries_t = [along_x(query_t, s) if s else query_t for s in range(group_count)]

    stored = jnp.where(jnp.arange(tp_count)[:, None] == tp_rank, fetch_slots.reshape(1, -1), 0)
    bit = 1
    while bit < tp_count:
        stored = stored + lax.ppermute(stored, "tp", [(i, i ^ bit) for i in range(tp_count)])
        bit *= 2
    stored = stored.reshape(-1)

    for shift in own:
        partner[shift] = to_other_core(own[shift])
    weight_partner = to_other_core(out_weight)

    named_at = HEAD_SIZE + list_length + 2
    named_all = jnp.concatenate([q[named_at : named_at + 1, :slots] for q in queries_t], axis=0)
    named_all = named_all.astype(jnp.int32).reshape(-1)
    place = jnp.stack([tp_rank, row])

    newest = lax.dynamic_slice_in_dim(newest_key_value, y * HEAD_SIZE, HEAD_SIZE, 2)
    newest_t = jnp.tile(jnp.transpose(newest, (1, 2, 0)), (1, 1, heads_dev))

    state = ()
    for n, shifts in enumerate(CHUNKS):
        bufs = [b for s in shifts for b in (own[s], partner[s])]
        last = n == len(CHUNKS) - 1
        state = attend_chunk(
            stored, named_all, place, bufs, queries_t, state, shifts, y_count, group_count, pages_dev, 2 if last else 4, n == 0, last
        )
    arrived = [along_x(state[s], -s) if s else state[s] for s in range(group_count)]

    mix_own = combine(arrived, query_t, newest_t, heads_dev)
    mix_partner = to_other_core(mix_own)
    partial = project(place, mix_own, mix_partner, out_weight, weight_partner, y_count)
    arrived = [along_y(partial[s], s) if s else partial[s] for s in range(y_count)]
    return sum(one.astype(jnp.float32) for one in arrived).astype(jnp.bfloat16)


def solution(mesh):
    in_specs = (
        P(("rep", "grp"), "tp"),
        P(("rep", "grp"), None, None),
        P(("rep", "grp", "tp"), None, None, None),
        P("rep", ("grp", "tp"), None),
        P(("rep", "grp"), None),
        P(("rep", "grp")),
        P("tp", None),
    )
    out_specs = P(("rep", "grp"), "tp")
    return jax.shard_map(per_device_inner, mesh=mesh, in_specs=in_specs, out_specs=out_specs, check_vma=False)
```

profile of v0, /device:TPU:513, one launch (start us, length us, event | category | flops | bytes accessed | tf_op | source)
XLA Modules:
  0.0 211.1 jit_solution(10388776597941319166)
XLA Ops:
  0.0 20.4 %collective-permute-start.34 = (bf16[512,8192]{1,0:T(8,128)(2,1)}, bf16[512,8192]{1,0:T(8,128)(2,1)}, u32[]{:S(2)}, u32[]{:S(2)}) collective-permute-start(bf16[512,8192]{1,0:T(8,128)(2,1)} %w_own_ref.1), channel_id=1, source_target_pairs={{0,1},{1,0},{2,3},{3,2},{4,5},{5,4},{6,7},{7,6},{8,9},{9,8},{10,11... | collective-permute-start | bytes 25165832 | tf_op jit(solution)/shard_map/ppermute | solution.py:294
  25.5 8.1 %collective-permute-done = s32[16,16]{1,0:T(8,128)S(1)} collective-permute-done((s32[16,16]{1,0:T(8,128)S(1)}, s32[16,16]{1,0:T(8,128)S(1)}, u32[]{:S(2)}, u32[]{:S(2)}) %collective-permute-start) | collective-permute-done | bytes 1056 | tf_op jit(solution)/shard_map/ppermute | solution.py:317
  33.7 2.4 %collective-permute-done.1 = s32[16,16]{1,0:T(8,128)S(1)} collective-permute-done((s32[16,16]{1,0:T(8,128)S(1)}, s32[16,16]{1,0:T(8,128)S(1)}, u32[]{:S(2)}, u32[]{:S(2)}) %collective-permute-start.1) | collective-permute-done | bytes 1056 | tf_op jit(solution)/shard_map/ppermute | solution.py:317
  36.4 3.4 %collective-permute-done.2 = s32[16,16]{1,0:T(8,128)S(1)} collective-permute-done((s32[16,16]{1,0:T(8,128)S(1)}, s32[16,16]{1,0:T(8,128)S(1)}, u32[]{:S(2)}, u32[]{:S(2)}) %collective-permute-start.2) | collective-permute-done | bytes 1056 | tf_op jit(solution)/shard_map/ppermute | solution.py:317
  39.7 6.4 %collective-permute-done.3 = s32[16,16]{1,0:T(8,128)S(1)} collective-permute-done((s32[16,16]{1,0:T(8,128)S(1)}, s32[16,16]{1,0:T(8,128)S(1)}, u32[]{:S(2)}, u32[]{:S(2)}) %collective-permute-start.3) | collective-permute-done | bytes 1056 | tf_op jit(solution)/shard_map/ppermute | solution.py:317
  48.2 2.3 %collective-permute-start.17 = (bf16[4,2,128,128]{3,2,1,0:T(8,128)(2,1)S(1)}, bf16[4,2,128,128]{3,2,1,0:T(8,128)(2,1)S(1)}, u32[]{:S(2)}, u32[]{:S(2)}) collective-permute-start(bf16[4,2,128,128]{3,2,1,0:T(8,128)(2,1)S(1)} %get-tuple-element.52), channel_id=1, source_target_pairs={{0,4},{1,5},{2,6},{3,7},{4,8},{5,9},{6,10},{7,11},{8,12},{9,13},{1... | collective-permute-start | bytes 786440 | tf_op jit(solution)/shard_map/ppermute | solution.py:288
  50.5 2.9 %collective-permute-done.7.refs_10_.refs_8_.refs_6_ = bf16[144,256]{1,0:T(8,128)(2,1)S(1)} collective-permute-done((bf16[144,256]{1,0:T(8,128)(2,1)S(1)}, bf16[144,256]{1,0:T(8,128)(2,1)S(1)}, u32[]{:S(2)}, u32[]{:S(2)}) %collective-permute-start.7) | collective-permute-done | bytes 73760 | tf_op jit(solution)/shard_map/ppermute | solution.py:291
  53.4 7.1 %collective-permute-done.6.refs_9_.refs_7_.refs_5_ = bf16[144,256]{1,0:T(8,128)(2,1)S(1)} collective-permute-done((bf16[144,256]{1,0:T(8,128)(2,1)S(1)}, bf16[144,256]{1,0:T(8,128)(2,1)S(1)}, u32[]{:S(2)}, u32[]{:S(2)}) %collective-permute-start.6) | collective-permute-done | bytes 73760 | tf_op jit(solution)/shard_map/ppermute | solution.py:291
  60.5 6.0 %collective-permute-done.5.refs_8_.refs_6_.refs_4_ = bf16[144,256]{1,0:T(8,128)(2,1)S(1)} collective-permute-done((bf16[144,256]{1,0:T(8,128)(2,1)S(1)}, bf16[144,256]{1,0:T(8,128)(2,1)S(1)}, u32[]{:S(2)}, u32[]{:S(2)}) %collective-permute-start.5) | collective-permute-done | bytes 73760 | tf_op jit(solution)/shard_map/ppermute | solution.py:291
  66.6 4.4 %collective-permute-done.4.refs_7_.refs_5_.refs_3_ = bf16[144,256]{1,0:T(8,128)(2,1)S(1)} collective-permute-done((bf16[144,256]{1,0:T(8,128)(2,1)S(1)}, bf16[144,256]{1,0:T(8,128)(2,1)S(1)}, u32[]{:S(2)}, u32[]{:S(2)}) %collective-permute-start.4) | collective-permute-done | bytes 73760 | tf_op jit(solution)/shard_map/ppermute | solution.py:291
  71.0 3.3 %collective-permute-start.13 = (bf16[4,2,128,128]{3,2,1,0:T(8,128)(2,1)S(1)}, bf16[4,2,128,128]{3,2,1,0:T(8,128)(2,1)}, u32[]{:S(2)}, u32[]{:S(2)}) collective-permute-start(bf16[4,2,128,128]{3,2,1,0:T(8,128)(2,1)S(1)} %get-tuple-element.54), channel_id=1, source_target_pairs={{0,6},{1,7},{2,8},{3,9},{4,10},{5,11},{6,12},{7,13},{8,14},{9,15},... | collective-permute-start | bytes 786440 | tf_op jit(solution)/shard_map/ppermute | solution.py:288
  76.8 5.7 %collective-permute-done.15.refs_2_ = bf16[4,2,128,128]{3,2,1,0:T(8,128)(2,1)} collective-permute-done((bf16[4,2,128,128]{3,2,1,0:T(8,128)(2,1)S(1)}, bf16[4,2,128,128]{3,2,1,0:T(8,128)(2,1)}, u32[]{:S(2)}, u32[]{:S(2)}) %collective-permute-start.15) | collective-permute-done | bytes 262176 | tf_op jit(solution)/shard_map/ppermute | solution.py:288
  82.5 12.6 %collective-permute-start.21 = (bf16[4,2,128,128]{3,2,1,0:T(8,128)(2,1)S(1)}, bf16[4,2,128,128]{3,2,1,0:T(8,128)(2,1)S(1)}, u32[]{:S(2)}, u32[]{:S(2)}) collective-permute-start(bf16[4,2,128,128]{3,2,1,0:T(8,128)(2,1)S(1)} %get-tuple-element.50.refs_0_), channel_id=1, source_target_pairs={{0,1},{1,0},{2,3},{3,2},{4,5},{5,4},{6,7},{7,6},{8,9},{9,8},{10,11... | collective-permute-start | bytes 786440 | tf_op jit(solution)/shard_map/ppermute | solution.py:294
  95.1 7.9 %collective-permute-start.25 = (bf16[4,2,128,128]{3,2,1,0:T(8,128)(2,1)S(1)}, bf16[4,2,128,128]{3,2,1,0:T(8,128)(2,1)S(1)}, u32[]{:S(2)}, u32[]{:S(2)}) collective-permute-start(bf16[4,2,128,128]{3,2,1,0:T(8,128)(2,1)S(1)} %collective-permute-done.24.refs_4_), channel_id=1, source_target_pairs={{0,1},{1,0},{2,3},{3,2},{4,5},{5,4},{6,7},{7,6},{8,9},{9,8},{10,11... | collective-permute-start | bytes 786440 | tf_op jit(solution)/shard_map/ppermute | solution.py:294
  103.1 3.2 %collective-permute-start.20 = (bf16[4,2,128,128]{3,2,1,0:T(8,128)(2,1)S(1)}, bf16[4,2,128,128]{3,2,1,0:T(8,128)(2,1)S(1)}, u32[]{:S(2)}, u32[]{:S(2)}) collective-permute-start(bf16[4,2,128,128]{3,2,1,0:T(8,128)(2,1)S(1)} %collective-permute-done.19.refs_2_), channel_id=1, source_target_pairs={{0,1},{1,0},{2,3},{3,2},{4,5},{5,4},{6,7},{7,6},{8,9},{9,8},{10,11... | collective-permute-start | bytes 786440 | tf_op jit(solution)/shard_map/ppermute | solution.py:294
  108.3 2.9 %collective-permute-start.23 = (bf16[4,2,128,128]{3,2,1,0:T(8,128)(2,1)S(1)}, bf16[4,2,128,128]{3,2,1,0:T(8,128)(2,1)S(1)}, u32[]{:S(2)}, u32[]{:S(2)}) collective-permute-start(bf16[4,2,128,128]{3,2,1,0:T(8,128)(2,1)S(1)} %collective-permute-done.22.refs_2_), channel_id=1, source_target_pairs={{0,1},{1,0},{2,3},{3,2},{4,5},{5,4},{6,7},{7,6},{8,9},{9,8},{10,11... | collective-permute-start | bytes 786440 | tf_op jit(solution)/shard_map/ppermute | solution.py:294
  114.9 10.8 %shard_map.73 = (f32[8,128,256]{2,1,0:T(8,128)}, f32[8,8,256]{2,1,0:T(8,128)}) custom-call(s32[256]{0:T(256)} %reshape.69.stored_ref, s32[2048]{0:T(1024)} %bitcast.22, s32[2]{0:T(128)} %pad_add_fusion.place_ref, bf16[4,2,128,128]{3,2,1,0:T(8,128)(2,1)} %copy-done.9, bf16[4,2,128,128]{3,2,1,0:T(8,128)(2,1)} %copy-done.13, ...), custom_call_target="tpu_custom_call" | custom-call | tf_op jit(solution)/shard_map/pallas_call | solution.py:182
  125.8 8.5 %shard_map.74 = (f32[8,128,256]{2,1,0:T(8,128)}, f32[8,8,256]{2,1,0:T(8,128)}) custom-call(s32[256]{0:T(256)} %reshape.69.stored_ref, s32[2048]{0:T(1024)} %bitcast.23, s32[2]{0:T(128)} %pad_add_fusion.place_ref, bf16[4,2,128,128]{3,2,1,0:T(8,128)(2,1)} %copy-done.18, ...), custom_call_target="tpu_custom_call", output_to_operand_aliasing={{0}: (15, {}), {1}: (16, {})} | custom-call | tf_op jit(solution)/shard_map/pallas_call | solution.py:182
  134.4 10.3 %shard_map.75 = (f32[8,128,256]{2,1,0:T(8,128)}, f32[8,8,256]{2,1,0:T(8,128)}) custom-call(s32[256]{0:T(256)} %reshape.69.stored_ref, s32[2048]{0:T(1024)} %bitcast.24, s32[2]{0:T(128)} %pad_add_fusion.place_ref, bf16[4,2,128,128]{3,2,1,0:T(8,128)(2,1)} %collective-permute-done.13.refs_0_, ...), custom_call_target="tpu_custom_call", output_to_operand_aliasing={{0}: (15, {}), {1}: (16, {})} | custom-call | tf_op jit(solution)/shard_map/pallas_call | solution.py:182
  145.5 7.2 %shard_map.76 = (bf16[144,256]{1,0:T(8,128)(2,1)}, bf16[144,256]{1,0:T(8,128)(2,1)}, bf16[144,256]{1,0:T(8,128)(2,1)}, bf16[144,256]{1,0:T(8,128)(2,1)}, bf16[14...) custom-call(s32[256]{0:T(256)} %reshape.69.stored_ref, ...), custom_call_target="tpu_custom_call" | custom-call | tf_op jit(solution)/shard_map/pallas_call | solution.py:182
  152.8 3.2 %collective-permute-start.27 = (bf16[144,256]{1,0:T(8,128)(2,1)}, bf16[144,256]{1,0:T(8,128)(2,1)S(1)}, u32[]{:S(2)}, u32[]{:S(2)}) collective-permute-start(bf16[144,256]{1,0:T(8,128)(2,1)} %get-tuple-element.35), channel_id=1, source_target_pairs={{0,96},{16,112},{32,0},{48,16},{64,32},{80,48},{96,64},{112,80},{1... | collective-permute-start | bytes 221192 | tf_op jit(solution)/shard_map/ppermute | solution.py:291
  155.9 2.5 %collective-permute-start.29 = (bf16[144,256]{1,0:T(8,128)(2,1)}, bf16[144,256]{1,0:T(8,128)(2,1)S(1)}, u32[]{:S(2)}, u32[]{:S(2)}) collective-permute-start(bf16[144,256]{1,0:T(8,128)(2,1)} %get-tuple-element.37), channel_id=1, source_target_pairs={{0,64},{16,80},{32,96},{48,112},{64,0},{80,16},{96,32},{112,48},{1... | collective-permute-start | bytes 221192 | tf_op jit(solution)/shard_map/ppermute | solution.py:291
  158.4 3.1 %collective-permute-start.30 = (bf16[144,256]{1,0:T(8,128)(2,1)}, bf16[144,256]{1,0:T(8,128)(2,1)S(1)}, u32[]{:S(2)}, u32[]{:S(2)}) collective-permute-start(bf16[144,256]{1,0:T(8,128)(2,1)} %get-tuple-element.38), channel_id=1, source_target_pairs={{0,48},{16,64},{32,80},{48,96},{64,112},{80,0},{96,16},{112,32},{1... | collective-permute-start | bytes 221192 | tf_op jit(solution)/shard_map/ppermute | solution.py:291
  161.5 2.2 %collective-permute-start.31 = (bf16[144,256]{1,0:T(8,128)(2,1)}, bf16[144,256]{1,0:T(8,128)(2,1)S(1)}, u32[]{:S(2)}, u32[]{:S(2)}) collective-permute-start(bf16[144,256]{1,0:T(8,128)(2,1)} %get-tuple-element.39), channel_id=1, source_target_pairs={{0,32},{16,48},{32,64},{48,80},{64,96},{80,112},{96,0},{112,16},{1... | collective-permute-start | bytes 221192 | tf_op jit(solution)/shard_map/ppermute | solution.py:291
  166.9 5.6 %collective-permute-done.31.refs_6_ = bf16[144,256]{1,0:T(8,128)(2,1)S(1)} collective-permute-done((bf16[144,256]{1,0:T(8,128)(2,1)}, bf16[144,256]{1,0:T(8,128)(2,1)S(1)}, u32[]{:S(2)}, u32[]{:S(2)}) %collective-permute-start.31) | collective-permute-done | bytes 73760 | tf_op jit(solution)/shard_map/ppermute | solution.py:291
  172.5 2.8 %collective-permute-done.32.refs_7_ = bf16[144,256]{1,0:T(8,128)(2,1)S(1)} collective-permute-done((bf16[144,256]{1,0:T(8,128)(2,1)}, bf16[144,256]{1,0:T(8,128)(2,1)S(1)}, u32[]{:S(2)}, u32[]{:S(2)}) %collective-permute-start.32) | collective-permute-done | bytes 73760 | tf_op jit(solution)/shard_map/ppermute | solution.py:291
  175.9 2.1 %combine.1.own_ref = bf16[64,512]{1,0:T(8,128)(2,1)} custom-call(bf16[144,256]{1,0:T(8,128)(2,1)} %get-tuple-element.33.refs_0_, bf16[144,256]{1,0:T(8,128)(2,1)} %copy-done.20, bf16[144,256]{1,0:T(8,128)(2,1)} %copy-done.21, bf16[144,256]{1,0:T(8,128)(2,1)} %copy-done.22, bf16[144,256]{1,0:T(8,128)(2,1)} %copy-done.23, bf16[144,256]{1,0:T(8,128)(2,1)} %copy-done.24, ...), custom_call_target="tpu_custom_call" | custom-call | tf_op jit(solution)/shard_map/combine/pallas_call | solution.py:229
  180.3 8.3 %project.1 = (bf16[64,512]{1,0:T(8,128)(2,1)}, bf16[64,512]{1,0:T(8,128)(2,1)}, bf16[64,512]{1,0:T(8,128)(2,1)}, bf16[64,512]{1,0:T(8,128)(2,1)}, bf16[64,512]{1...) custom-call(s32[2]{0:T(128)} %pad_add_fusion.place_ref, ...), custom_call_target="tpu_custom_call" | custom-call | tf_op jit(solution)/shard_map/project/pallas_call | solution.py:256
  189.2 2.6 %collective-permute-start.36 = (bf16[64,512]{1,0:T(8,128)(2,1)}, bf16[64,512]{1,0:T(8,128)(2,1)S(1)}, u32[]{:S(2)}, u32[]{:S(2)}) collective-permute-start(bf16[64,512]{1,0:T(8,128)(2,1)} %get-tuple-element.43), channel_id=1, source_target_pairs={{0,4},{1,5},{2,6},{3,7},{4,8},{5,9},{6,10},{7,11},{8,12},{9,13},{1... | collective-permute-start | bytes 196616 | tf_op jit(solution)/shard_map/ppermute | solution.py:288
  191.7 2.3 %collective-permute-start.37 = (bf16[64,512]{1,0:T(8,128)(2,1)}, bf16[64,512]{1,0:T(8,128)(2,1)S(1)}, u32[]{:S(2)}, u32[]{:S(2)}) collective-permute-start(bf16[64,512]{1,0:T(8,128)(2,1)} %get-tuple-element.44), channel_id=1, source_target_pairs={{0,6},{1,7},{2,8},{3,9},{4,10},{5,11},{6,12},{7,13},{8,14},{9,15},... | collective-permute-start | bytes 196616 | tf_op jit(solution)/shard_map/ppermute | solution.py:288
  195.3 3.0 %collective-permute-start.39 = (bf16[64,512]{1,0:T(8,128)(2,1)}, bf16[64,512]{1,0:T(8,128)(2,1)S(1)}, u32[]{:S(2)}, u32[]{:S(2)}) collective-permute-start(bf16[64,512]{1,0:T(8,128)(2,1)} %get-tuple-element.46), channel_id=1, source_target_pairs={{0,10},{1,11},{2,12},{3,13},{4,14},{5,15},{6,0},{7,1},{8,2},{9,3},... | collective-permute-start | bytes 196616 | tf_op jit(solution)/shard_map/ppermute | solution.py:288
  201.9 6.8 %collective-permute-done.40 = bf16[64,512]{1,0:T(8,128)(2,1)S(1)} collective-permute-done((bf16[64,512]{1,0:T(8,128)(2,1)}, bf16[64,512]{1,0:T(8,128)(2,1)S(1)}, u32[]{:S(2)}, u32[]{:S(2)}) %collective-permute-start.40) | collective-permute-done | bytes 65568 | tf_op jit(solution)/shard_map/ppermute | solution.py:288
  (156 shorter events, 30.1 us)
Async XLA Ops:
  0.0 179.7 %collective-permute-start.34 = (bf16[512,8192]{1,0:T(8,128)(2,1)}, bf16[512,8192]{1,0:T(8,128)(2,1)}, u32[]{:S(2)}, u32[]{:S(2)}) collective-permute-start(bf16[512,8192]{1,0:T(8,128)(2,1)} %w_own_ref.1), channel_id=1, source_target_pairs={{0,1},{1,0},{2,3},{3,2},{4,5},{5,4},{6,7},{7,6},{8,9},{9,8},{10,11... | collective-permute-start | bytes 25165832 | tf_op jit(solution)/shard_map/ppermute | solution.py:294
  24.0 23.8 %collective-permute-start.10 = (bf16[144,256]{1,0:T(8,128)(2,1)S(1)}, bf16[144,256]{1,0:T(8,128)(2,1)S(1)}, u32[]{:S(2)}, u32[]{:S(2)}) collective-permute-start(bf16[144,256]{1,0:T(8,128)(2,1)S(1)} %maximum_maximum_fusion.refs_6_.refs_4_.refs_2_.refs_8_), channel_id=1, source_target_pairs={{0,112},{16,0},{32,16},{48,32},{64,48},{80,64},{96,80},{112,96},{1... | collective-permute-start | bytes 221192 | tf_op jit(solution)/shard_map/ppermute | solution.py:291
  24.2 23.9 %collective-permute-start.9 = (bf16[144,256]{1,0:T(8,128)(2,1)S(1)}, bf16[144,256]{1,0:T(8,128)(2,1)S(1)}, u32[]{:S(2)}, u32[]{:S(2)}) collective-permute-start(bf16[144,256]{1,0:T(8,128)(2,1)S(1)} %maximum_maximum_fusion.refs_6_.refs_4_.refs_2_.refs_8_), channel_id=1, source_target_pairs={{0,96},{16,112},{32,0},{48,16},{64,32},{80,48},{96,64},{112,80},{1... | collective-permute-start | bytes 221192 | tf_op jit(solution)/shard_map/ppermute | solution.py:291
  24.3 23.9 %collective-permute-start.8 = (bf16[144,256]{1,0:T(8,128)(2,1)S(1)}, bf16[144,256]{1,0:T(8,128)(2,1)S(1)}, u32[]{:S(2)}, u32[]{:S(2)}) collective-permute-start(bf16[144,256]{1,0:T(8,128)(2,1)S(1)} %maximum_maximum_fusion.refs_6_.refs_4_.refs_2_.refs_8_), channel_id=1, source_target_pairs={{0,80},{16,96},{32,112},{48,0},{64,16},{80,32},{96,48},{112,64},{1... | collective-permute-start | bytes 221192 | tf_op jit(solution)/shard_map/ppermute | solution.py:291
  25.4 8.2 %collective-permute-start = (s32[16,16]{1,0:T(8,128)S(1)}, s32[16,16]{1,0:T(8,128)S(1)}, u32[]{:S(2)}, u32[]{:S(2)}) collective-permute-start(s32[16,16]{1,0:T(8,128)S(1)} %broadcast_select_fusion), channel_id=1, source_target_pairs={{0,1},{1,0},{2,3},{3,2},{4,5},{5,4},{6,7},{7,6},{8,9},{9,8},{10,11... | collective-permute-start | bytes 3080 | tf_op jit(solution)/shard_map/ppermute | solution.py:317
  46.1 7.3 %collective-permute-start.7 = (bf16[144,256]{1,0:T(8,128)(2,1)S(1)}, bf16[144,256]{1,0:T(8,128)(2,1)S(1)}, u32[]{:S(2)}, u32[]{:S(2)}) collective-permute-start(bf16[144,256]{1,0:T(8,128)(2,1)S(1)} %maximum_maximum_fusion.refs_6_.refs_4_.refs_2_.refs_8_), channel_id=1, source_target_pairs={{0,64},{16,80},{32,96},{48,112},{64,0},{80,16},{96,32},{112,48},{1... | collective-permute-start | bytes 221192 | tf_op jit(solution)/shard_map/ppermute | solution.py:291
  47.9 23.1 %collective-permute-start.24 = (bf16[4,2,128,128]{3,2,1,0:T(8,128)(2,1)S(1)}, bf16[4,2,128,128]{3,2,1,0:T(8,128)(2,1)S(1)}, u32[]{:S(2)}, u32[]{:S(2)}) collective-permute-start(bf16[4,2,128,128]{3,2,1,0:T(8,128)(2,1)S(1)} %get-tuple-element.49), channel_id=1, source_target_pairs={{0,14},{1,15},{2,0},{3,1},{4,2},{5,3},{6,4},{7,5},{8,6},{9,7},{10,... | collective-permute-start | bytes 786440 | tf_op jit(solution)/shard_map/ppermute | solution.py:288
  48.0 26.2 %collective-permute-start.19 = (bf16[4,2,128,128]{3,2,1,0:T(8,128)(2,1)S(1)}, bf16[4,2,128,128]{3,2,1,0:T(8,128)(2,1)S(1)}, u32[]{:S(2)}, u32[]{:S(2)}) collective-permute-start(bf16[4,2,128,128]{3,2,1,0:T(8,128)(2,1)S(1)} %get-tuple-element.51), channel_id=1, source_target_pairs={{0,12},{1,13},{2,14},{3,15},{4,0},{5,1},{6,2},{7,3},{8,4},{9,5},{1... | collective-permute-start | bytes 786440 | tf_op jit(solution)/shard_map/ppermute | solution.py:288
  48.2 27.6 %collective-permute-start.17 = (bf16[4,2,128,128]{3,2,1,0:T(8,128)(2,1)S(1)}, bf16[4,2,128,128]{3,2,1,0:T(8,128)(2,1)S(1)}, u32[]{:S(2)}, u32[]{:S(2)}) collective-permute-start(bf16[4,2,128,128]{3,2,1,0:T(8,128)(2,1)S(1)} %get-tuple-element.52), channel_id=1, source_target_pairs={{0,4},{1,5},{2,6},{3,7},{4,8},{5,9},{6,10},{7,11},{8,12},{9,13},{1... | collective-permute-start | bytes 786440 | tf_op jit(solution)/shard_map/ppermute | solution.py:288
  71.0 11.5 %collective-permute-start.15 = (bf16[4,2,128,128]{3,2,1,0:T(8,128)(2,1)S(1)}, bf16[4,2,128,128]{3,2,1,0:T(8,128)(2,1)}, u32[]{:S(2)}, u32[]{:S(2)}) collective-permute-start(bf16[4,2,128,128]{3,2,1,0:T(8,128)(2,1)S(1)} %get-tuple-element.53), channel_id=1, source_target_pairs={{0,10},{1,11},{2,12},{3,13},{4,14},{5,15},{6,0},{7,1},{8,2},{9,3},... | collective-permute-start | bytes 786440 | tf_op jit(solution)/shard_map/ppermute | solution.py:288
  71.0 24.1 %collective-permute-start.13 = (bf16[4,2,128,128]{3,2,1,0:T(8,128)(2,1)S(1)}, bf16[4,2,128,128]{3,2,1,0:T(8,128)(2,1)}, u32[]{:S(2)}, u32[]{:S(2)}) collective-permute-start(bf16[4,2,128,128]{3,2,1,0:T(8,128)(2,1)S(1)} %get-tuple-element.54), channel_id=1, source_target_pairs={{0,6},{1,7},{2,8},{3,9},{4,10},{5,11},{6,12},{7,13},{8,14},{9,15},... | collective-permute-start | bytes 786440 | tf_op jit(solution)/shard_map/ppermute | solution.py:288
  74.3 28.8 %collective-permute-start.11 = (bf16[4,2,128,128]{3,2,1,0:T(8,128)(2,1)S(1)}, bf16[4,2,128,128]{3,2,1,0:T(8,128)(2,1)S(1)}, u32[]{:S(2)}, u32[]{:S(2)}) collective-permute-start(bf16[4,2,128,128]{3,2,1,0:T(8,128)(2,1)S(1)} %get-tuple-element.55), channel_id=1, source_target_pairs={{0,8},{1,9},{2,10},{3,11},{4,12},{5,13},{6,14},{7,15},{8,0},{9,1},... | collective-permute-start | bytes 786440 | tf_op jit(solution)/shard_map/ppermute | solution.py:288
  75.8 32.6 %collective-permute-start.22 = (bf16[4,2,128,128]{3,2,1,0:T(8,128)(2,1)S(1)}, bf16[4,2,128,128]{3,2,1,0:T(8,128)(2,1)S(1)}, u32[]{:S(2)}, u32[]{:S(2)}) collective-permute-start(bf16[4,2,128,128]{3,2,1,0:T(8,128)(2,1)S(1)} %get-tuple-element.56), channel_id=1, source_target_pairs={{0,2},{1,3},{2,4},{3,5},{4,6},{5,7},{6,8},{7,9},{8,10},{9,11},{10,... | collective-permute-start | bytes 786440 | tf_op jit(solution)/shard_map/ppermute | solution.py:288
  82.5 28.7 %collective-permute-start.21 = (bf16[4,2,128,128]{3,2,1,0:T(8,128)(2,1)S(1)}, bf16[4,2,128,128]{3,2,1,0:T(8,128)(2,1)S(1)}, u32[]{:S(2)}, u32[]{:S(2)}) collective-permute-start(bf16[4,2,128,128]{3,2,1,0:T(8,128)(2,1)S(1)} %get-tuple-element.50.refs_0_), channel_id=1, source_target_pairs={{0,1},{1,0},{2,3},{3,2},{4,5},{5,4},{6,7},{7,6},{8,9},{9,8},{10,11... | collective-permute-start | bytes 786440 | tf_op jit(solution)/shard_map/ppermute | solution.py:294
  95.1 16.3 %collective-permute-start.25 = (bf16[4,2,128,128]{3,2,1,0:T(8,128)(2,1)S(1)}, bf16[4,2,128,128]{3,2,1,0:T(8,128)(2,1)S(1)}, u32[]{:S(2)}, u32[]{:S(2)}) collective-permute-start(bf16[4,2,128,128]{3,2,1,0:T(8,128)(2,1)S(1)} %collective-permute-done.24.refs_4_), channel_id=1, source_target_pairs={{0,1},{1,0},{2,3},{3,2},{4,5},{5,4},{6,7},{7,6},{8,9},{9,8},{10,11... | collective-permute-start | bytes 786440 | tf_op jit(solution)/shard_map/ppermute | solution.py:294
  103.1 8.7 %collective-permute-start.20 = (bf16[4,2,128,128]{3,2,1,0:T(8,128)(2,1)S(1)}, bf16[4,2,128,128]{3,2,1,0:T(8,128)(2,1)S(1)}, u32[]{:S(2)}, u32[]{:S(2)}) collective-permute-start(bf16[4,2,128,128]{3,2,1,0:T(8,128)(2,1)S(1)} %collective-permute-done.19.refs_2_), channel_id=1, source_target_pairs={{0,1},{1,0},{2,3},{3,2},{4,5},{5,4},{6,7},{7,6},{8,9},{9,8},{10,11... | collective-permute-start | bytes 786440 | tf_op jit(solution)/shard_map/ppermute | solution.py:294
  111.3 14.5 %collective-permute-start.18 = (bf16[4,2,128,128]{3,2,1,0:T(8,128)(2,1)S(1)}, bf16[4,2,128,128]{3,2,1,0:T(8,128)(2,1)}, u32[]{:S(2)}, u32[]{:S(2)}) collective-permute-start(bf16[4,2,128,128]{3,2,1,0:T(8,128)(2,1)S(1)} %collective-permute-done.17.refs_0_), channel_id=1, source_target_pairs={{0,1},{1,0},{2,3},{3,2},{4,5},{5,4},{6,7},{7,6},{8,9},{9,8},{10,11... | collective-permute-start | bytes 786440 | tf_op jit(solution)/shard_map/ppermute | solution.py:294
  111.4 23.0 %collective-permute-start.16 = (bf16[4,2,128,128]{3,2,1,0:T(8,128)(2,1)}, bf16[4,2,128,128]{3,2,1,0:T(8,128)(2,1)}, u32[]{:S(2)}, u32[]{:S(2)}) collective-permute-start(bf16[4,2,128,128]{3,2,1,0:T(8,128)(2,1)} %collective-permute-done.15.refs_2_), channel_id=1, source_target_pairs={{0,1},{1,0},{2,3},{3,2},{4,5},{5,4},{6,7},{7,6},{8,9},{9,8},{10,11... | collective-permute-start | bytes 786440 | tf_op jit(solution)/shard_map/ppermute | solution.py:294
  111.8 22.6 %collective-permute-start.14 = (bf16[4,2,128,128]{3,2,1,0:T(8,128)(2,1)}, bf16[4,2,128,128]{3,2,1,0:T(8,128)(2,1)}, u32[]{:S(2)}, u32[]{:S(2)}) collective-permute-start(bf16[4,2,128,128]{3,2,1,0:T(8,128)(2,1)} %collective-permute-done.13.refs_0_), channel_id=1, source_target_pairs={{0,1},{1,0},{2,3},{3,2},{4,5},{5,4},{6,7},{7,6},{8,9},{9,8},{10,11... | collective-permute-start | bytes 786440 | tf_op jit(solution)/shard_map/ppermute | solution.py:294
  112.5 32.2 %collective-permute-start.12 = (bf16[4,2,128,128]{3,2,1,0:T(8,128)(2,1)S(1)}, bf16[4,2,128,128]{3,2,1,0:T(8,128)(2,1)S(1)}, u32[]{:S(2)}, u32[]{:S(2)}) collective-permute-start(bf16[4,2,128,128]{3,2,1,0:T(8,128)(2,1)S(1)} %collective-permute-done.11.refs_0_), channel_id=1, source_target_pairs={{0,1},{1,0},{2,3},{3,2},{4,5},{5,4},{6,7},{7,6},{8,9},{9,8},{10,11... | collective-permute-start | bytes 786440 | tf_op jit(solution)/shard_map/ppermute | solution.py:294
  152.8 8.8 %collective-permute-start.27 = (bf16[144,256]{1,0:T(8,128)(2,1)}, bf16[144,256]{1,0:T(8,128)(2,1)S(1)}, u32[]{:S(2)}, u32[]{:S(2)}) collective-permute-start(bf16[144,256]{1,0:T(8,128)(2,1)} %get-tuple-element.35), channel_id=1, source_target_pairs={{0,96},{16,112},{32,0},{48,16},{64,32},{80,48},{96,64},{112,80},{1... | collective-permute-start | bytes 221192 | tf_op jit(solution)/shard_map/ppermute | solution.py:291
  155.9 8.7 %collective-permute-start.28 = (bf16[144,256]{1,0:T(8,128)(2,1)}, bf16[144,256]{1,0:T(8,128)(2,1)S(1)}, u32[]{:S(2)}, u32[]{:S(2)}) collective-permute-start(bf16[144,256]{1,0:T(8,128)(2,1)} %get-tuple-element.36), channel_id=1, source_target_pairs={{0,80},{16,96},{32,112},{48,0},{64,16},{80,32},{96,48},{112,64},{1... | collective-permute-start | bytes 221192 | tf_op jit(solution)/shard_map/ppermute | solution.py:291
  155.9 10.9 %collective-permute-start.29 = (bf16[144,256]{1,0:T(8,128)(2,1)}, bf16[144,256]{1,0:T(8,128)(2,1)S(1)}, u32[]{:S(2)}, u32[]{:S(2)}) collective-permute-start(bf16[144,256]{1,0:T(8,128)(2,1)} %get-tuple-element.37), channel_id=1, source_target_pairs={{0,64},{16,80},{32,96},{48,112},{64,0},{80,16},{96,32},{112,48},{1... | collective-permute-start | bytes 221192 | tf_op jit(solution)/shard_map/ppermute | solution.py:291
  158.4 8.5 %collective-permute-start.30 = (bf16[144,256]{1,0:T(8,128)(2,1)}, bf16[144,256]{1,0:T(8,128)(2,1)S(1)}, u32[]{:S(2)}, u32[]{:S(2)}) collective-permute-start(bf16[144,256]{1,0:T(8,128)(2,1)} %get-tuple-element.38), channel_id=1, source_target_pairs={{0,48},{16,64},{32,80},{48,96},{64,112},{80,0},{96,16},{112,32},{1... | collective-permute-start | bytes 221192 | tf_op jit(solution)/shard_map/ppermute | solution.py:291
  161.5 11.0 %collective-permute-start.31 = (bf16[144,256]{1,0:T(8,128)(2,1)}, bf16[144,256]{1,0:T(8,128)(2,1)S(1)}, u32[]{:S(2)}, u32[]{:S(2)}) collective-permute-start(bf16[144,256]{1,0:T(8,128)(2,1)} %get-tuple-element.39), channel_id=1, source_target_pairs={{0,32},{16,48},{32,64},{48,80},{64,96},{80,112},{96,0},{112,16},{1... | collective-permute-start | bytes 221192 | tf_op jit(solution)/shard_map/ppermute | solution.py:291
  164.6 10.7 %collective-permute-start.32 = (bf16[144,256]{1,0:T(8,128)(2,1)}, bf16[144,256]{1,0:T(8,128)(2,1)S(1)}, u32[]{:S(2)}, u32[]{:S(2)}) collective-permute-start(bf16[144,256]{1,0:T(8,128)(2,1)} %get-tuple-element.40), channel_id=1, source_target_pairs={{0,16},{16,32},{32,48},{48,64},{64,80},{80,96},{96,112},{112,0},{1... | collective-permute-start | bytes 221192 | tf_op jit(solution)/shard_map/ppermute | solution.py:291
  188.6 9.8 %collective-permute-start.35 = (bf16[64,512]{1,0:T(8,128)(2,1)}, bf16[64,512]{1,0:T(8,128)(2,1)S(1)}, u32[]{:S(2)}, u32[]{:S(2)}) collective-permute-start(bf16[64,512]{1,0:T(8,128)(2,1)} %get-tuple-element.42), channel_id=1, source_target_pairs={{0,2},{1,3},{2,4},{3,5},{4,6},{5,7},{6,8},{7,9},{8,10},{9,11},{10,... | collective-permute-start | bytes 196616 | tf_op jit(solution)/shard_map/ppermute | solution.py:288
  189.2 10.8 %collective-permute-start.36 = (bf16[64,512]{1,0:T(8,128)(2,1)}, bf16[64,512]{1,0:T(8,128)(2,1)S(1)}, u32[]{:S(2)}, u32[]{:S(2)}) collective-permute-start(bf16[64,512]{1,0:T(8,128)(2,1)} %get-tuple-element.43), channel_id=1, source_target_pairs={{0,4},{1,5},{2,6},{3,7},{4,8},{5,9},{6,10},{7,11},{8,12},{9,13},{1... | collective-permute-start | bytes 196616 | tf_op jit(solution)/shard_map/ppermute | solution.py:288
  191.7 10.1 %collective-permute-start.37 = (bf16[64,512]{1,0:T(8,128)(2,1)}, bf16[64,512]{1,0:T(8,128)(2,1)S(1)}, u32[]{:S(2)}, u32[]{:S(2)}) collective-permute-start(bf16[64,512]{1,0:T(8,128)(2,1)} %get-tuple-element.44), channel_id=1, source_target_pairs={{0,6},{1,7},{2,8},{3,9},{4,10},{5,11},{6,12},{7,13},{8,14},{9,15},... | collective-permute-start | bytes 196616 | tf_op jit(solution)/shard_map/ppermute | solution.py:288
  194.0 7.9 %collective-permute-start.38 = (bf16[64,512]{1,0:T(8,128)(2,1)}, bf16[64,512]{1,0:T(8,128)(2,1)S(1)}, u32[]{:S(2)}, u32[]{:S(2)}) collective-permute-start(bf16[64,512]{1,0:T(8,128)(2,1)} %get-tuple-element.45), channel_id=1, source_target_pairs={{0,8},{1,9},{2,10},{3,11},{4,12},{5,13},{6,14},{7,15},{8,0},{9,1},... | collective-permute-start | bytes 196616 | tf_op jit(solution)/shard_map/ppermute | solution.py:288
  198.4 10.3 %collective-permute-start.40 = (bf16[64,512]{1,0:T(8,128)(2,1)}, bf16[64,512]{1,0:T(8,128)(2,1)S(1)}, u32[]{:S(2)}, u32[]{:S(2)}) collective-permute-start(bf16[64,512]{1,0:T(8,128)(2,1)} %get-tuple-element.47), channel_id=1, source_target_pairs={{0,12},{1,13},{2,14},{3,15},{4,0},{5,1},{6,2},{7,3},{8,4},{9,5},{1... | collective-permute-start | bytes 196616 | tf_op jit(solution)/shard_map/ppermute | solution.py:288
  200.0 9.6 %collective-permute-start.41 = (bf16[64,512]{1,0:T(8,128)(2,1)}, bf16[64,512]{1,0:T(8,128)(2,1)S(1)}, u32[]{:S(2)}, u32[]{:S(2)}) collective-permute-start(bf16[64,512]{1,0:T(8,128)(2,1)} %get-tuple-element.48), channel_id=1, source_target_pairs={{0,14},{1,15},{2,0},{3,1},{4,2},{5,3},{6,4},{7,5},{8,6},{9,7},{10,... | collective-permute-start | bytes 196616 | tf_op jit(solution)/shard_map/ppermute | solution.py:288
  (38 other events, 1047.5 us)
where the time goes:
time: 212 us; the launch traced here: 211 us
  starting transfers between devices  82.8 us (39%)
  waiting for transfers between devices  67.2 us (32%)
  Pallas kernels  47.3 us (22%)
  local copies, waits for them, and re-layouts  8.43 us (4%)
  other arithmetic  4.81 us (2%)
    ppermute x10, starting transfers between devices, to_other_core(): return lax.ppermute(x, 'tp', swap)  48.5 us
    pallas_call x4, Pallas kernels, attend_chunk(): pl.pallas_call(kernel, out_shape=out_shape, grid_spec=pltpu.PrefetchScala...  36.9 us
    ppermute x14, waiting for transfers between devices, along_x(): lax.ppermute(x, 'grp', [(i, (i + shift) % group_count) for i in range(gro...  29.7 us
    ppermute x14, starting transfers between devices, along_y(): lax.ppermute(x, 'tp', [(i, (i + 2 * shift) % tp_count) for i in range(tp_...  21.1 us
    ppermute x4, waiting for transfers between devices, per_device_inner(): lax.ppermute(stored, 'tp', [(i, i ^ bit) for i in range(tp_count)])  20.3 us
    ppermute x14, waiting for transfers between devices, along_y(): lax.ppermute(x, 'tp', [(i, (i + 2 * shift) % tp_count) for i in range(tp_...  16.1 us
    ppermute x14, starting transfers between devices, along_x(): lax.ppermute(x, 'grp', [(i, (i + shift) % group_count) for i in range(gro...  13 us
    pallas_call x1, Pallas kernels, project(): pl.pallas_call(kernel, out_shape=[jax.ShapeDtypeStruct((req_rows, width),...  8.29 us
  transfers between devices with their start and end apart: 42, of which 18 were waited for; matrix products, arithmetic and copies ran while one was open for 4% of the time, Pallas kernels for 18%

commit v1 on v0

v1 whole, which is shorter than its diff:
```python
import math

import jax
import jax.numpy as jnp
from jax import lax
from jax.experimental import pallas as pl
from jax.experimental.pallas import tpu as pltpu
from jax.sharding import PartitionSpec as P

HEAD_SIZE = 128
PAGE_TOKENS = 128
META_ROWS = 16
NAMED_ROW = 10
LOW = -1e30
CHUNKS = ((0, 1, 7), (2, 6), (3, 5), (4,))
INTERPRET = False


def split3(x):
    hi = x.astype(jnp.bfloat16)
    rest = x - hi.astype(jnp.float32)
    mid = rest.astype(jnp.bfloat16)
    low = (rest - mid.astype(jnp.float32)).astype(jnp.bfloat16)
    return [part.astype(jnp.float32) for part in (hi, mid, low)]


def prepare(queries, block_table, prefix_len, heads_dev, slots):
    req_rows = queries.shape[0]
    list_length = block_table.shape[1]
    cols = heads_dev * req_rows

    def kernel(q_ref, table_ref, length_ref, out_ref):
        for h in range(heads_dev):
            one = q_ref[:, h * HEAD_SIZE : (h + 1) * HEAD_SIZE].astype(jnp.float32)
            out_ref[0:HEAD_SIZE, h * req_rows : (h + 1) * req_rows] = one.T.astype(jnp.bfloat16)
        table = table_ref[...]
        length = length_ref[...]
        slot = lax.broadcasted_iota(jnp.int32, (req_rows, slots), 1)
        hit = jnp.zeros((req_rows, slots), jnp.float32)
        for j in range(list_length):
            entry = jnp.where(PAGE_TOKENS * j < length, table[:, j : j + 1], -1)
            hit = jnp.where(slot == entry, 1.0, hit)
        named = jnp.max(hit, axis=0, keepdims=True)
        high = lax.div(length, 8)
        small = jnp.concatenate([table, high, length - 8 * high], axis=1).astype(jnp.float32)
        small = jnp.concatenate([small, jnp.zeros((req_rows, HEAD_SIZE - list_length - 2), jnp.float32)], axis=1)
        small = small.T[0:META_ROWS]
        small = jnp.concatenate([small] * heads_dev, axis=1)
        sub = lax.broadcasted_iota(jnp.int32, (META_ROWS, cols), 0)
        out_ref[HEAD_SIZE:] = jnp.where(sub == list_length + 2, named, small).astype(jnp.bfloat16)

    return pl.pallas_call(
        kernel,
        out_shape=jax.ShapeDtypeStruct((HEAD_SIZE + META_ROWS, cols), jnp.bfloat16),
        interpret=INTERPRET,
        name="prepare",
    )(queries, block_table, prefix_len.reshape(-1, 1))


def attend_chunk(place, bufs, queries_t, state, shifts, y_count, group_count, per_batch, first, last):
    n_buf = len(bufs)
    buf_rows = bufs[0].shape[0]
    rows, cols = queries_t[0].shape
    limit = 2 * n_buf
    factor = math.log2(math.e) / math.sqrt(HEAD_SIZE)
    int_rows = group_count + 8 * ((n_buf + 7) // 8)

    def kernel(place_ref, *refs):
        buf_refs = refs[:n_buf]
        q_refs = refs[n_buf : n_buf + group_count]
        rest = list(refs[n_buf + group_count :])
        if not first:
            acc_in, ml_in = rest[:2]
            rest = rest[2:]
        if last:
            out_refs = rest[:group_count]
            rest = rest[group_count:]
        else:
            acc_out, ml_out = rest[:2]
            rest = rest[2:]
        (acc, ml, store, query_all, out_all, ints, numbers, item_row, item_slot, sem_store, sem_query, sem_acc, sem_ml, sem_int, sem_out) = rest
        tp_rank = place_ref[0]
        row = place_ref[1]
        core = lax.rem(tp_rank, 2)

        query_copies = [pltpu.make_async_copy(q_refs[g], query_all.at[g], sem_query.at[g]) for g in range(group_count)]
        store_copies = [
            pltpu.make_async_copy(buf_refs[b], store.at[pl.ds(b * buf_rows, buf_rows)], sem_store.at[b]) for b in range(n_buf)
        ]
        for one in query_copies + store_copies:
            one.start()
        if first:
            acc[...] = jnp.zeros(acc.shape, jnp.float32)
            ml[...] = jnp.where(lax.broadcasted_iota(jnp.int32, ml.shape, 1) == 0, LOW, 0.0)
        else:
            ml_copy = pltpu.make_async_copy(ml_in, ml, sem_ml)
            ml_copy.start()
            for g in range(group_count):
                pltpu.make_async_copy(acc_in.at[g], acc.at[g], sem_acc.at[g]).start()
        for one in query_copies + store_copies:
            one.wait()
        for g in range(group_count):
            ints[g : g + 1] = query_all[g, HEAD_SIZE:].astype(jnp.float32)[NAMED_ROW : NAMED_ROW + 1].astype(jnp.int32)
        for b in range(n_buf):
            pages = store[(b + 1) * buf_rows - META_ROWS : (b + 1) * buf_rows].astype(jnp.float32)
            ints[group_count + b : group_count + b + 1, 0:HEAD_SIZE] = pages[0:1].astype(jnp.int32)
        int_copy = pltpu.make_async_copy(ints, numbers, sem_int)
        int_copy.start()
        int_copy.wait()
        if not first:
            ml_copy.wait()

        entry = lax.broadcasted_iota(jnp.int32, (8, cols), 0).astype(jnp.float32)
        token = lax.broadcasted_iota(jnp.int32, (PAGE_TOKENS, cols), 0).astype(jnp.float32)

        def group(g, _):
            number = lax.rem(row + group_count - g, group_count)
            count = jnp.int32(0)
            for b in range(n_buf):
                source_y = lax.rem(lax.div(tp_rank, 2) + y_count - shifts[b // 2], y_count)
                owner = 2 * source_y + (core if b % 2 == 0 else 1 - core)
                for column in range(2):
                    page = numbers[group_count + b, 2 * number + column]
                    slot = (row * 2 * y_count + owner) * 2 + column
                    used = numbers[g, slot]
                    item_row[count] = b * buf_rows + page * (2 * PAGE_TOKENS)
                    item_slot[count] = slot
                    count = count + jnp.where((page >= 0) & (used > 0), 1, 0)
            for pad in range(per_batch):
                item_row[count + pad] = 0
                item_slot[count + pad] = -1

            table = query_all[g, HEAD_SIZE:].astype(jnp.float32)
            length = table[8:9] * 8.0 + table[9:10]
            table = table[0:8]
            live = jnp.clip(length - PAGE_TOKENS * entry, 0.0, 1.0 * PAGE_TOKENS)
            whole = live == PAGE_TOKENS
            if not first:
                pltpu.make_async_copy(acc_in.at[g], acc.at[g], sem_acc.at[g]).wait()

            def batch(i, _):
                query = query_all[g, 0:HEAD_SIZE]
                starts = [pl.multiple_of(item_row[i * per_batch + j], META_ROWS) for j in range(per_batch)]
                keys = jnp.concatenate([store[pl.ds(start, PAGE_TOKENS)] for start in starts], axis=0)
                raw = jnp.dot(keys, query, preferred_element_type=jnp.float32)
                old = ml[g, 0:1]
                top = old
                scores, counts = [], []
                for j in range(per_batch):
                    slot = item_slot[i * per_batch + j].astype(jnp.float32)
                    match = table == slot
                    full = jnp.sum(jnp.where(match & whole, 1.0, 0.0), axis=0, keepdims=True)
                    part = jnp.max(jnp.where(match & ~whole, live, 0.0), axis=0, keepdims=True)
                    reach = jnp.where(full > 0.0, 1.0 * PAGE_TOKENS, part)
                    score = raw[j * PAGE_TOKENS : (j + 1) * PAGE_TOKENS] * factor
                    score = jnp.where(token < reach, score, LOW)
                    top = jnp.maximum(top, jnp.max(score, axis=0, keepdims=True))
                    scores.append(score)
                    counts.append((full, part))
                shrink = jnp.exp2(old - top)
                total = ml[g, 1:2] * shrink
                weights = []
                for j in range(per_batch):
                    full, part = counts[j]
                    weight = jnp.exp2(scores[j] - top) * jnp.where(token < part, full + 1.0, full)
                    total = total + jnp.sum(weight, axis=0, keepdims=True)
                    weights.append(weight.astype(jnp.bfloat16))
                values = jnp.concatenate([store[pl.ds(start + PAGE_TOKENS, PAGE_TOKENS)] for start in starts], axis=0)
                added = lax.dot_general(
                    values, jnp.concatenate(weights, axis=0), (((0,), (0,)), ((), ())), preferred_element_type=jnp.float32
                )
                acc[g] = acc[g] * shrink + added
                ml[g, 0:1] = top
                ml[g, 1:2] = total
                return 0

            lax.fori_loop(0, lax.div(count + per_batch - 1, per_batch), batch, 0)

            if last:
                top = ml[g, 0:1]
                total = ml[g, 1:2]
                inverse = jnp.where(total > 0.0, 1.0 / jnp.where(total > 0.0, total, 1.0), 0.0)
                out_all[g, 0:HEAD_SIZE] = (acc[g] * inverse).astype(jnp.bfloat16)
                sub = lax.broadcasted_iota(jnp.int32, (META_ROWS, cols), 0)
                packed = jnp.zeros((META_ROWS, cols), jnp.float32)
                for n, part in enumerate(split3(top) + split3(total)):
                    packed = jnp.where(sub == n, part, packed)
                out_all[g, HEAD_SIZE:] = packed.astype(jnp.bfloat16)
                for n in range(group_count):

                    @pl.when(g == n)
                    def _():
                        pltpu.make_async_copy(out_all.at[n], out_refs[n], sem_out.at[n]).start()
            else:
                pltpu.make_async_copy(acc.at[g], acc_out.at[g], sem_out.at[g]).start()
            return 0

        lax.fori_loop(0, group_count, group, 0)
        if last:
            for n in range(group_count):
                pltpu.make_async_copy(out_all.at[n], out_refs[n], sem_out.at[n]).wait()
        else:
            ml_back = pltpu.make_async_copy(ml, ml_out, sem_ml)
            ml_back.start()
            for n in range(group_count):
                pltpu.make_async_copy(acc.at[n], acc_out.at[n], sem_out.at[n]).wait()
            ml_back.wait()

    if last:
        out_shape = [jax.ShapeDtypeStruct((HEAD_SIZE + META_ROWS, cols), jnp.bfloat16)] * group_count
    else:
        out_shape = [
            jax.ShapeDtypeStruct((group_count, HEAD_SIZE, cols), jnp.float32),
            jax.ShapeDtypeStruct((group_count, 8, cols), jnp.float32),
        ]
    n_out_slots = group_count if last else 1
    scratch = [
        pltpu.VMEM((group_count, HEAD_SIZE, cols), jnp.float32),
        pltpu.VMEM((group_count, 8, cols), jnp.float32),
        pltpu.VMEM((n_buf * buf_rows, HEAD_SIZE), jnp.bfloat16),
        pltpu.VMEM((group_count, rows, cols), jnp.bfloat16),
        pltpu.VMEM((n_out_slots, HEAD_SIZE + META_ROWS, cols), jnp.bfloat16),
        pltpu.VMEM((int_rows, cols), jnp.int32),
        pltpu.SMEM((int_rows, cols), jnp.int32),
        pltpu.SMEM((limit + per_batch,), jnp.int32),
        pltpu.SMEM((limit + per_batch,), jnp.int32),
        pltpu.SemaphoreType.DMA((n_buf,)),
        pltpu.SemaphoreType.DMA((group_count,)),
        pltpu.SemaphoreType.DMA((group_count,)),
        pltpu.SemaphoreType.DMA,
        pltpu.SemaphoreType.DMA,
        pltpu.SemaphoreType.DMA((group_count,)),
    ]
    anywhere = pl.BlockSpec(memory_space=pltpu.MemorySpace.HBM)
    n_in = n_buf + group_count + (0 if first else 2)
    return pl.pallas_call(
        kernel,
        out_shape=out_shape,
        grid_spec=pltpu.PrefetchScalarGridSpec(
            num_scalar_prefetch=1,
            grid=(),
            in_specs=[anywhere] * n_in,
            out_specs=[anywhere] * len(out_shape),
            scratch_shapes=scratch,
        ),
        interpret=INTERPRET,
    )(place, *bufs, *queries_t, *(() if first else state))


def combine(arrived, query_t, newest_t, heads_dev):
    parts = len(arrived)
    cols = arrived[0].shape[1]
    req_rows = cols // heads_dev
    factor = math.log2(math.e) / math.sqrt(HEAD_SIZE)

    def kernel(*refs):
        in_refs = refs[:parts]
        q_ref, new_ref, out_ref = refs[parts:]
        query = q_ref[0:HEAD_SIZE].astype(jnp.float32)
        own = jnp.sum(query * new_ref[0].astype(jnp.float32), axis=0, keepdims=True) * factor
        top = own
        tops, totals = [], []
        for n in range(parts):
            packed = in_refs[n][HEAD_SIZE:].astype(jnp.float32)
            tops.append(packed[0:1] + packed[1:2] + packed[2:3])
            totals.append(packed[3:4] + packed[4:5] + packed[5:6])
            top = jnp.maximum(top, tops[-1])
        own_weight = jnp.exp2(own - top)
        denominator = own_weight
        scales = []
        for n in range(parts):
            scales.append(totals[n] * jnp.exp2(tops[n] - top))
            denominator = denominator + scales[-1]
        inverse = 1.0 / denominator
        mix = new_ref[1].astype(jnp.float32) * (own_weight * inverse)
        for n in range(parts):
            mix = mix + in_refs[n][0:HEAD_SIZE].astype(jnp.float32) * (scales[n] * inverse)
        for h in range(heads_dev):
            one = mix[:, h * req_rows : (h + 1) * req_rows]
            out_ref[:, h * HEAD_SIZE : (h + 1) * HEAD_SIZE] = one.T.astype(jnp.bfloat16)

    return pl.pallas_call(
        kernel,
        out_shape=jax.ShapeDtypeStruct((req_rows, heads_dev * HEAD_SIZE), jnp.bfloat16),
        interpret=INTERPRET,
        name="combine",
    )(*arrived, query_t, newest_t)


def project(place, mix_own, mix_partner, weight_own, weight_partner, y_count):
    width = weight_own.shape[1] // (2 * y_count)
    req_rows, depth = mix_own.shape

    def kernel(place_ref, own_ref, partner_ref, w_own_ref, w_partner_ref, out_ref, w_all, sem):
        core = lax.rem(place_ref[0], 2)
        copies = []
        for n in range(y_count):
            start = pl.multiple_of((2 * n + core) * width, width)
            for k, ref in enumerate((w_own_ref, w_partner_ref)):
                copies.append(
                    pltpu.make_async_copy(
                        ref.at[:, pl.ds(start, width)], w_all.at[n, pl.ds(k * depth, depth)], sem.at[2 * n + k]
                    )
                )
        for one in copies:
            one.start()
        mix = jnp.concatenate([own_ref[...], partner_ref[...]], axis=1)
        for n in range(y_count):
            copies[2 * n].wait()
            copies[2 * n + 1].wait()
            out_ref[n] = jnp.dot(mix, w_all[n], preferred_element_type=jnp.float32).astype(jnp.bfloat16)

    vmem = pl.BlockSpec(memory_space=pltpu.MemorySpace.VMEM)
    anywhere = pl.BlockSpec(memory_space=pltpu.MemorySpace.HBM)
    return pl.pallas_call(
        kernel,
        out_shape=jax.ShapeDtypeStruct((y_count, req_rows, width), jnp.bfloat16),
        grid_spec=pltpu.PrefetchScalarGridSpec(
            num_scalar_prefetch=1,
            grid=(),
            in_specs=[vmem, vmem, anywhere, anywhere],
            out_specs=vmem,
            scratch_shapes=[
                pltpu.VMEM((y_count, 2 * depth, width), jnp.bfloat16),
                pltpu.SemaphoreType.DMA((2 * y_count,)),
            ],
        ),
        interpret=INTERPRET,
        name="project",
    )(place, mix_own, mix_partner, weight_own, weight_partner)


def per_device_inner(
    queries, newest_key_value, kv_pages, fetch_slots, block_table, prefix_len, out_weight
):
    tp_count = lax.axis_size("tp")
    group_count = lax.axis_size("grp")
    y_count = tp_count // 2
    tp_rank = lax.axis_index("tp").astype(jnp.int32)
    row = lax.axis_index("grp").astype(jnp.int32)
    y = lax.div(tp_rank, 2)
    heads_dev = queries.shape[1] // HEAD_SIZE
    slots = 2 * tp_count * group_count
    swap = [(i, i ^ 1) for i in range(tp_count)]

    def along_y(x, shift):
        return lax.ppermute(x, "tp", [(i, (i + 2 * shift) % tp_count) for i in range(tp_count)])

    def along_x(x, shift):
        return lax.ppermute(x, "grp", [(i, (i + shift) % group_count) for i in range(group_count)])

    def to_other_core(x):
        return lax.ppermute(x, "tp", swap)

    slots_block = jnp.pad(fetch_slots.reshape(1, -1).astype(jnp.bfloat16), ((0, META_ROWS - 1), (0, HEAD_SIZE - 2 * group_count)))
    own, partner = {}, {}
    for shift in [s for chunk in CHUNKS for s in chunk]:
        head = lax.rem(y + shift, y_count)
        piece = lax.dynamic_slice_in_dim(kv_pages, head * HEAD_SIZE, HEAD_SIZE, 3)
        piece = jnp.concatenate([piece.reshape(-1, HEAD_SIZE), slots_block], axis=0)
        own[shift] = along_y(piece, shift) if shift else piece
    for shift in own:
        partner[shift] = to_other_core(own[shift])
    weight_partner = to_other_core(out_weight)

    query_t = prepare(queries, block_table, prefix_len, heads_dev, slots)
    queries_t = [along_x(query_t, s) if s else query_t for s in range(group_count)]
    place = jnp.stack([tp_rank, row])

    newest = lax.dynamic_slice_in_dim(newest_key_value, y * HEAD_SIZE, HEAD_SIZE, 2)
    newest_t = jnp.tile(jnp.transpose(newest, (1, 2, 0)), (1, 1, heads_dev))

    state = ()
    for n, shifts in enumerate(CHUNKS):
        bufs = [b for s in shifts for b in (own[s], partner[s])]
        last = n == len(CHUNKS) - 1
        state = attend_chunk(
            place, bufs, queries_t, state, shifts, y_count, group_count, 2 if last else 4, n == 0, last
        )
    arrived = [along_x(state[s], -s) if s else state[s] for s in range(group_count)]

    mix_own = combine(arrived, query_t, newest_t, heads_dev)
    mix_partner = to_other_core(mix_own)
    partial = project(place, mix_own, mix_partner, out_weight, weight_partner, y_count)
    same_core = [[2 * i + c for i in range(y_count)] for c in range(2)]
    arrived = lax.all_to_all(partial, "tp", split_axis=0, concat_axis=0, axis_index_groups=same_core, tiled=True)
    return jnp.sum(arrived.astype(jnp.float32), axis=0).astype(jnp.bfloat16)


def solution(mesh):
    in_specs = (
        P(("rep", "grp"), "tp"),
        P(("rep", "grp"), None, None),
        P(("rep", "grp", "tp"), None, None, None),
        P("rep", ("grp", "tp"), None),
        P(("rep", "grp"), None),
        P(("rep", "grp")),
        P("tp", None),
    )
    out_specs = P(("rep", "grp"), "tp")
    return jax.shard_map(per_device_inner, mesh=mesh, in_specs=in_specs, out_specs=out_specs, check_vma=False)
```

time: 212 us -> 189 us (0.89)
  starting transfers between devices: 82.8 us -> 56.3 us
  blocking collectives: 0 us -> 22 us
  waiting for transfers between devices: 67.2 us -> 50.3 us
  other arithmetic: 4.81 us -> 2.13 us
    all_to_all x0 -> x1, blocking collectives: none -> 22 us  [per_device_inner(): lax.all_to_all(partial, 'tp', split_axis=0, concat_axis=0, axis_index_gro...]
    ppermute x4 -> x0, waiting for transfers between devices: 20.3 us -> none  [per_device_inner(): lax.ppermute(stored, 'tp', [(i, i ^ bit) for i in range(tp_count)])]
    ppermute x14 -> x7, starting transfers between devices: 21.1 us -> 4.47 us  [along_y(): lax.ppermute(x, 'tp', [(i, (i + 2 * shift) % tp_count) for i in range(tp_...]
    ppermute x10, starting transfers between devices: 48.5 us -> 32.6 us  [to_other_core(): return lax.ppermute(x, 'tp', swap)]
    ppermute x14, starting transfers between devices: 13 us -> 19.2 us  [along_x(): lax.ppermute(x, 'grp', [(i, (i + shift) % group_count) for i in range(gro...]
    ppermute x14 -> x7, waiting for transfers between devices: 16.1 us -> 17.7 us  [along_y(): lax.ppermute(x, 'tp', [(i, (i + 2 * shift) % tp_count) for i in range(tp_...]
    unnamed x58 -> x61, local copies, waits for them, and re-layouts: 3.92 us -> 4.43 us
    pallas_call x1 -> x2, Pallas kernels: 8.29 us -> 8.51 us  [the longest x1 6.27 us: project(): pl.pallas_call(kernel, out_shape=jax.ShapeDtypeStruct((y_count, req_rows,...]
  transfers between devices with their start and end apart: 42 -> 31, of which waited for: 18 -> 14; matrix products, arithmetic and copies ran while one was open for 4% -> 4% of each run, Pallas kernels for 18% -> 23%
where the time goes in v1:
time: 189 us; the launch traced here: 188 us
  starting transfers between devices  56.3 us (30%)
  waiting for transfers between devices  50.3 us (27%)
  Pallas kernels  48.7 us (26%)
  blocking collectives  22 us (12%)
  local copies, waits for them, and re-layouts  8.49 us (4%)
  other arithmetic  2.13 us (1%)
    pallas_call x4, Pallas kernels, attend_chunk(): pl.pallas_call(kernel, out_shape=out_shape, grid_spec=pltpu.PrefetchScala...  38.1 us
    ppermute x10, starting transfers between devices, to_other_core(): return lax.ppermute(x, 'tp', swap)  32.6 us
    ppermute x14, waiting for transfers between devices, along_x(): lax.ppermute(x, 'grp', [(i, (i + shift) % group_count) for i in range(gro...  31 us
    all_to_all x1, blocking collectives, per_device_inner(): lax.all_to_all(partial, 'tp', split_axis=0, concat_axis=0, axis_index_gro...  22 us
    ppermute x14, starting transfers between devices, along_x(): lax.ppermute(x, 'grp', [(i, (i + shift) % group_count) for i in range(gro...  19.2 us
    ppermute x7, waiting for transfers between devices, along_y(): lax.ppermute(x, 'tp', [(i, (i + 2 * shift) % tp_count) for i in range(tp_...  17.7 us
    pallas_call x1, Pallas kernels, project(): pl.pallas_call(kernel, out_shape=jax.ShapeDtypeStruct((y_count, req_rows,...  6.27 us
    ppermute x7, starting transfers between devices, along_y(): lax.ppermute(x, 'tp', [(i, (i + 2 * shift) % tp_count) for i in range(tp_...  4.47 us
  transfers between devices with their start and end apart: 31, of which 14 were waited for; matrix products, arithmetic and copies ran while one was open for 4% of the time, Pallas kernels for 23%

profile of v1, /device:TPU:513, one launch (start us, length us, event | category | flops | bytes accessed | tf_op | source)
XLA Modules:
  0.0 188.4 jit_solution(9630637832730293426)
XLA Ops:
  0.0 20.4 %collective-permute-start.30 = (bf16[512,8192]{1,0:T(8,128)(2,1)}, bf16[512,8192]{1,0:T(8,128)(2,1)}, u32[]{:S(2)}, u32[]{:S(2)}) collective-permute-start(bf16[512,8192]{1,0:T(8,128)(2,1)} %w_own_ref.1), channel_id=1, source_target_pairs={{0,1},{1,0},{2,3},{3,2},{4,5},{5,4},{6,7},{7,6},{8,9},{9,8},{10,11... | collective-permute-start | bytes 25165832 | tf_op jit(solution)/shard_map/ppermute | solution.py:353
  20.4 1.4 copy.13.table_ref
  21.8 1.4 copy.14.length_ref
  23.2 2.2 %prepare.1.refs_6_.refs_4_.refs_2_.refs_8_ = bf16[144,256]{1,0:T(8,128)(2,1)} custom-call(bf16[64,512]{1,0:T(8,128)(2,1)} %q_ref.1, s32[64,8]{1,0:T(8,128)} %copy.13.table_ref, s32[64,1]{1,0:T(8,128)} %copy.14.length_ref), custom_call_target="tpu_custom_call" | custom-call | tf_op jit(solution)/shard_map/prepare/pallas_call | solution.py:52
  25.6 5.5 %collective-permute-start.5 = (bf16[144,256]{1,0:T(8,128)(2,1)}, bf16[144,256]{1,0:T(8,128)(2,1)S(1)}, u32[]{:S(2)}, u32[]{:S(2)}) collective-permute-start(bf16[144,256]{1,0:T(8,128)(2,1)} %prepare.1.refs_6_.refs_4_.refs_2_.refs_8_), channel_id=1, source_target_pairs={{0,64},{16,80},{32,96},{48,112},{64,0},{80,16},{96,32},{112,48},{1... | collective-permute-start | bytes 221192 | tf_op jit(solution)/shard_map/ppermute | solution.py:350
  31.9 1.7 constant_dynamic-slice_fusion
  34.1 0.7 collective-permute-done.6.refs_11_.refs_9_.refs_7_
  34.9 3.5 %collective-permute-start.4 = (bf16[144,256]{1,0:T(8,128)(2,1)S(1)}, bf16[144,256]{1,0:T(8,128)(2,1)S(1)}, u32[]{:S(2)}, u32[]{:S(2)}) collective-permute-start(bf16[144,256]{1,0:T(8,128)(2,1)S(1)} %copy-done.1), channel_id=1, source_target_pairs={{0,48},{16,64},{32,80},{48,96},{64,112},{80,0},{96,16},{112,32},{1... | collective-permute-start | bytes 221192 | tf_op jit(solution)/shard_map/ppermute | solution.py:350
  38.4 10.2 %collective-permute-done.4.refs_9_.refs_7_.refs_5_ = bf16[144,256]{1,0:T(8,128)(2,1)S(1)} collective-permute-done((bf16[144,256]{1,0:T(8,128)(2,1)S(1)}, bf16[144,256]{1,0:T(8,128)(2,1)S(1)}, u32[]{:S(2)}, u32[]{:S(2)}) %collective-permute-start.4) | collective-permute-done | bytes 73760 | tf_op jit(solution)/shard_map/ppermute | solution.py:350
  48.6 5.7 %collective-permute-done.3.refs_8_.refs_6_.refs_4_ = bf16[144,256]{1,0:T(8,128)(2,1)S(1)} collective-permute-done((bf16[144,256]{1,0:T(8,128)(2,1)S(1)}, bf16[144,256]{1,0:T(8,128)(2,1)S(1)}, u32[]{:S(2)}, u32[]{:S(2)}) %collective-permute-start.3) | collective-permute-done | bytes 73760 | tf_op jit(solution)/shard_map/ppermute | solution.py:350
  54.3 4.7 %collective-permute-done.2.refs_7_.refs_5_.refs_3_ = bf16[144,256]{1,0:T(8,128)(2,1)S(1)} collective-permute-done((bf16[144,256]{1,0:T(8,128)(2,1)S(1)}, bf16[144,256]{1,0:T(8,128)(2,1)S(1)}, u32[]{:S(2)}, u32[]{:S(2)}) %collective-permute-start.2) | collective-permute-done | bytes 73760 | tf_op jit(solution)/shard_map/ppermute | solution.py:350
  59.7 3.6 %collective-permute-start.15 = (bf16[1040,128]{1,0:T(8,128)(2,1)S(1)}, bf16[1040,128]{1,0:T(8,128)(2,1)S(1)}, u32[]{:S(2)}, u32[]{:S(2)}) collective-permute-start(bf16[1040,128]{1,0:T(8,128)(2,1)S(1)} %get-tuple-element.46), channel_id=1, source_target_pairs={{0,12},{1,13},{2,14},{3,15},{4,0},{5,1},{6,2},{7,3},{8,4},{9,5},{1... | collective-permute-start | bytes 798728 | tf_op jit(solution)/shard_map/ppermute | solution.py:347
  63.3 3.4 %collective-permute-done.9.refs_0_ = bf16[1040,128]{1,0:T(8,128)(2,1)S(1)} collective-permute-done((bf16[1040,128]{1,0:T(8,128)(2,1)S(1)}, bf16[1040,128]{1,0:T(8,128)(2,1)S(1)}, u32[]{:S(2)}, u32[]{:S(2)}) %collective-permute-start.9) | collective-permute-done | bytes 266272 | tf_op jit(solution)/shard_map/ppermute | solution.py:347
  66.6 10.7 %collective-permute-done.11.refs_2_ = bf16[1040,128]{1,0:T(8,128)(2,1)S(1)} collective-permute-done((bf16[1040,128]{1,0:T(8,128)(2,1)S(1)}, bf16[1040,128]{1,0:T(8,128)(2,1)S(1)}, u32[]{:S(2)}, u32[]{:S(2)}) %collective-permute-start.11) | collective-permute-done | bytes 266272 | tf_op jit(solution)/shard_map/ppermute | solution.py:347
  77.4 2.6 %collective-permute-start.17 = (bf16[1040,128]{1,0:T(8,128)(2,1)S(1)}, bf16[1040,128]{1,0:T(8,128)(2,1)S(1)}, u32[]{:S(2)}, u32[]{:S(2)}) collective-permute-start(bf16[1040,128]{1,0:T(8,128)(2,1)S(1)} %get-tuple-element.47.refs_0_), channel_id=1, source_target_pairs={{0,1},{1,0},{2,3},{3,2},{4,5},{5,4},{6,7},{7,6},{8,9},{9,8},{10,11... | collective-permute-start | bytes 798728 | tf_op jit(solution)/shard_map/ppermute | solution.py:353
  80.1 3.6 %collective-permute-done.15.refs_2_ = bf16[1040,128]{1,0:T(8,128)(2,1)S(1)} collective-permute-done((bf16[1040,128]{1,0:T(8,128)(2,1)S(1)}, bf16[1040,128]{1,0:T(8,128)(2,1)S(1)}, u32[]{:S(2)}, u32[]{:S(2)}) %collective-permute-start.15) | collective-permute-done | bytes 266272 | tf_op jit(solution)/shard_map/ppermute | solution.py:347
  83.7 5.9 %collective-permute-start.14 = (bf16[1040,128]{1,0:T(8,128)(2,1)S(1)}, bf16[1040,128]{1,0:T(8,128)(2,1)S(1)}, u32[]{:S(2)}, u32[]{:S(2)}) collective-permute-start(bf16[1040,128]{1,0:T(8,128)(2,1)S(1)} %collective-permute-done.13.refs_0_), channel_id=1, source_target_pairs={{0,1},{1,0},{2,3},{3,2},{4,5},{5,4},{6,7},{7,6},{8,9},{9,8},{10,11... | collective-permute-start | bytes 798728 | tf_op jit(solution)/shard_map/ppermute | solution.py:353
  93.3 11.1 %shard_map.73 = (f32[8,128,256]{2,1,0:T(8,128)}, f32[8,8,256]{2,1,0:T(8,128)}) custom-call(s32[2]{0:T(128)} %pad_add_fusion.place_ref, bf16[1040,128]{1,0:T(8,128)(2,1)} %copy-done.9, bf16[1040,128]{1,0:T(8,128)(2,1)} %copy-done.18, bf16[1040,128]{1,0:T(8,128)(2,1)} %copy-done.16, bf16[1040,128]{1,0:T(8,128)(2,1)} %copy-done.21, ...), custom_call_target="tpu_custom_call" | custom-call | tf_op jit(solution)/shard_map/pallas_call | solution.py:236
  104.4 8.8 %shard_map.74 = (f32[8,128,256]{2,1,0:T(8,128)}, f32[8,8,256]{2,1,0:T(8,128)}) custom-call(s32[2]{0:T(128)} %pad_add_fusion.place_ref, bf16[1040,128]{1,0:T(8,128)(2,1)} %copy-done.14, bf16[1040,128]{1,0:T(8,128)(2,1)} %copy-done.19, bf16[1040,128]{1,0:T(8,128)(2,1)} %copy-done.15, bf16[1040,128]{1,0:T(8,128)(2,1)} %collective-permute-done.16.refs_3_, ...), custom_call_target="tpu_custom_call" | custom-call | tf_op jit(solution)/shard_map/pallas_call | solution.py:236
  113.3 10.5 %shard_map.75 = (f32[8,128,256]{2,1,0:T(8,128)}, f32[8,8,256]{2,1,0:T(8,128)}) custom-call(s32[2]{0:T(128)} %pad_add_fusion.place_ref, bf16[1040,128]{1,0:T(8,128)(2,1)} %copy-done.11, bf16[1040,128]{1,0:T(8,128)(2,1)} %collective-permute-done.10.refs_1_, bf16[1040,128]{1,0:T(8,128)(2,1)} %copy-done.13, bf16[1040,128]{1,0:T(8,128)(2,1)} %collective-permute-done.12.refs_3_, ...), custom_call_target="tpu_custom_call" | custom-call | tf_op jit(solution)/shard_map/pallas_call | solution.py:236
  124.5 7.7 %shard_map.76 = (bf16[144,256]{1,0:T(8,128)(2,1)}, bf16[144,256]{1,0:T(8,128)(2,1)}, bf16[144,256]{1,0:T(8,128)(2,1)}, bf16[144,256]{1,0:T(8,128)(2,1)}, bf16[14...) custom-call(s32[2]{0:T(128)} %pad_add_fusion.place_ref, ...), custom_call_target="tpu_custom_call" | custom-call | tf_op jit(solution)/shard_map/pallas_call | solution.py:236
  132.3 1.6 collective-permute-start.23
  134.0 4.3 %collective-permute-start.25 = (bf16[144,256]{1,0:T(8,128)(2,1)}, bf16[144,256]{1,0:T(8,128)(2,1)S(1)}, u32[]{:S(2)}, u32[]{:S(2)}) collective-permute-start(bf16[144,256]{1,0:T(8,128)(2,1)} %get-tuple-element.29), channel_id=1, source_target_pairs={{0,64},{16,80},{32,96},{48,112},{64,0},{80,16},{96,32},{112,48},{1... | collective-permute-start | bytes 221192 | tf_op jit(solution)/shard_map/ppermute | solution.py:350
  138.3 3.3 %collective-permute-start.26 = (bf16[144,256]{1,0:T(8,128)(2,1)}, bf16[144,256]{1,0:T(8,128)(2,1)S(1)}, u32[]{:S(2)}, u32[]{:S(2)}) collective-permute-start(bf16[144,256]{1,0:T(8,128)(2,1)} %get-tuple-element.30), channel_id=1, source_target_pairs={{0,48},{16,64},{32,80},{48,96},{64,112},{80,0},{96,16},{112,32},{1... | collective-permute-start | bytes 221192 | tf_op jit(solution)/shard_map/ppermute | solution.py:350
  143.1 0.8 copy.16.refs_9_
  143.9 5.0 %collective-permute-done.26.refs_5_ = bf16[144,256]{1,0:T(8,128)(2,1)S(1)} collective-permute-done((bf16[144,256]{1,0:T(8,128)(2,1)}, bf16[144,256]{1,0:T(8,128)(2,1)S(1)}, u32[]{:S(2)}, u32[]{:S(2)}) %collective-permute-start.26) | collective-permute-done | bytes 73760 | tf_op jit(solution)/shard_map/ppermute | solution.py:350
  149.1 3.6 %collective-permute-done.28.refs_7_ = bf16[144,256]{1,0:T(8,128)(2,1)S(1)} collective-permute-done((bf16[144,256]{1,0:T(8,128)(2,1)}, bf16[144,256]{1,0:T(8,128)(2,1)S(1)}, u32[]{:S(2)}, u32[]{:S(2)}) %collective-permute-start.28) | collective-permute-done | bytes 73760 | tf_op jit(solution)/shard_map/ppermute | solution.py:350
  153.3 2.1 %combine.1.own_ref = bf16[64,512]{1,0:T(8,128)(2,1)} custom-call(bf16[144,256]{1,0:T(8,128)(2,1)} %get-tuple-element.25.refs_0_, bf16[144,256]{1,0:T(8,128)(2,1)} %copy-done.22, bf16[144,256]{1,0:T(8,128)(2,1)} %copy-done.23, bf16[144,256]{1,0:T(8,128)(2,1)} %copy-done.24, bf16[144,256]{1,0:T(8,128)(2,1)} %copy-done.25, bf16[144,256]{1,0:T(8,128)(2,1)} %copy-done.26, ...), custom_call_target="tpu_custom_call" | custom-call | tf_op jit(solution)/shard_map/combine/pallas_call | solution.py:282
  155.5 2.2 %collective-permute-start.29 = (bf16[64,512]{1,0:T(8,128)(2,1)}, bf16[64,512]{1,0:T(8,128)(2,1)S(1)}, u32[]{:S(2)}, u32[]{:S(2)}) collective-permute-start(bf16[64,512]{1,0:T(8,128)(2,1)} %combine.1.own_ref), channel_id=1, source_target_pairs={{0,1},{1,0},{2,3},{3,2},{4,5},{5,4},{6,7},{7,6},{8,9},{9,8},{10,11... | collective-permute-start | bytes 196616 | tf_op jit(solution)/shard_map/ppermute | solution.py:353
  157.6 1.1 collective-permute-done.29.partner_ref
  159.4 6.3 %project.1 = bf16[8,64,512]{2,1,0:T(8,128)(2,1)} custom-call(s32[2]{0:T(128)} %pad_add_fusion.place_ref, bf16[64,512]{1,0:T(8,128)(2,1)} %combine.1.own_ref, bf16[64,512]{1,0:T(8,128)(2,1)} %copy-done.29, bf16[512,8192]{1,0:T(8,128)(2,1)} %w_own_ref.1, bf16[512,8192]{1,0:T(8,128)(2,1)} %collective-permute-done.30.w_partner_ref), custom_call_target="tpu_custom_call" | custom-call | tf_op jit(solution)/shard_map/project/pallas_call | solution.py:315
  165.7 22.0 %all_to_all.5 = bf16[8,64,512]{2,1,0:T(8,128)(2,1)S(1)} all-to-all(bf16[8,64,512]{2,1,0:T(8,128)(2,1)} %project.1), channel_id=1, replica_groups={{0,2,4,6,8,10,12,14},{1,3,5,7,9,11,13,15},{16,18,20,22,24,26,28,30},{17..., dimensions={0} | all-to-all | bytes 1048576 | tf_op jit(solution)/shard_map/all_to_all | solution.py:386
  (111 shorter events, 10.4 us)
Async XLA Ops:
  0.0 143.1 %copy-start = (bf16[64,2,1024]{2,1,0:T(2,128)(2,1)S(1)}, bf16[64,2,1024]{2,1,0:T(2,128)(2,1)}, u32[]{:S(2)}) copy-start(bf16[64,2,1024]{2,1,0:T(2,128)(2,1)} %param.8) | copy-start | bytes 786436
  0.0 158.8 %collective-permute-start.30 = (bf16[512,8192]{1,0:T(8,128)(2,1)}, bf16[512,8192]{1,0:T(8,128)(2,1)}, u32[]{:S(2)}, u32[]{:S(2)}) collective-permute-start(bf16[512,8192]{1,0:T(8,128)(2,1)} %w_own_ref.1), channel_id=1, source_target_pairs={{0,1},{1,0},{2,3},{3,2},{4,5},{5,4},{6,7},{7,6},{8,9},{9,8},{10,11... | collective-permute-start | bytes 25165832 | tf_op jit(solution)/shard_map/ppermute | solution.py:353
  25.4 8.4 %collective-permute-start.8 = (bf16[144,256]{1,0:T(8,128)(2,1)}, bf16[144,256]{1,0:T(8,128)(2,1)S(1)}, u32[]{:S(2)}, u32[]{:S(2)}) collective-permute-start(bf16[144,256]{1,0:T(8,128)(2,1)} %prepare.1.refs_6_.refs_4_.refs_2_.refs_8_), channel_id=1, source_target_pairs={{0,112},{16,0},{32,16},{48,32},{64,48},{80,64},{96,80},{112,96},{1... | collective-permute-start | bytes 221192 | tf_op jit(solution)/shard_map/ppermute | solution.py:350
  25.4 8.6 %collective-permute-start.7 = (bf16[144,256]{1,0:T(8,128)(2,1)}, bf16[144,256]{1,0:T(8,128)(2,1)S(1)}, u32[]{:S(2)}, u32[]{:S(2)}) collective-permute-start(bf16[144,256]{1,0:T(8,128)(2,1)} %prepare.1.refs_6_.refs_4_.refs_2_.refs_8_), channel_id=1, source_target_pairs={{0,96},{16,112},{32,0},{48,16},{64,32},{80,48},{96,64},{112,80},{1... | collective-permute-start | bytes 221192 | tf_op jit(solution)/shard_map/ppermute | solution.py:350
  25.4 9.4 %collective-permute-start.6 = (bf16[144,256]{1,0:T(8,128)(2,1)}, bf16[144,256]{1,0:T(8,128)(2,1)S(1)}, u32[]{:S(2)}, u32[]{:S(2)}) collective-permute-start(bf16[144,256]{1,0:T(8,128)(2,1)} %prepare.1.refs_6_.refs_4_.refs_2_.refs_8_), channel_id=1, source_target_pairs={{0,80},{16,96},{32,112},{48,0},{64,16},{80,32},{96,48},{112,64},{1... | collective-permute-start | bytes 221192 | tf_op jit(solution)/shard_map/ppermute | solution.py:350
  25.6 9.3 %collective-permute-start.5 = (bf16[144,256]{1,0:T(8,128)(2,1)}, bf16[144,256]{1,0:T(8,128)(2,1)S(1)}, u32[]{:S(2)}, u32[]{:S(2)}) collective-permute-start(bf16[144,256]{1,0:T(8,128)(2,1)} %prepare.1.refs_6_.refs_4_.refs_2_.refs_8_), channel_id=1, source_target_pairs={{0,64},{16,80},{32,96},{48,112},{64,0},{80,16},{96,32},{112,48},{1... | collective-permute-start | bytes 221192 | tf_op jit(solution)/shard_map/ppermute | solution.py:350
  33.8 25.9 %collective-permute-start.20 = (bf16[1040,128]{1,0:T(8,128)(2,1)S(1)}, bf16[1040,128]{1,0:T(8,128)(2,1)S(1)}, u32[]{:S(2)}, u32[]{:S(2)}) collective-permute-start(bf16[1040,128]{1,0:T(8,128)(2,1)S(1)} %get-tuple-element.41), channel_id=1, source_target_pairs={{0,14},{1,15},{2,0},{3,1},{4,2},{5,3},{6,4},{7,5},{8,6},{9,7},{10,... | collective-permute-start | bytes 798728 | tf_op jit(solution)/shard_map/ppermute | solution.py:347
  34.0 25.7 %collective-permute-start = (bf16[1040,128]{1,0:T(8,128)(2,1)S(1)}, bf16[1040,128]{1,0:T(8,128)(2,1)S(1)}, u32[]{:S(2)}, u32[]{:S(2)}) collective-permute-start(bf16[1040,128]{1,0:T(8,128)(2,1)S(1)} %get-tuple-element.42), channel_id=1, source_target_pairs={{0,8},{1,9},{2,10},{3,11},{4,12},{5,13},{6,14},{7,15},{8,0},{9,1},... | collective-permute-start | bytes 798728 | tf_op jit(solution)/shard_map/ppermute | solution.py:347
  34.9 31.8 %collective-permute-start.9 = (bf16[1040,128]{1,0:T(8,128)(2,1)S(1)}, bf16[1040,128]{1,0:T(8,128)(2,1)S(1)}, u32[]{:S(2)}, u32[]{:S(2)}) collective-permute-start(bf16[1040,128]{1,0:T(8,128)(2,1)S(1)} %get-tuple-element.43), channel_id=1, source_target_pairs={{0,6},{1,7},{2,8},{3,9},{4,10},{5,11},{6,12},{7,13},{8,14},{9,15},... | collective-permute-start | bytes 798728 | tf_op jit(solution)/shard_map/ppermute | solution.py:347
  34.9 13.7 %collective-permute-start.4 = (bf16[144,256]{1,0:T(8,128)(2,1)S(1)}, bf16[144,256]{1,0:T(8,128)(2,1)S(1)}, u32[]{:S(2)}, u32[]{:S(2)}) collective-permute-start(bf16[144,256]{1,0:T(8,128)(2,1)S(1)} %copy-done.1), channel_id=1, source_target_pairs={{0,48},{16,64},{32,80},{48,96},{64,112},{80,0},{96,16},{112,32},{1... | collective-permute-start | bytes 221192 | tf_op jit(solution)/shard_map/ppermute | solution.py:350
  48.6 5.7 %collective-permute-start.3 = (bf16[144,256]{1,0:T(8,128)(2,1)S(1)}, bf16[144,256]{1,0:T(8,128)(2,1)S(1)}, u32[]{:S(2)}, u32[]{:S(2)}) collective-permute-start(bf16[144,256]{1,0:T(8,128)(2,1)S(1)} %copy-done.1), channel_id=1, source_target_pairs={{0,32},{16,48},{32,64},{48,80},{64,96},{80,112},{96,0},{112,16},{1... | collective-permute-start | bytes 221192 | tf_op jit(solution)/shard_map/ppermute | solution.py:350
  54.3 4.7 %collective-permute-start.2 = (bf16[144,256]{1,0:T(8,128)(2,1)S(1)}, bf16[144,256]{1,0:T(8,128)(2,1)S(1)}, u32[]{:S(2)}, u32[]{:S(2)}) collective-permute-start(bf16[144,256]{1,0:T(8,128)(2,1)S(1)} %copy-done.1), channel_id=1, source_target_pairs={{0,16},{16,32},{32,48},{48,64},{64,80},{80,96},{96,112},{112,0},{1... | collective-permute-start | bytes 221192 | tf_op jit(solution)/shard_map/ppermute | solution.py:350
  59.0 18.3 %collective-permute-start.11 = (bf16[1040,128]{1,0:T(8,128)(2,1)S(1)}, bf16[1040,128]{1,0:T(8,128)(2,1)S(1)}, u32[]{:S(2)}, u32[]{:S(2)}) collective-permute-start(bf16[1040,128]{1,0:T(8,128)(2,1)S(1)} %get-tuple-element.44), channel_id=1, source_target_pairs={{0,10},{1,11},{2,12},{3,13},{4,14},{5,15},{6,0},{7,1},{8,2},{9,3},... | collective-permute-start | bytes 798728 | tf_op jit(solution)/shard_map/ppermute | solution.py:347
  59.7 20.3 %collective-permute-start.13 = (bf16[1040,128]{1,0:T(8,128)(2,1)S(1)}, bf16[1040,128]{1,0:T(8,128)(2,1)S(1)}, u32[]{:S(2)}, u32[]{:S(2)}) collective-permute-start(bf16[1040,128]{1,0:T(8,128)(2,1)S(1)} %get-tuple-element.45), channel_id=1, source_target_pairs={{0,4},{1,5},{2,6},{3,7},{4,8},{5,9},{6,10},{7,11},{8,12},{9,13},{1... | collective-permute-start | bytes 798728 | tf_op jit(solution)/shard_map/ppermute | solution.py:347
  59.7 24.0 %collective-permute-start.15 = (bf16[1040,128]{1,0:T(8,128)(2,1)S(1)}, bf16[1040,128]{1,0:T(8,128)(2,1)S(1)}, u32[]{:S(2)}, u32[]{:S(2)}) collective-permute-start(bf16[1040,128]{1,0:T(8,128)(2,1)S(1)} %get-tuple-element.46), channel_id=1, source_target_pairs={{0,12},{1,13},{2,14},{3,15},{4,0},{5,1},{6,2},{7,3},{8,4},{9,5},{1... | collective-permute-start | bytes 798728 | tf_op jit(solution)/shard_map/ppermute | solution.py:347
  66.6 23.0 %collective-permute-start.18 = (bf16[1040,128]{1,0:T(8,128)(2,1)S(1)}, bf16[1040,128]{1,0:T(8,128)(2,1)S(1)}, u32[]{:S(2)}, u32[]{:S(2)}) collective-permute-start(bf16[1040,128]{1,0:T(8,128)(2,1)S(1)} %get-tuple-element.48), channel_id=1, source_target_pairs={{0,2},{1,3},{2,4},{3,5},{4,6},{5,7},{6,8},{7,9},{8,10},{9,11},{10,... | collective-permute-start | bytes 798728 | tf_op jit(solution)/shard_map/ppermute | solution.py:347
  77.4 12.4 %collective-permute-start.17 = (bf16[1040,128]{1,0:T(8,128)(2,1)S(1)}, bf16[1040,128]{1,0:T(8,128)(2,1)S(1)}, u32[]{:S(2)}, u32[]{:S(2)}) collective-permute-start(bf16[1040,128]{1,0:T(8,128)(2,1)S(1)} %get-tuple-element.47.refs_0_), channel_id=1, source_target_pairs={{0,1},{1,0},{2,3},{3,2},{4,5},{5,4},{6,7},{7,6},{8,9},{9,8},{10,11... | collective-permute-start | bytes 798728 | tf_op jit(solution)/shard_map/ppermute | solution.py:353
  80.0 10.2 %collective-permute-start.21 = (bf16[1040,128]{1,0:T(8,128)(2,1)S(1)}, bf16[1040,128]{1,0:T(8,128)(2,1)S(1)}, u32[]{:S(2)}, u32[]{:S(2)}) collective-permute-start(bf16[1040,128]{1,0:T(8,128)(2,1)S(1)} %collective-permute-done.20.refs_4_), channel_id=1, source_target_pairs={{0,1},{1,0},{2,3},{3,2},{4,5},{5,4},{6,7},{7,6},{8,9},{9,8},{10,11... | collective-permute-start | bytes 798728 | tf_op jit(solution)/shard_map/ppermute | solution.py:353
  83.7 7.1 %collective-permute-start.14 = (bf16[1040,128]{1,0:T(8,128)(2,1)S(1)}, bf16[1040,128]{1,0:T(8,128)(2,1)S(1)}, u32[]{:S(2)}, u32[]{:S(2)}) collective-permute-start(bf16[1040,128]{1,0:T(8,128)(2,1)S(1)} %collective-permute-done.13.refs_0_), channel_id=1, source_target_pairs={{0,1},{1,0},{2,3},{3,2},{4,5},{5,4},{6,7},{7,6},{8,9},{9,8},{10,11... | collective-permute-start | bytes 798728 | tf_op jit(solution)/shard_map/ppermute | solution.py:353
  89.6 1.9 collective-permute-start.19
  89.8 14.6 %collective-permute-start.16 = (bf16[1040,128]{1,0:T(8,128)(2,1)S(1)}, bf16[1040,128]{1,0:T(8,128)(2,1)}, u32[]{:S(2)}, u32[]{:S(2)}) collective-permute-start(bf16[1040,128]{1,0:T(8,128)(2,1)S(1)} %collective-permute-done.15.refs_2_), channel_id=1, source_target_pairs={{0,1},{1,0},{2,3},{3,2},{4,5},{5,4},{6,7},{7,6},{8,9},{9,8},{10,11... | collective-permute-start | bytes 798728 | tf_op jit(solution)/shard_map/ppermute | solution.py:353
  90.2 23.1 %collective-permute-start.10 = (bf16[1040,128]{1,0:T(8,128)(2,1)S(1)}, bf16[1040,128]{1,0:T(8,128)(2,1)}, u32[]{:S(2)}, u32[]{:S(2)}) collective-permute-start(bf16[1040,128]{1,0:T(8,128)(2,1)S(1)} %collective-permute-done.9.refs_0_), channel_id=1, source_target_pairs={{0,1},{1,0},{2,3},{3,2},{4,5},{5,4},{6,7},{7,6},{8,9},{9,8},{10,11... | collective-permute-start | bytes 798728 | tf_op jit(solution)/shard_map/ppermute | solution.py:353
  90.8 22.4 %collective-permute-start.12 = (bf16[1040,128]{1,0:T(8,128)(2,1)S(1)}, bf16[1040,128]{1,0:T(8,128)(2,1)}, u32[]{:S(2)}, u32[]{:S(2)}) collective-permute-start(bf16[1040,128]{1,0:T(8,128)(2,1)S(1)} %collective-permute-done.11.refs_2_), channel_id=1, source_target_pairs={{0,1},{1,0},{2,3},{3,2},{4,5},{5,4},{6,7},{7,6},{8,9},{9,8},{10,11... | collective-permute-start | bytes 798728 | tf_op jit(solution)/shard_map/ppermute | solution.py:353
  92.2 31.5 %collective-permute-start.1 = (bf16[1040,128]{1,0:T(8,128)(2,1)S(1)}, bf16[1040,128]{1,0:T(8,128)(2,1)S(1)}, u32[]{:S(2)}, u32[]{:S(2)}) collective-permute-start(bf16[1040,128]{1,0:T(8,128)(2,1)S(1)} %collective-permute-done.refs_0_), channel_id=1, source_target_pairs={{0,1},{1,0},{2,3},{3,2},{4,5},{5,4},{6,7},{7,6},{8,9},{9,8},{10,11... | collective-permute-start | bytes 798728 | tf_op jit(solution)/shard_map/ppermute | solution.py:353
  132.2 6.1 %collective-permute-start.22 = (bf16[144,256]{1,0:T(8,128)(2,1)}, bf16[144,256]{1,0:T(8,128)(2,1)S(1)}, u32[]{:S(2)}, u32[]{:S(2)}) collective-permute-start(bf16[144,256]{1,0:T(8,128)(2,1)} %get-tuple-element.26), channel_id=1, source_target_pairs={{0,112},{16,0},{32,16},{48,32},{64,48},{80,64},{96,80},{112,96},{1... | collective-permute-start | bytes 221192 | tf_op jit(solution)/shard_map/ppermute | solution.py:350
  132.3 9.5 %collective-permute-start.23 = (bf16[144,256]{1,0:T(8,128)(2,1)}, bf16[144,256]{1,0:T(8,128)(2,1)S(1)}, u32[]{:S(2)}, u32[]{:S(2)}) collective-permute-start(bf16[144,256]{1,0:T(8,128)(2,1)} %get-tuple-element.27), channel_id=1, source_target_pairs={{0,96},{16,112},{32,0},{48,16},{64,32},{80,48},{96,64},{112,80},{1... | collective-permute-start | bytes 221192 | tf_op jit(solution)/shard_map/ppermute | solution.py:350
  134.0 8.4 %collective-permute-start.24 = (bf16[144,256]{1,0:T(8,128)(2,1)}, bf16[144,256]{1,0:T(8,128)(2,1)S(1)}, u32[]{:S(2)}, u32[]{:S(2)}) collective-permute-start(bf16[144,256]{1,0:T(8,128)(2,1)} %get-tuple-element.28), channel_id=1, source_target_pairs={{0,80},{16,96},{32,112},{48,0},{64,16},{80,32},{96,48},{112,64},{1... | collective-permute-start | bytes 221192 | tf_op jit(solution)/shard_map/ppermute | solution.py:350
  134.0 9.9 %collective-permute-start.25 = (bf16[144,256]{1,0:T(8,128)(2,1)}, bf16[144,256]{1,0:T(8,128)(2,1)S(1)}, u32[]{:S(2)}, u32[]{:S(2)}) collective-permute-start(bf16[144,256]{1,0:T(8,128)(2,1)} %get-tuple-element.29), channel_id=1, source_target_pairs={{0,64},{16,80},{32,96},{48,112},{64,0},{80,16},{96,32},{112,48},{1... | collective-permute-start | bytes 221192 | tf_op jit(solution)/shard_map/ppermute | solution.py:350
  138.3 10.6 %collective-permute-start.26 = (bf16[144,256]{1,0:T(8,128)(2,1)}, bf16[144,256]{1,0:T(8,128)(2,1)S(1)}, u32[]{:S(2)}, u32[]{:S(2)}) collective-permute-start(bf16[144,256]{1,0:T(8,128)(2,1)} %get-tuple-element.30), channel_id=1, source_target_pairs={{0,48},{16,64},{32,80},{48,96},{64,112},{80,0},{96,16},{112,32},{1... | collective-permute-start | bytes 221192 | tf_op jit(solution)/shard_map/ppermute | solution.py:350
  141.8 7.3 %collective-permute-start.27 = (bf16[144,256]{1,0:T(8,128)(2,1)}, bf16[144,256]{1,0:T(8,128)(2,1)S(1)}, u32[]{:S(2)}, u32[]{:S(2)}) collective-permute-start(bf16[144,256]{1,0:T(8,128)(2,1)} %get-tuple-element.31), channel_id=1, source_target_pairs={{0,32},{16,48},{32,64},{48,80},{64,96},{80,112},{96,0},{112,16},{1... | collective-permute-start | bytes 221192 | tf_op jit(solution)/shard_map/ppermute | solution.py:350
  142.4 10.3 %collective-permute-start.28 = (bf16[144,256]{1,0:T(8,128)(2,1)}, bf16[144,256]{1,0:T(8,128)(2,1)S(1)}, u32[]{:S(2)}, u32[]{:S(2)}) collective-permute-start(bf16[144,256]{1,0:T(8,128)(2,1)} %get-tuple-element.32), channel_id=1, source_target_pairs={{0,16},{16,32},{32,48},{48,64},{64,80},{80,96},{96,112},{112,0},{1... | collective-permute-start | bytes 221192 | tf_op jit(solution)/shard_map/ppermute | solution.py:350
  155.5 3.3 %collective-permute-start.29 = (bf16[64,512]{1,0:T(8,128)(2,1)}, bf16[64,512]{1,0:T(8,128)(2,1)S(1)}, u32[]{:S(2)}, u32[]{:S(2)}) collective-permute-start(bf16[64,512]{1,0:T(8,128)(2,1)} %combine.1.own_ref), channel_id=1, source_target_pairs={{0,1},{1,0},{2,3},{3,2},{4,5},{5,4},{6,7},{7,6},{8,9},{9,8},{10,11... | collective-permute-start | bytes 196616 | tf_op jit(solution)/shard_map/ppermute | solution.py:353
  (29 other events, 710.7 us)

commit v2 on v1

--- a/solution.py
+++ b/solution.py
@@ -12,7 +12,8 @@
 META_ROWS = 16
 NAMED_ROW = 10
 LOW = -1e30
-CHUNKS = ((0, 1, 7), (2, 6), (3, 5), (4,))
+CHUNKS = ((0, 1, 7, 2, 6), (3, 5, 4))
+STAT_ROWS = 16
 INTERPRET = False
 
 
@@ -28,24 +29,24 @@
     req_rows = queries.shape[0]
     list_length = block_table.shape[1]
     cols = heads_dev * req_rows
+    assert slots == cols
 
     def kernel(q_ref, table_ref, length_ref, out_ref):
         for h in range(heads_dev):
             one = q_ref[:, h * HEAD_SIZE : (h + 1) * HEAD_SIZE].astype(jnp.float32)
             out_ref[0:HEAD_SIZE, h * req_rows : (h + 1) * req_rows] = one.T.astype(jnp.bfloat16)
-        table = table_ref[...]
         length = length_ref[...]
-        slot = lax.broadcasted_iota(jnp.int32, (req_rows, slots), 1)
+        high = lax.div(length, 8)
+        small = jnp.concatenate([table_ref[...], high, length - 8 * high, length], axis=0).astype(jnp.float32)
+        small = jnp.concatenate([small, jnp.zeros((HEAD_SIZE - list_length - 3, req_rows), jnp.float32)], axis=0)
+        lists = small.T
+        slot = lax.broadcasted_iota(jnp.int32, (req_rows, slots), 1).astype(jnp.float32)
         hit = jnp.zeros((req_rows, slots), jnp.float32)
         for j in range(list_length):
-            entry = jnp.where(PAGE_TOKENS * j < length, table[:, j : j + 1], -1)
+            entry = jnp.where(lists[:, list_length + 2 : list_length + 3] > PAGE_TOKENS * j, lists[:, j : j + 1], -1.0)
             hit = jnp.where(slot == entry, 1.0, hit)
         named = jnp.max(hit, axis=0, keepdims=True)
-        high = lax.div(length, 8)
-        small = jnp.concatenate([table, high, length - 8 * high], axis=1).astype(jnp.float32)
-        small = jnp.concatenate([small, jnp.zeros((req_rows, HEAD_SIZE - list_length - 2), jnp.float32)], axis=1)
-        small = small.T[0:META_ROWS]
-        small = jnp.concatenate([small] * heads_dev, axis=1)
+        small = jnp.concatenate([small[0:META_ROWS]] * heads_dev, axis=1)
         sub = lax.broadcasted_iota(jnp.int32, (META_ROWS, cols), 0)
         out_ref[HEAD_SIZE:] = jnp.where(sub == list_length + 2, named, small).astype(jnp.bfloat16)
 
@@ -54,7 +55,7 @@
         out_shape=jax.ShapeDtypeStruct((HEAD_SIZE + META_ROWS, cols), jnp.bfloat16),
         interpret=INTERPRET,
         name="prepare",
-    )(queries, block_table, prefix_len.reshape(-1, 1))
+    )(queries, block_table.T, prefix_len.reshape(1, -1))
 
 
 def attend_chunk(place, bufs, queries_t, state, shifts, y_count, group_count, per_batch, first, last):
@@ -73,8 +74,8 @@
             acc_in, ml_in = rest[:2]
             rest = rest[2:]
         if last:
-            out_refs = rest[:group_count]
-            rest = rest[group_count:]
+            out_ref = rest[0]
+            rest = rest[1:]
         else:
             acc_out, ml_out = rest[:2]
             rest = rest[2:]
@@ -181,16 +182,12 @@
                 total = ml[g, 1:2]
                 inverse = jnp.where(total > 0.0, 1.0 / jnp.where(total > 0.0, total, 1.0), 0.0)
                 out_all[g, 0:HEAD_SIZE] = (acc[g] * inverse).astype(jnp.bfloat16)
-                sub = lax.broadcasted_iota(jnp.int32, (META_ROWS, cols), 0)
-                packed = jnp.zeros((META_ROWS, cols), jnp.float32)
+                sub = lax.broadcasted_iota(jnp.int32, (STAT_ROWS, cols), 0)
+                packed = jnp.zeros((STAT_ROWS, cols), jnp.float32)
                 for n, part in enumerate(split3(top) + split3(total)):
                     packed = jnp.where(sub == n, part, packed)
                 out_all[g, HEAD_SIZE:] = packed.astype(jnp.bfloat16)
-                for n in range(group_count):
-
-                    @pl.when(g == n)
-                    def _():
-                        pltpu.make_async_copy(out_all.at[n], out_refs[n], sem_out.at[n]).start()
+                pltpu.make_async_copy(out_all.at[g], out_ref.at[number], sem_out.at[g]).start()
             else:
                 pltpu.make_async_copy(acc.at[g], acc_out.at[g], sem_out.at[g]).start()
             return 0
@@ -198,7 +195,7 @@
         lax.fori_loop(0, group_count, group, 0)
         if last:
             for n in range(group_count):
-                pltpu.make_async_copy(out_all.at[n], out_refs[n], sem_out.at[n]).wait()
+                pltpu.make_async_copy(out_all.at[n], out_ref.at[n], sem_out.at[n]).wait()
         else:
             ml_back = pltpu.make_async_copy(ml, ml_out, sem_ml)
             ml_back.start()
@@ -207,7 +204,7 @@
             ml_back.wait()
 
     if last:
-        out_shape = [jax.ShapeDtypeStruct((HEAD_SIZE + META_ROWS, cols), jnp.bfloat16)] * group_count
+        out_shape = [jax.ShapeDtypeStruct((group_count, HEAD_SIZE + STAT_ROWS, cols), jnp.bfloat16)]
     else:
         out_shape = [
             jax.ShapeDtypeStruct((group_count, HEAD_SIZE, cols), jnp.float32),
@@ -219,7 +216,7 @@
         pltpu.VMEM((group_count, 8, cols), jnp.float32),
         pltpu.VMEM((n_buf * buf_rows, HEAD_SIZE), jnp.bfloat16),
         pltpu.VMEM((group_count, rows, cols), jnp.bfloat16),
-        pltpu.VMEM((n_out_slots, HEAD_SIZE + META_ROWS, cols), jnp.bfloat16),
+        pltpu.VMEM((n_out_slots, HEAD_SIZE + STAT_ROWS, cols), jnp.bfloat16),
         pltpu.VMEM((int_rows, cols), jnp.int32),
         pltpu.SMEM((int_rows, cols), jnp.int32),
         pltpu.SMEM((limit + per_batch,), jnp.int32),
@@ -248,20 +245,17 @@
 
 
 def combine(arrived, query_t, newest_t, heads_dev):
-    parts = len(arrived)
-    cols = arrived[0].shape[1]
+    parts, _, cols = arrived.shape
     req_rows = cols // heads_dev
     factor = math.log2(math.e) / math.sqrt(HEAD_SIZE)
 
-    def kernel(*refs):
-        in_refs = refs[:parts]
-        q_ref, new_ref, out_ref = refs[parts:]
+    def kernel(in_ref, q_ref, new_ref, out_ref):
         query = q_ref[0:HEAD_SIZE].astype(jnp.float32)
         own = jnp.sum(query * new_ref[0].astype(jnp.float32), axis=0, keepdims=True) * factor
         top = own
         tops, totals = [], []
         for n in range(parts):
-            packed = in_refs[n][HEAD_SIZE:].astype(jnp.float32)
+            packed = in_ref[n, HEAD_SIZE:].astype(jnp.float32)
             tops.append(packed[0:1] + packed[1:2] + packed[2:3])
             totals.append(packed[3:4] + packed[4:5] + packed[5:6])
             top = jnp.maximum(top, tops[-1])
@@ -274,7 +268,7 @@
         inverse = 1.0 / denominator
         mix = new_ref[1].astype(jnp.float32) * (own_weight * inverse)
         for n in range(parts):
-            mix = mix + in_refs[n][0:HEAD_SIZE].astype(jnp.float32) * (scales[n] * inverse)
+            mix = mix + in_ref[n, 0:HEAD_SIZE].astype(jnp.float32) * (scales[n] * inverse)
         for h in range(heads_dev):
             one = mix[:, h * req_rows : (h + 1) * req_rows]
             out_ref[:, h * HEAD_SIZE : (h + 1) * HEAD_SIZE] = one.T.astype(jnp.bfloat16)
@@ -284,7 +278,7 @@
         out_shape=jax.ShapeDtypeStruct((req_rows, heads_dev * HEAD_SIZE), jnp.bfloat16),
         interpret=INTERPRET,
         name="combine",
-    )(*arrived, query_t, newest_t)
+    )(arrived, query_t, newest_t)
 
 
 def project(place, mix_own, mix_partner, weight_own, weight_partner, y_count):
@@ -375,9 +369,9 @@
         bufs = [b for s in shifts for b in (own[s], partner[s])]
         last = n == len(CHUNKS) - 1
         state = attend_chunk(
-            place, bufs, queries_t, state, shifts, y_count, group_count, 2 if last else 4, n == 0, last
+            place, bufs, queries_t, state, shifts, y_count, group_count, 4, n == 0, last
         )
-    arrived = [along_x(state[s], -s) if s else state[s] for s in range(group_count)]
+    arrived = lax.all_to_all(state[0], "grp", split_axis=0, concat_axis=0, tiled=True)
 
     mix_own = combine(arrived, query_t, newest_t, heads_dev)
     mix_partner = to_other_core(mix_own)

time: 189 us -> 180 us (0.952)
  Pallas kernels: 48.7 us -> 35.8 us
  starting transfers between devices: 56.3 us -> 68.6 us
  waiting for transfers between devices: 50.3 us -> 44.9 us
  local copies, waits for them, and re-layouts: 8.49 us -> 6.16 us
    all_to_all x0 -> x1, waiting for transfers between devices: none -> 18.6 us  [per_device_inner(): lax.all_to_all(state[0], 'grp', split_axis=0, concat_axis=0, tiled=True)]
    ppermute x14 -> x7, waiting for transfers between devices: 31 us -> 15.7 us  [along_x(): lax.ppermute(x, 'grp', [(i, (i + shift) % group_count) for i in range(gro...]
    pallas_call x4 -> x2, Pallas kernels: 38.1 us -> 25.4 us  [attend_chunk(): pl.pallas_call(kernel, out_shape=out_shape, grid_spec=pltpu.PrefetchScala...]
    ppermute x14 -> x7, starting transfers between devices: 19.2 us -> 9.33 us  [along_x(): lax.ppermute(x, 'grp', [(i, (i + shift) % group_count) for i in range(gro...]
    ppermute x10, starting transfers between devices: 32.6 us -> 42.5 us  [to_other_core(): return lax.ppermute(x, 'tp', swap)]
    ppermute x7, waiting for transfers between devices: 17.7 us -> 9.49 us  [along_y(): lax.ppermute(x, 'tp', [(i, (i + 2 * shift) % tp_count) for i in range(tp_...]
    all_to_all x0 -> x1, starting transfers between devices: none -> 6.8 us  [per_device_inner(): lax.all_to_all(state[0], 'grp', split_axis=0, concat_axis=0, tiled=True)]
    ppermute x7, starting transfers between devices: 4.47 us -> 10 us  [along_y(): lax.ppermute(x, 'tp', [(i, (i + 2 * shift) % tp_count) for i in range(tp_...]
  transfers between devices with their start and end apart: 31 -> 25, of which waited for: 14 -> 8; matrix products, arithmetic and copies ran while one was open for 4% -> 2% of each run, Pallas kernels for 23% -> 16%
where the time goes in v2:
time: 180 us; the launch traced here: 179 us
  starting transfers between devices  68.6 us (38%)
  waiting for transfers between devices  44.9 us (25%)
  Pallas kernels  35.8 us (20%)
  blocking collectives  21.4 us (12%)
  local copies, waits for them, and re-layouts  6.16 us (3%)
  other arithmetic  2.18 us (1%)
    ppermute x10, starting transfers between devices, to_other_core(): return lax.ppermute(x, 'tp', swap)  42.5 us
    pallas_call x2, Pallas kernels, attend_chunk(): pl.pallas_call(kernel, out_shape=out_shape, grid_spec=pltpu.PrefetchScala...  25.4 us
    all_to_all x1, blocking collectives, per_device_inner(): lax.all_to_all(partial, 'tp', split_axis=0, concat_axis=0, axis_index_gro...  21.4 us
    all_to_all x1, waiting for transfers between devices, per_device_inner(): lax.all_to_all(state[0], 'grp', split_axis=0, concat_axis=0, tiled=True)  18.6 us
    ppermute x7, waiting for transfers between devices, along_x(): lax.ppermute(x, 'grp', [(i, (i + shift) % group_count) for i in range(gro...  15.7 us
    ppermute x7, starting transfers between devices, along_y(): lax.ppermute(x, 'tp', [(i, (i + 2 * shift) % tp_count) for i in range(tp_...  10 us
    ppermute x7, waiting for transfers between devices, along_y(): lax.ppermute(x, 'tp', [(i, (i + 2 * shift) % tp_count) for i in range(tp_...  9.49 us
    ppermute x7, starting transfers between devices, along_x(): lax.ppermute(x, 'grp', [(i, (i + shift) % group_count) for i in range(gro...  9.33 us
  transfers between devices with their start and end apart: 25, of which 8 were waited for; matrix products, arithmetic and copies ran while one was open for 2% of the time, Pallas kernels for 16%

profile of v2, /device:TPU:513, one launch (start us, length us, event | category | flops | bytes accessed | tf_op | source)
XLA Modules:
  0.0 179.4 jit_solution(11633861158139919356)
XLA Ops:
  0.0 20.4 %collective-permute-start.23 = (bf16[512,8192]{1,0:T(8,128)(2,1)}, bf16[512,8192]{1,0:T(8,128)(2,1)}, u32[]{:S(2)}, u32[]{:S(2)}) collective-permute-start(bf16[512,8192]{1,0:T(8,128)(2,1)} %w_own_ref.1), channel_id=1, source_target_pairs={{0,1},{1,0},{2,3},{3,2},{4,5},{5,4},{6,7},{7,6},{8,9},{9,8},{10,11... | collective-permute-start | bytes 25165832 | tf_op jit(solution)/shard_map/ppermute | solution.py:347
  20.4 2.2 %prepare.1.refs_10_.refs_6_.q_ref = bf16[144,256]{1,0:T(8,128)(2,1)} custom-call(bf16[64,512]{1,0:T(8,128)(2,1)} %q_ref.1, s32[8,64]{1,0:T(8,128)} %bitcast.26, s32[1,64]{1,0:T(1,128)} %bitcast.27), custom_call_target="tpu_custom_call" | custom-call | tf_op jit(solution)/shard_map/prepare/pallas_call | solution.py:53
  22.8 5.5 %collective-permute-start.9 = (bf16[144,256]{1,0:T(8,128)(2,1)}, bf16[144,256]{1,0:T(8,128)(2,1)S(1)}, u32[]{:S(2)}, u32[]{:S(2)}) collective-permute-start(bf16[144,256]{1,0:T(8,128)(2,1)} %prepare.1.refs_10_.refs_6_.q_ref), channel_id=1, source_target_pairs={{0,64},{16,80},{32,96},{48,112},{64,0},{80,16},{96,32},{112,48},{1... | collective-permute-start | bytes 221192 | tf_op jit(solution)/shard_map/ppermute | solution.py:344
  28.2 0.7 convert_element_type.18
  29.1 1.7 constant_dynamic-slice_fusion
  31.3 0.7 collective-permute-done.10.refs_15_.refs_11_
  32.0 3.7 %collective-permute-start.2 = (bf16[1040,128]{1,0:T(8,128)(2,1)S(1)}, bf16[1040,128]{1,0:T(8,128)(2,1)S(1)}, u32[]{:S(2)}, u32[]{:S(2)}) collective-permute-start(bf16[1040,128]{1,0:T(8,128)(2,1)S(1)} %get-tuple-element.19), channel_id=1, source_target_pairs={{0,10},{1,11},{2,12},{3,13},{4,14},{5,15},{6,0},{7,1},{8,2},{9,3},... | collective-permute-start | bytes 798728 | tf_op jit(solution)/shard_map/ppermute | solution.py:341
  35.9 8.1 %collective-permute-done.8.refs_13_.refs_9_ = bf16[144,256]{1,0:T(8,128)(2,1)S(1)} collective-permute-done((bf16[144,256]{1,0:T(8,128)(2,1)S(1)}, bf16[144,256]{1,0:T(8,128)(2,1)S(1)}, u32[]{:S(2)}, u32[]{:S(2)}) %collective-permute-start.8) | collective-permute-done | bytes 73760 | tf_op jit(solution)/shard_map/ppermute | solution.py:344
  44.0 3.3 %collective-permute-start.7 = (bf16[144,256]{1,0:T(8,128)(2,1)S(1)}, bf16[144,256]{1,0:T(8,128)(2,1)S(1)}, u32[]{:S(2)}, u32[]{:S(2)}) collective-permute-start(bf16[144,256]{1,0:T(8,128)(2,1)S(1)} %copy-done.2), channel_id=1, source_target_pairs={{0,32},{16,48},{32,64},{48,80},{64,96},{80,112},{96,0},{112,16},{1... | collective-permute-start | bytes 221192 | tf_op jit(solution)/shard_map/ppermute | solution.py:344
  47.3 2.3 %collective-permute-done.7.refs_12_.refs_8_ = bf16[144,256]{1,0:T(8,128)(2,1)S(1)} collective-permute-done((bf16[144,256]{1,0:T(8,128)(2,1)S(1)}, bf16[144,256]{1,0:T(8,128)(2,1)S(1)}, u32[]{:S(2)}, u32[]{:S(2)}) %collective-permute-start.7) | collective-permute-done | bytes 73760 | tf_op jit(solution)/shard_map/ppermute | solution.py:344
  49.8 4.6 %collective-permute-done.6.refs_11_.refs_7_ = bf16[144,256]{1,0:T(8,128)(2,1)S(1)} collective-permute-done((bf16[144,256]{1,0:T(8,128)(2,1)S(1)}, bf16[144,256]{1,0:T(8,128)(2,1)S(1)}, u32[]{:S(2)}, u32[]{:S(2)}) %collective-permute-start.6) | collective-permute-done | bytes 73760 | tf_op jit(solution)/shard_map/ppermute | solution.py:344
  54.4 2.2 %collective-permute-start.14 = (bf16[1040,128]{1,0:T(8,128)(2,1)S(1)}, bf16[1040,128]{1,0:T(8,128)(2,1)S(1)}, u32[]{:S(2)}, u32[]{:S(2)}) collective-permute-start(bf16[1040,128]{1,0:T(8,128)(2,1)S(1)} %get-tuple-element.22), channel_id=1, source_target_pairs={{0,2},{1,3},{2,4},{3,5},{4,6},{5,7},{6,8},{7,9},{8,10},{9,11},{10,... | collective-permute-start | bytes 798728 | tf_op jit(solution)/shard_map/ppermute | solution.py:341
  56.6 1.3 collective-permute-start.16
  58.0 2.5 %collective-permute-start.18 = (bf16[1040,128]{1,0:T(8,128)(2,1)S(1)}, bf16[1040,128]{1,0:T(8,128)(2,1)}, u32[]{:S(2)}, u32[]{:S(2)}) collective-permute-start(bf16[1040,128]{1,0:T(8,128)(2,1)S(1)} %get-tuple-element.24), channel_id=1, source_target_pairs={{0,4},{1,5},{2,6},{3,7},{4,8},{5,9},{6,10},{7,11},{8,12},{9,13},{1... | collective-permute-start | bytes 798728 | tf_op jit(solution)/shard_map/ppermute | solution.py:341
  60.5 5.4 %collective-permute-done.4.refs_4_ = bf16[1040,128]{1,0:T(8,128)(2,1)S(1)} collective-permute-done((bf16[1040,128]{1,0:T(8,128)(2,1)S(1)}, bf16[1040,128]{1,0:T(8,128)(2,1)S(1)}, u32[]{:S(2)}, u32[]{:S(2)}) %collective-permute-start.4) | collective-permute-done | bytes 266272 | tf_op jit(solution)/shard_map/ppermute | solution.py:341
  65.9 9.8 %collective-permute-start.13 = (bf16[1040,128]{1,0:T(8,128)(2,1)S(1)}, bf16[1040,128]{1,0:T(8,128)(2,1)}, u32[]{:S(2)}, u32[]{:S(2)}) collective-permute-start(bf16[1040,128]{1,0:T(8,128)(2,1)S(1)} %get-tuple-element.21.refs_0_), channel_id=1, source_target_pairs={{0,1},{1,0},{2,3},{3,2},{4,5},{5,4},{6,7},{7,6},{8,9},{9,8},{10,11... | collective-permute-start | bytes 798728 | tf_op jit(solution)/shard_map/ppermute | solution.py:347
  75.6 4.6 %collective-permute-start.21 = (bf16[1040,128]{1,0:T(8,128)(2,1)S(1)}, bf16[1040,128]{1,0:T(8,128)(2,1)S(1)}, u32[]{:S(2)}, u32[]{:S(2)}) collective-permute-start(bf16[1040,128]{1,0:T(8,128)(2,1)S(1)} %collective-permute-done.20.refs_8_), channel_id=1, source_target_pairs={{0,1},{1,0},{2,3},{3,2},{4,5},{5,4},{6,7},{7,6},{8,9},{9,8},{10,11... | collective-permute-start | bytes 798728 | tf_op jit(solution)/shard_map/ppermute | solution.py:347
  80.4 4.1 %collective-permute-done.18.refs_6_ = bf16[1040,128]{1,0:T(8,128)(2,1)} collective-permute-done((bf16[1040,128]{1,0:T(8,128)(2,1)S(1)}, bf16[1040,128]{1,0:T(8,128)(2,1)}, u32[]{:S(2)}, u32[]{:S(2)}) %collective-permute-start.18) | collective-permute-done | bytes 266272 | tf_op jit(solution)/shard_map/ppermute | solution.py:341
  84.5 5.5 %collective-permute-start.17 = (bf16[1040,128]{1,0:T(8,128)(2,1)S(1)}, bf16[1040,128]{1,0:T(8,128)(2,1)S(1)}, u32[]{:S(2)}, u32[]{:S(2)}) collective-permute-start(bf16[1040,128]{1,0:T(8,128)(2,1)S(1)} %collective-permute-done.16.refs_4_), channel_id=1, source_target_pairs={{0,1},{1,0},{2,3},{3,2},{4,5},{5,4},{6,7},{7,6},{8,9},{9,8},{10,11... | collective-permute-start | bytes 798728 | tf_op jit(solution)/shard_map/ppermute | solution.py:347
  91.5 0.7 copy-done.22
  92.7 0.7 pad_add_fusion.place_ref
  93.4 13.1 %shard_map.73 = (f32[8,128,256]{2,1,0:T(8,128)}, f32[8,8,256]{2,1,0:T(8,128)}) custom-call(s32[2]{0:T(128)} %pad_add_fusion.place_ref, bf16[1040,128]{1,0:T(8,128)(2,1)} %copy-done.3, bf16[1040,128]{1,0:T(8,128)(2,1)} %collective-permute-done.13.refs_1_, bf16[1040,128]{1,0:T(8,128)(2,1)} %copy-done.18, bf16[1040,128]{1,0:T(8,128)(2,1)} %copy-done.21, ...), custom_call_target="tpu_custom_call" | custom-call | tf_op jit(solution)/shard_map/pallas_call | solution.py:233
  107.5 12.2 %shard_map.74 = bf16[8,144,256]{2,1,0:T(8,128)(2,1)} custom-call(s32[2]{0:T(128)} %pad_add_fusion.place_ref, bf16[1040,128]{1,0:T(8,128)(2,1)} %copy-done.11, bf16[1040,128]{1,0:T(8,128)(2,1)} %copy-done.14, bf16[1040,128]{1,0:T(8,128)(2,1)} %copy-done.12, bf16[1040,128]{1,0:T(8,128)(2,1)} %copy-done.15, bf16[1040,128]{1,0:T(8,128)(2,1)} %copy-done.13, ...), custom_call_target="tpu_custom_call" | custom-call | tf_op jit(solution)/shard_map/pallas_call | solution.py:233
  119.7 6.8 %all-to-all-start = ((bf16[8,144,256]{2,1,0:T(8,128)(2,1)}), bf16[8,144,256]{2,1,0:T(8,128)(2,1)S(1)}, u32[]{:S(2)}, u32[]{:S(2)}) async-start(bf16[8,144,256]{2,1,0:T(8,128)(2,1)} %shard_map.74), calls=%async_computation | async-start | bytes 1179648 | tf_op jit(solution)/shard_map/all_to_all | solution.py:374
  126.6 0.8 copy.12.new_ref
  127.4 18.6 %all-to-all-done.in_ref = bf16[8,144,256]{2,1,0:T(8,128)(2,1)S(1)} async-done(((bf16[8,144,256]{2,1,0:T(8,128)(2,1)}), bf16[8,144,256]{2,1,0:T(8,128)(2,1)S(1)}, u32[]{:S(2)}, u32[]{:S(2)}) %all-to-all-start) | async-done | bytes 589856 | tf_op jit(solution)/shard_map/all_to_all | solution.py:374
  146.0 0.8 copy-done.1
  146.8 2.1 %combine.1.own_ref = bf16[64,512]{1,0:T(8,128)(2,1)} custom-call(bf16[8,144,256]{2,1,0:T(8,128)(2,1)} %copy-done.1, bf16[144,256]{1,0:T(8,128)(2,1)} %prepare.1.refs_10_.refs_6_.q_ref, bf16[2,128,256]{2,1,0:T(8,128)(2,1)} %copy.12.new_ref), custom_call_target="tpu_custom_call" | custom-call | tf_op jit(solution)/shard_map/combine/pallas_call | solution.py:276
  149.3 1.1 collective-permute-done.22.partner_ref
  151.1 6.3 %project.1 = bf16[8,64,512]{2,1,0:T(8,128)(2,1)} custom-call(s32[2]{0:T(128)} %pad_add_fusion.place_ref, bf16[64,512]{1,0:T(8,128)(2,1)} %combine.1.own_ref, bf16[64,512]{1,0:T(8,128)(2,1)} %copy-done.23, bf16[512,8192]{1,0:T(8,128)(2,1)} %w_own_ref.1, bf16[512,8192]{1,0:T(8,128)(2,1)} %collective-permute-done.23.w_partner_ref), custom_call_target="tpu_custom_call" | custom-call | tf_op jit(solution)/shard_map/project/pallas_call | solution.py:309
  157.3 21.4 %all_to_all.10 = bf16[8,64,512]{2,1,0:T(8,128)(2,1)S(1)} all-to-all(bf16[8,64,512]{2,1,0:T(8,128)(2,1)} %project.1), channel_id=1, replica_groups={{0,2,4,6,8,10,12,14},{1,3,5,7,9,11,13,15},{16,18,20,22,24,26,28,30},{17..., dimensions={0} | all-to-all | bytes 1048576 | tf_op jit(solution)/shard_map/all_to_all | solution.py:380
  178.7 0.7 reduce_sum.12
  (83 shorter events, 5.3 us)
Async XLA Ops:
  0.0 126.5 %copy-start = (bf16[64,2,1024]{2,1,0:T(2,128)(2,1)S(1)}, bf16[64,2,1024]{2,1,0:T(2,128)(2,1)}, u32[]{:S(2)}) copy-start(bf16[64,2,1024]{2,1,0:T(2,128)(2,1)} %param.8) | copy-start | bytes 786436
  0.0 150.4 %collective-permute-start.23 = (bf16[512,8192]{1,0:T(8,128)(2,1)}, bf16[512,8192]{1,0:T(8,128)(2,1)}, u32[]{:S(2)}, u32[]{:S(2)}) collective-permute-start(bf16[512,8192]{1,0:T(8,128)(2,1)} %w_own_ref.1), channel_id=1, source_target_pairs={{0,1},{1,0},{2,3},{3,2},{4,5},{5,4},{6,7},{7,6},{8,9},{9,8},{10,11... | collective-permute-start | bytes 25165832 | tf_op jit(solution)/shard_map/ppermute | solution.py:347
  22.6 8.4 %collective-permute-start.12 = (bf16[144,256]{1,0:T(8,128)(2,1)}, bf16[144,256]{1,0:T(8,128)(2,1)S(1)}, u32[]{:S(2)}, u32[]{:S(2)}) collective-permute-start(bf16[144,256]{1,0:T(8,128)(2,1)} %prepare.1.refs_10_.refs_6_.q_ref), channel_id=1, source_target_pairs={{0,112},{16,0},{32,16},{48,32},{64,48},{80,64},{96,80},{112,96},{1... | collective-permute-start | bytes 221192 | tf_op jit(solution)/shard_map/ppermute | solution.py:344
  22.6 8.6 %collective-permute-start.11 = (bf16[144,256]{1,0:T(8,128)(2,1)}, bf16[144,256]{1,0:T(8,128)(2,1)S(1)}, u32[]{:S(2)}, u32[]{:S(2)}) collective-permute-start(bf16[144,256]{1,0:T(8,128)(2,1)} %prepare.1.refs_10_.refs_6_.q_ref), channel_id=1, source_target_pairs={{0,96},{16,112},{32,0},{48,16},{64,32},{80,48},{96,64},{112,80},{1... | collective-permute-start | bytes 221192 | tf_op jit(solution)/shard_map/ppermute | solution.py:344
  22.6 9.4 %collective-permute-start.10 = (bf16[144,256]{1,0:T(8,128)(2,1)}, bf16[144,256]{1,0:T(8,128)(2,1)S(1)}, u32[]{:S(2)}, u32[]{:S(2)}) collective-permute-start(bf16[144,256]{1,0:T(8,128)(2,1)} %prepare.1.refs_10_.refs_6_.q_ref), channel_id=1, source_target_pairs={{0,80},{16,96},{32,112},{48,0},{64,16},{80,32},{96,48},{112,64},{1... | collective-permute-start | bytes 221192 | tf_op jit(solution)/shard_map/ppermute | solution.py:344
  22.8 13.0 %collective-permute-start.9 = (bf16[144,256]{1,0:T(8,128)(2,1)}, bf16[144,256]{1,0:T(8,128)(2,1)S(1)}, u32[]{:S(2)}, u32[]{:S(2)}) collective-permute-start(bf16[144,256]{1,0:T(8,128)(2,1)} %prepare.1.refs_10_.refs_6_.q_ref), channel_id=1, source_target_pairs={{0,64},{16,80},{32,96},{48,112},{64,0},{80,16},{96,32},{112,48},{1... | collective-permute-start | bytes 221192 | tf_op jit(solution)/shard_map/ppermute | solution.py:344
  31.0 62.4 %copy-start.3 = (bf16[1040,128]{1,0:T(8,128)(2,1)}, bf16[1040,128]{1,0:T(8,128)(2,1)S(1)}, u32[]{:S(2)}) copy-start(bf16[1040,128]{1,0:T(8,128)(2,1)S(1)} %get-tuple-element.21.refs_0_) | copy-start | bytes 798724
  31.0 62.3 %copy-start.4 = (bf16[144,256]{1,0:T(8,128)(2,1)}, bf16[144,256]{1,0:T(8,128)(2,1)S(1)}, u32[]{:S(2)}) copy-start(bf16[144,256]{1,0:T(8,128)(2,1)S(1)} %collective-permute-done.12.refs_17_.refs_13_) | copy-start | bytes 221188
  31.0 23.4 %collective-permute-start.20 = (bf16[1040,128]{1,0:T(8,128)(2,1)S(1)}, bf16[1040,128]{1,0:T(8,128)(2,1)S(1)}, u32[]{:S(2)}, u32[]{:S(2)}) collective-permute-start(bf16[1040,128]{1,0:T(8,128)(2,1)S(1)} %get-tuple-element.17), channel_id=1, source_target_pairs={{0,12},{1,13},{2,14},{3,15},{4,0},{5,1},{6,2},{7,3},{8,4},{9,5},{1... | collective-permute-start | bytes 798728 | tf_op jit(solution)/shard_map/ppermute | solution.py:341
  31.2 62.2 %copy-start.5 = (bf16[144,256]{1,0:T(8,128)(2,1)}, bf16[144,256]{1,0:T(8,128)(2,1)S(1)}, u32[]{:S(2)}) copy-start(bf16[144,256]{1,0:T(8,128)(2,1)S(1)} %collective-permute-done.11.refs_16_.refs_12_) | copy-start | bytes 221188
  31.2 25.5 %collective-permute-start = (bf16[1040,128]{1,0:T(8,128)(2,1)S(1)}, bf16[1040,128]{1,0:T(8,128)(2,1)S(1)}, u32[]{:S(2)}, u32[]{:S(2)}) collective-permute-start(bf16[1040,128]{1,0:T(8,128)(2,1)S(1)} %get-tuple-element.18), channel_id=1, source_target_pairs={{0,6},{1,7},{2,8},{3,9},{4,10},{5,11},{6,12},{7,13},{8,14},{9,15},... | collective-permute-start | bytes 798728 | tf_op jit(solution)/shard_map/ppermute | solution.py:341
  32.0 61.3 %copy-start.6 = (bf16[144,256]{1,0:T(8,128)(2,1)}, bf16[144,256]{1,0:T(8,128)(2,1)S(1)}, u32[]{:S(2)}) copy-start(bf16[144,256]{1,0:T(8,128)(2,1)S(1)} %collective-permute-done.10.refs_15_.refs_11_) | copy-start | bytes 221188
  32.0 25.9 %collective-permute-start.2 = (bf16[1040,128]{1,0:T(8,128)(2,1)S(1)}, bf16[1040,128]{1,0:T(8,128)(2,1)S(1)}, u32[]{:S(2)}, u32[]{:S(2)}) collective-permute-start(bf16[1040,128]{1,0:T(8,128)(2,1)S(1)} %get-tuple-element.19), channel_id=1, source_target_pairs={{0,10},{1,11},{2,12},{3,13},{4,14},{5,15},{6,0},{7,1},{8,2},{9,3},... | collective-permute-start | bytes 798728 | tf_op jit(solution)/shard_map/ppermute | solution.py:341
  35.8 57.6 %copy-start.7 = (bf16[144,256]{1,0:T(8,128)(2,1)}, bf16[144,256]{1,0:T(8,128)(2,1)S(1)}, u32[]{:S(2)}) copy-start(bf16[144,256]{1,0:T(8,128)(2,1)S(1)} %collective-permute-done.9.refs_14_.refs_10_) | copy-start | bytes 221188
  35.8 8.2 %collective-permute-start.8 = (bf16[144,256]{1,0:T(8,128)(2,1)S(1)}, bf16[144,256]{1,0:T(8,128)(2,1)S(1)}, u32[]{:S(2)}, u32[]{:S(2)}) collective-permute-start(bf16[144,256]{1,0:T(8,128)(2,1)S(1)} %copy-done.2), channel_id=1, source_target_pairs={{0,48},{16,64},{32,80},{48,96},{64,112},{80,0},{96,16},{112,32},{1... | collective-permute-start | bytes 221192 | tf_op jit(solution)/shard_map/ppermute | solution.py:344
  44.0 5.6 %collective-permute-start.7 = (bf16[144,256]{1,0:T(8,128)(2,1)S(1)}, bf16[144,256]{1,0:T(8,128)(2,1)S(1)}, u32[]{:S(2)}, u32[]{:S(2)}) collective-permute-start(bf16[144,256]{1,0:T(8,128)(2,1)S(1)} %copy-done.2), channel_id=1, source_target_pairs={{0,32},{16,48},{32,64},{48,80},{64,96},{80,112},{96,0},{112,16},{1... | collective-permute-start | bytes 221192 | tf_op jit(solution)/shard_map/ppermute | solution.py:344
  49.6 4.8 %collective-permute-start.6 = (bf16[144,256]{1,0:T(8,128)(2,1)S(1)}, bf16[144,256]{1,0:T(8,128)(2,1)S(1)}, u32[]{:S(2)}, u32[]{:S(2)}) collective-permute-start(bf16[144,256]{1,0:T(8,128)(2,1)S(1)} %copy-done.2), channel_id=1, source_target_pairs={{0,16},{16,32},{32,48},{48,64},{64,80},{80,96},{96,112},{112,0},{1... | collective-permute-start | bytes 221192 | tf_op jit(solution)/shard_map/ppermute | solution.py:344
  54.4 11.4 %collective-permute-start.4 = (bf16[1040,128]{1,0:T(8,128)(2,1)S(1)}, bf16[1040,128]{1,0:T(8,128)(2,1)S(1)}, u32[]{:S(2)}, u32[]{:S(2)}) collective-permute-start(bf16[1040,128]{1,0:T(8,128)(2,1)S(1)} %get-tuple-element.20), channel_id=1, source_target_pairs={{0,8},{1,9},{2,10},{3,11},{4,12},{5,13},{6,14},{7,15},{8,0},{9,1},... | collective-permute-start | bytes 798728 | tf_op jit(solution)/shard_map/ppermute | solution.py:341
  54.4 21.2 %collective-permute-start.14 = (bf16[1040,128]{1,0:T(8,128)(2,1)S(1)}, bf16[1040,128]{1,0:T(8,128)(2,1)S(1)}, u32[]{:S(2)}, u32[]{:S(2)}) collective-permute-start(bf16[1040,128]{1,0:T(8,128)(2,1)S(1)} %get-tuple-element.22), channel_id=1, source_target_pairs={{0,2},{1,3},{2,4},{3,5},{4,6},{5,7},{6,8},{7,9},{8,10},{9,11},{10,... | collective-permute-start | bytes 798728 | tf_op jit(solution)/shard_map/ppermute | solution.py:341
  56.6 50.0 %copy-start.11 = (bf16[1040,128]{1,0:T(8,128)(2,1)}, bf16[1040,128]{1,0:T(8,128)(2,1)S(1)}, u32[]{:S(2)}) copy-start(bf16[1040,128]{1,0:T(8,128)(2,1)S(1)} %collective-permute-done.refs_0_) | copy-start | bytes 798724
  56.6 23.6 %collective-permute-start.16 = (bf16[1040,128]{1,0:T(8,128)(2,1)S(1)}, bf16[1040,128]{1,0:T(8,128)(2,1)S(1)}, u32[]{:S(2)}, u32[]{:S(2)}) collective-permute-start(bf16[1040,128]{1,0:T(8,128)(2,1)S(1)} %get-tuple-element.23), channel_id=1, source_target_pairs={{0,14},{1,15},{2,0},{3,1},{4,2},{5,3},{6,4},{7,5},{8,6},{9,7},{10,... | collective-permute-start | bytes 798728 | tf_op jit(solution)/shard_map/ppermute | solution.py:341
  58.0 26.5 %collective-permute-start.18 = (bf16[1040,128]{1,0:T(8,128)(2,1)S(1)}, bf16[1040,128]{1,0:T(8,128)(2,1)}, u32[]{:S(2)}, u32[]{:S(2)}) collective-permute-start(bf16[1040,128]{1,0:T(8,128)(2,1)S(1)} %get-tuple-element.24), channel_id=1, source_target_pairs={{0,4},{1,5},{2,6},{3,7},{4,8},{5,9},{6,10},{7,11},{8,12},{9,13},{1... | collective-permute-start | bytes 798728 | tf_op jit(solution)/shard_map/ppermute | solution.py:341
  65.9 24.2 %collective-permute-start.13 = (bf16[1040,128]{1,0:T(8,128)(2,1)S(1)}, bf16[1040,128]{1,0:T(8,128)(2,1)}, u32[]{:S(2)}, u32[]{:S(2)}) collective-permute-start(bf16[1040,128]{1,0:T(8,128)(2,1)S(1)} %get-tuple-element.21.refs_0_), channel_id=1, source_target_pairs={{0,1},{1,0},{2,3},{3,2},{4,5},{5,4},{6,7},{7,6},{8,9},{9,8},{10,11... | collective-permute-start | bytes 798728 | tf_op jit(solution)/shard_map/ppermute | solution.py:347
  75.6 14.4 %collective-permute-start.21 = (bf16[1040,128]{1,0:T(8,128)(2,1)S(1)}, bf16[1040,128]{1,0:T(8,128)(2,1)S(1)}, u32[]{:S(2)}, u32[]{:S(2)}) collective-permute-start(bf16[1040,128]{1,0:T(8,128)(2,1)S(1)} %collective-permute-done.20.refs_8_), channel_id=1, source_target_pairs={{0,1},{1,0},{2,3},{3,2},{4,5},{5,4},{6,7},{7,6},{8,9},{9,8},{10,11... | collective-permute-start | bytes 798728 | tf_op jit(solution)/shard_map/ppermute | solution.py:347
  80.2 10.5 %collective-permute-start.15 = (bf16[1040,128]{1,0:T(8,128)(2,1)S(1)}, bf16[1040,128]{1,0:T(8,128)(2,1)S(1)}, u32[]{:S(2)}, u32[]{:S(2)}) collective-permute-start(bf16[1040,128]{1,0:T(8,128)(2,1)S(1)} %collective-permute-done.14.refs_2_), channel_id=1, source_target_pairs={{0,1},{1,0},{2,3},{3,2},{4,5},{5,4},{6,7},{7,6},{8,9},{9,8},{10,11... | collective-permute-start | bytes 798728 | tf_op jit(solution)/shard_map/ppermute | solution.py:347
  84.5 6.8 %collective-permute-start.17 = (bf16[1040,128]{1,0:T(8,128)(2,1)S(1)}, bf16[1040,128]{1,0:T(8,128)(2,1)S(1)}, u32[]{:S(2)}, u32[]{:S(2)}) collective-permute-start(bf16[1040,128]{1,0:T(8,128)(2,1)S(1)} %collective-permute-done.16.refs_4_), channel_id=1, source_target_pairs={{0,1},{1,0},{2,3},{3,2},{4,5},{5,4},{6,7},{7,6},{8,9},{9,8},{10,11... | collective-permute-start | bytes 798728 | tf_op jit(solution)/shard_map/ppermute | solution.py:347
  90.1 16.5 %collective-permute-start.1 = (bf16[1040,128]{1,0:T(8,128)(2,1)S(1)}, bf16[1040,128]{1,0:T(8,128)(2,1)S(1)}, u32[]{:S(2)}, u32[]{:S(2)}) collective-permute-start(bf16[1040,128]{1,0:T(8,128)(2,1)S(1)} %collective-permute-done.refs_0_), channel_id=1, source_target_pairs={{0,1},{1,0},{2,3},{3,2},{4,5},{5,4},{6,7},{7,6},{8,9},{9,8},{10,11... | collective-permute-start | bytes 798728 | tf_op jit(solution)/shard_map/ppermute | solution.py:347
  90.1 3.3 %collective-permute-start.19 = (bf16[1040,128]{1,0:T(8,128)(2,1)}, bf16[1040,128]{1,0:T(8,128)(2,1)}, u32[]{:S(2)}, u32[]{:S(2)}) collective-permute-start(bf16[1040,128]{1,0:T(8,128)(2,1)} %collective-permute-done.18.refs_6_), channel_id=1, source_target_pairs={{0,1},{1,0},{2,3},{3,2},{4,5},{5,4},{6,7},{7,6},{8,9},{9,8},{10,11... | collective-permute-start | bytes 798728 | tf_op jit(solution)/shard_map/ppermute | solution.py:347
  90.8 15.8 %collective-permute-start.3 = (bf16[1040,128]{1,0:T(8,128)(2,1)S(1)}, bf16[1040,128]{1,0:T(8,128)(2,1)S(1)}, u32[]{:S(2)}, u32[]{:S(2)}) collective-permute-start(bf16[1040,128]{1,0:T(8,128)(2,1)S(1)} %collective-permute-done.2.refs_2_), channel_id=1, source_target_pairs={{0,1},{1,0},{2,3},{3,2},{4,5},{5,4},{6,7},{7,6},{8,9},{9,8},{10,11... | collective-permute-start | bytes 798728 | tf_op jit(solution)/shard_map/ppermute | solution.py:347
  92.2 14.4 %collective-permute-start.5 = (bf16[1040,128]{1,0:T(8,128)(2,1)S(1)}, bf16[1040,128]{1,0:T(8,128)(2,1)S(1)}, u32[]{:S(2)}, u32[]{:S(2)}) collective-permute-start(bf16[1040,128]{1,0:T(8,128)(2,1)S(1)} %collective-permute-done.4.refs_4_), channel_id=1, source_target_pairs={{0,1},{1,0},{2,3},{3,2},{4,5},{5,4},{6,7},{7,6},{8,9},{9,8},{10,11... | collective-permute-start | bytes 798728 | tf_op jit(solution)/shard_map/ppermute | solution.py:347
  119.7 26.2 %all-to-all-start = ((bf16[8,144,256]{2,1,0:T(8,128)(2,1)}), bf16[8,144,256]{2,1,0:T(8,128)(2,1)S(1)}, u32[]{:S(2)}, u32[]{:S(2)}) async-start(bf16[8,144,256]{2,1,0:T(8,128)(2,1)} %shard_map.74), calls=%async_computation | async-start | bytes 1179648 | tf_op jit(solution)/shard_map/all_to_all | solution.py:374
  148.8 1.6 collective-permute-start.22
  (17 other events, 308.5 us)

commit v3 on v2

--- a/solution.py
+++ b/solution.py
@@ -25,16 +25,15 @@
     return [part.astype(jnp.float32) for part in (hi, mid, low)]
 
 
-def prepare(queries, block_table, prefix_len, heads_dev, slots):
+def prepare(queries, block_table, prefix_len, heads_dev, slots, group_count):
     req_rows = queries.shape[0]
     list_length = block_table.shape[1]
     cols = heads_dev * req_rows
     assert slots == cols
 
     def kernel(q_ref, table_ref, length_ref, out_ref):
-        for h in range(heads_dev):
-            one = q_ref[:, h * HEAD_SIZE : (h + 1) * HEAD_SIZE].astype(jnp.float32)
-            out_ref[0:HEAD_SIZE, h * req_rows : (h + 1) * req_rows] = one.T.astype(jnp.bfloat16)
+        heads = [q_ref[:, h * HEAD_SIZE : (h + 1) * HEAD_SIZE].astype(jnp.float32).T for h in range(heads_dev)]
+        query = jnp.concatenate(heads, axis=1).astype(jnp.bfloat16)
         length = length_ref[...]
         high = lax.div(length, 8)
         small = jnp.concatenate([table_ref[...], high, length - 8 * high, length], axis=0).astype(jnp.float32)
@@ -48,28 +47,31 @@
         named = jnp.max(hit, axis=0, keepdims=True)
         small = jnp.concatenate([small[0:META_ROWS]] * heads_dev, axis=1)
         sub = lax.broadcasted_iota(jnp.int32, (META_ROWS, cols), 0)
-        out_ref[HEAD_SIZE:] = jnp.where(sub == list_length + 2, named, small).astype(jnp.bfloat16)
+        small = jnp.where(sub == list_length + 2, named, small).astype(jnp.bfloat16)
+        for g in range(group_count):
+            out_ref[g, 0:HEAD_SIZE] = query
+            out_ref[g, HEAD_SIZE:] = small
 
     return pl.pallas_call(
         kernel,
-        out_shape=jax.ShapeDtypeStruct((HEAD_SIZE + META_ROWS, cols), jnp.bfloat16),
+        out_shape=jax.ShapeDtypeStruct((group_count, HEAD_SIZE + META_ROWS, cols), jnp.bfloat16),
         interpret=INTERPRET,
         name="prepare",
     )(queries, block_table.T, prefix_len.reshape(1, -1))
 
 
-def attend_chunk(place, bufs, queries_t, state, shifts, y_count, group_count, per_batch, first, last):
+def attend_chunk(place, bufs, queries_t, state, shifts, y_count, per_batch, first, last):
     n_buf = len(bufs)
     buf_rows = bufs[0].shape[0]
-    rows, cols = queries_t[0].shape
+    group_count, rows, cols = queries_t.shape
     limit = 2 * n_buf
     factor = math.log2(math.e) / math.sqrt(HEAD_SIZE)
     int_rows = group_count + 8 * ((n_buf + 7) // 8)
 
     def kernel(place_ref, *refs):
         buf_refs = refs[:n_buf]
-        q_refs = refs[n_buf : n_buf + group_count]
-        rest = list(refs[n_buf + group_count :])
+        q_ref = refs[n_buf]
+        rest = list(refs[n_buf + 1 :])
         if not first:
             acc_in, ml_in = rest[:2]
             rest = rest[2:]
@@ -79,16 +81,20 @@
         else:
             acc_out, ml_out = rest[:2]
             rest = rest[2:]
-        (acc, ml, store, query_all, out_all, ints, numbers, item_row, item_slot, sem_store, sem_query, sem_acc, sem_ml, sem_int, sem_out) = rest
+        (acc, ml, store, lists, query_all, out_all, ints, numbers, item_row, item_slot, sem_store, sem_list, sem_query, sem_acc, sem_ml, sem_int, sem_out) = rest
         tp_rank = place_ref[0]
         row = place_ref[1]
         core = lax.rem(tp_rank, 2)
 
-        query_copies = [pltpu.make_async_copy(q_refs[g], query_all.at[g], sem_query.at[g]) for g in range(group_count)]
+        query_copies = [pltpu.make_async_copy(q_ref.at[g], query_all.at[g], sem_query.at[g]) for g in range(group_count)]
         store_copies = [
             pltpu.make_async_copy(buf_refs[b], store.at[pl.ds(b * buf_rows, buf_rows)], sem_store.at[b]) for b in range(n_buf)
         ]
-        for one in query_copies + store_copies:
+        list_copies = [
+            pltpu.make_async_copy(buf_refs[b].at[pl.ds(buf_rows - META_ROWS, META_ROWS)], lists.at[b], sem_list.at[b])
+            for b in range(n_buf)
+        ]
+        for one in list_copies + query_copies + store_copies:
             one.start()
         if first:
             acc[...] = jnp.zeros(acc.shape, jnp.float32)
@@ -98,30 +104,31 @@
             ml_copy.start()
             for g in range(group_count):
                 pltpu.make_async_copy(acc_in.at[g], acc.at[g], sem_acc.at[g]).start()
-        for one in query_copies + store_copies:
+        for one in list_copies + query_copies:
             one.wait()
         for g in range(group_count):
             ints[g : g + 1] = query_all[g, HEAD_SIZE:].astype(jnp.float32)[NAMED_ROW : NAMED_ROW + 1].astype(jnp.int32)
         for b in range(n_buf):
-            pages = store[(b + 1) * buf_rows - META_ROWS : (b + 1) * buf_rows].astype(jnp.float32)
+            pages = lists[b].astype(jnp.float32)
             ints[group_count + b : group_count + b + 1, 0:HEAD_SIZE] = pages[0:1].astype(jnp.int32)
         int_copy = pltpu.make_async_copy(ints, numbers, sem_int)
         int_copy.start()
         int_copy.wait()
         if not first:
             ml_copy.wait()
+        for one in store_copies:
+            one.wait()
 
         entry = lax.broadcasted_iota(jnp.int32, (8, cols), 0).astype(jnp.float32)
         token = lax.broadcasted_iota(jnp.int32, (PAGE_TOKENS, cols), 0).astype(jnp.float32)
 
         def group(g, _):
-            number = lax.rem(row + group_count - g, group_count)
             count = jnp.int32(0)
             for b in range(n_buf):
                 source_y = lax.rem(lax.div(tp_rank, 2) + y_count - shifts[b // 2], y_count)
                 owner = 2 * source_y + (core if b % 2 == 0 else 1 - core)
                 for column in range(2):
-                    page = numbers[group_count + b, 2 * number + column]
+                    page = numbers[group_count + b, 2 * g + column]
                     slot = (row * 2 * y_count + owner) * 2 + column
                     used = numbers[g, slot]
                     item_row[count] = b * buf_rows + page * (2 * PAGE_TOKENS)
@@ -187,7 +194,7 @@
                 for n, part in enumerate(split3(top) + split3(total)):
                     packed = jnp.where(sub == n, part, packed)
                 out_all[g, HEAD_SIZE:] = packed.astype(jnp.bfloat16)
-                pltpu.make_async_copy(out_all.at[g], out_ref.at[number], sem_out.at[g]).start()
+                pltpu.make_async_copy(out_all.at[g], out_ref.at[g], sem_out.at[g]).start()
             else:
                 pltpu.make_async_copy(acc.at[g], acc_out.at[g], sem_out.at[g]).start()
             return 0
@@ -215,12 +222,14 @@
         pltpu.VMEM((group_count, HEAD_SIZE, cols), jnp.float32),
         pltpu.VMEM((group_count, 8, cols), jnp.float32),
         pltpu.VMEM((n_buf * buf_rows, HEAD_SIZE), jnp.bfloat16),
+        pltpu.VMEM((n_buf, META_ROWS, HEAD_SIZE), jnp.bfloat16),
         pltpu.VMEM((group_count, rows, cols), jnp.bfloat16),
         pltpu.VMEM((n_out_slots, HEAD_SIZE + STAT_ROWS, cols), jnp.bfloat16),
         pltpu.VMEM((int_rows, cols), jnp.int32),
         pltpu.SMEM((int_rows, cols), jnp.int32),
         pltpu.SMEM((limit + per_batch,), jnp.int32),
         pltpu.SMEM((limit + per_batch,), jnp.int32),
+        pltpu.SemaphoreType.DMA((n_buf,)),
         pltpu.SemaphoreType.DMA((n_buf,)),
         pltpu.SemaphoreType.DMA((group_count,)),
         pltpu.SemaphoreType.DMA((group_count,)),
@@ -229,7 +238,7 @@
         pltpu.SemaphoreType.DMA((group_count,)),
     ]
     anywhere = pl.BlockSpec(memory_space=pltpu.MemorySpace.HBM)
-    n_in = n_buf + group_count + (0 if first else 2)
+    n_in = n_buf + (1 if first else 3)
     return pl.pallas_call(
         kernel,
         out_shape=out_shape,
@@ -241,16 +250,16 @@
             scratch_shapes=scratch,
         ),
         interpret=INTERPRET,
-    )(place, *bufs, *queries_t, *(() if first else state))
-
-
-def combine(arrived, query_t, newest_t, heads_dev):
+    )(place, *bufs, queries_t, *(() if first else state))
+
+
+def combine(arrived, query_blocks, newest_t, heads_dev):
     parts, _, cols = arrived.shape
     req_rows = cols // heads_dev
     factor = math.log2(math.e) / math.sqrt(HEAD_SIZE)
 
     def kernel(in_ref, q_ref, new_ref, out_ref):
-        query = q_ref[0:HEAD_SIZE].astype(jnp.float32)
+        query = q_ref[0, 0:HEAD_SIZE].astype(jnp.float32)
         own = jnp.sum(query * new_ref[0].astype(jnp.float32), axis=0, keepdims=True) * factor
         top = own
         tops, totals = [], []
@@ -275,10 +284,17 @@
 
     return pl.pallas_call(
         kernel,
+        grid=(1,),
         out_shape=jax.ShapeDtypeStruct((req_rows, heads_dev * HEAD_SIZE), jnp.bfloat16),
+        in_specs=[
+            pl.BlockSpec(arrived.shape, lambda i: (0, 0, 0)),
+            pl.BlockSpec((1,) + query_blocks.shape[1:], lambda i: (0, 0, 0)),
+            pl.BlockSpec(newest_t.shape, lambda i: (0, 0, 0)),
+        ],
+        out_specs=pl.BlockSpec((req_rows, heads_dev * HEAD_SIZE), lambda i: (0, 0)),
         interpret=INTERPRET,
         name="combine",
-    )(arrived, query_t, newest_t)
+    )(arrived, query_blocks, newest_t)
 
 
 def project(place, mix_own, mix_partner, weight_own, weight_partner, y_count):
@@ -340,8 +356,8 @@
     def along_y(x, shift):
         return lax.ppermute(x, "tp", [(i, (i + 2 * shift) % tp_count) for i in range(tp_count)])
 
-    def along_x(x, shift):
-        return lax.ppermute(x, "grp", [(i, (i + shift) % group_count) for i in range(group_count)])
+    def along_x(x):
+        return lax.all_to_all(x, "grp", split_axis=0, concat_axis=0, tiled=True)
 
     def to_other_core(x):
         return lax.ppermute(x, "tp", swap)
@@ -357,8 +373,8 @@
         partner[shift] = to_other_core(own[shift])
     weight_partner = to_other_core(out_weight)
 
-    query_t = prepare(queries, block_table, prefix_len, heads_dev, slots)
-    queries_t = [along_x(query_t, s) if s else query_t for s in range(group_count)]
+    query_blocks = prepare(queries, block_table, prefix_len, heads_dev, slots, group_count)
+    queries_t = along_x(query_blocks)
     place = jnp.stack([tp_rank, row])
 
     newest = lax.dynamic_slice_in_dim(newest_key_value, y * HEAD_SIZE, HEAD_SIZE, 2)
@@ -369,11 +385,11 @@
         bufs = [b for s in shifts for b in (own[s], partner[s])]
         last = n == len(CHUNKS) - 1
         state = attend_chunk(
-            place, bufs, queries_t, state, shifts, y_count, group_count, 4, n == 0, last
+            place, bufs, queries_t, state, shifts, y_count, 4, n == 0, last
         )
-    arrived = lax.all_to_all(state[0], "grp", split_axis=0, concat_axis=0, tiled=True)
-
-    mix_own = combine(arrived, query_t, newest_t, heads_dev)
+    arrived = along_x(state[0])
+
+    mix_own = combine(arrived, query_blocks, newest_t, heads_dev)
     mix_partner = to_other_core(mix_own)
     partial = project(place, mix_own, mix_partner, out_weight, weight_partner, y_count)
     same_core = [[2 * i + c for i in range(y_count)] for c in range(2)]

time: 180 us -> 165 us (0.917)
  the two profiles are of different devices: /device:TPU:513 before, /device:TPU:641 now
where the time goes in v3:
time: 165 us
  waiting for transfers between devices  49.2 us (30%)
  starting transfers between devices  48.3 us (29%)
  Pallas kernels  35.9 us (22%)
  blocking collectives  21.4 us (13%)
  local copies, waits for them, and re-layouts  6.73 us (4%)
  other arithmetic  2.85 us (2%)
    ppermute x7, waiting for transfers between devices, along_y(): lax.ppermute(x, 'tp', [(i, (i + 2 * shift) % tp_count) for i in range(tp_...  29.2 us
    pallas_call x2, Pallas kernels, attend_chunk(): pl.pallas_call(kernel, out_shape=out_shape, grid_spec=pltpu.PrefetchScala...  25.2 us
    ppermute x7, starting transfers between devices, along_y(): lax.ppermute(x, 'tp', [(i, (i + 2 * shift) % tp_count) for i in range(tp_...  24.2 us
    all_to_all x1, blocking collectives, per_device_inner(): lax.all_to_all(partial, 'tp', split_axis=0, concat_axis=0, axis_index_gro...  21.4 us
    all_to_all x2, waiting for transfers between devices, along_x(): return lax.all_to_all(x, 'grp', split_axis=0, concat_axis=0, tiled=True)  18.6 us
    all_to_all x2, starting transfers between devices, along_x(): return lax.all_to_all(x, 'grp', split_axis=0, concat_axis=0, tiled=True)  16.9 us
    ppermute x10, starting transfers between devices, to_other_core(): return lax.ppermute(x, 'tp', swap)  7.28 us
    pallas_call x1, Pallas kernels, project(): pl.pallas_call(kernel, out_shape=jax.ShapeDtypeStruct((y_count, req_rows,...  6.29 us
  transfers between devices with their start and end apart: 19, of which 6 were waited for; matrix products, arithmetic and copies ran while one was open for 3% of the time, Pallas kernels for 18%

profile of v3, /device:TPU:641, one launch (start us, length us, event | category | flops | bytes accessed | tf_op | source)
XLA Modules:
  0.0 164.6 jit_solution(99525834918065502)
XLA Ops:
  0.0 0.6 collective-permute-start.16
  0.6 0.7 convert_element_type.18
  1.5 1.7 %constant_dynamic-slice_fusion = (bf16[4,2,128,128]{3,2,1,0:T(8,128)(2,1)S(1)}, bf16[4,2,128,128]{3,2,1,0:T(8,128)(2,1)S(1)}, bf16[4,2,128,128]{3,2,1,0:T(8,128)...) fusion(bf16[4,2,128,1024]{3,2,1,0:T(8,128)(2,1)} %param.9, ...), kind=kLoop, calls=%fused_computation.11 | loop fusion | bytes 4194336 | tf_op jit(solution)/shard_map/dynamic_slice | solution.py:369
  3.2 0.9 fusion.8
  4.1 11.2 %collective-permute-start.13 = (bf16[1040,128]{1,0:T(8,128)(2,1)}, bf16[1040,128]{1,0:T(8,128)(2,1)}, u32[]{:S(2)}, u32[]{:S(2)}) collective-permute-start(bf16[1040,128]{1,0:T(8,128)(2,1)} %get-tuple-element.17), channel_id=1, source_target_pairs={{0,12},{1,13},{2,14},{3,15},{4,0},{5,1},{6,2},{7,3},{8,4},{9,5},{1... | collective-permute-start | bytes 798728 | tf_op jit(solution)/shard_map/ppermute | solution.py:357
  15.3 4.5 %collective-permute-start.2 = (bf16[1040,128]{1,0:T(8,128)(2,1)S(1)}, bf16[1040,128]{1,0:T(8,128)(2,1)S(1)}, u32[]{:S(2)}, u32[]{:S(2)}) collective-permute-start(bf16[1040,128]{1,0:T(8,128)(2,1)S(1)} %get-tuple-element.19), channel_id=1, source_target_pairs={{0,10},{1,11},{2,12},{3,13},{4,14},{5,15},{6,0},{7,1},{8,2},{9,3},... | collective-permute-start | bytes 798728 | tf_op jit(solution)/shard_map/ppermute | solution.py:357
  19.7 2.3 %prepare.1.q_ref = bf16[8,144,256]{2,1,0:T(8,128)(2,1)} custom-call(bf16[64,512]{1,0:T(8,128)(2,1)} %q_ref.1, s32[8,64]{1,0:T(8,128)} %bitcast.26, s32[1,64]{1,0:T(1,128)} %bitcast.27), custom_call_target="tpu_custom_call" | custom-call | tf_op jit(solution)/shard_map/prepare/pallas_call | solution.py:55
  22.1 7.0 %all-to-all-start = ((bf16[8,144,256]{2,1,0:T(8,128)(2,1)}), bf16[8,144,256]{2,1,0:T(8,128)(2,1)S(1)}, u32[]{:S(2)}, u32[]{:S(2)}) async-start(bf16[8,144,256]{2,1,0:T(8,128)(2,1)} %prepare.1.q_ref), calls=%async_computation | async-start | bytes 1179648 | tf_op jit(solution)/shard_map/all_to_all | solution.py:360
  29.1 1.3 collective-permute-start.4
  30.4 3.8 %collective-permute-start.7 = (bf16[1040,128]{1,0:T(8,128)(2,1)S(1)}, bf16[1040,128]{1,0:T(8,128)(2,1)S(1)}, u32[]{:S(2)}, u32[]{:S(2)}) collective-permute-start(bf16[1040,128]{1,0:T(8,128)(2,1)S(1)} %get-tuple-element.22), channel_id=1, source_target_pairs={{0,2},{1,3},{2,4},{3,5},{4,6},{5,7},{6,8},{7,9},{8,10},{9,11},{10,... | collective-permute-start | bytes 798728 | tf_op jit(solution)/shard_map/ppermute | solution.py:357
  34.2 3.4 %collective-permute-start.9 = (bf16[1040,128]{1,0:T(8,128)(2,1)S(1)}, bf16[1040,128]{1,0:T(8,128)(2,1)S(1)}, u32[]{:S(2)}, u32[]{:S(2)}) collective-permute-start(bf16[1040,128]{1,0:T(8,128)(2,1)S(1)} %get-tuple-element.23), channel_id=1, source_target_pairs={{0,14},{1,15},{2,0},{3,1},{4,2},{5,3},{6,4},{7,5},{8,6},{9,7},{10,... | collective-permute-start | bytes 798728 | tf_op jit(solution)/shard_map/ppermute | solution.py:357
  37.6 17.7 %collective-permute-done.2.refs_2_ = bf16[1040,128]{1,0:T(8,128)(2,1)S(1)} collective-permute-done((bf16[1040,128]{1,0:T(8,128)(2,1)S(1)}, bf16[1040,128]{1,0:T(8,128)(2,1)S(1)}, u32[]{:S(2)}, u32[]{:S(2)}) %collective-permute-start.2) | collective-permute-done | bytes 266272 | tf_op jit(solution)/shard_map/ppermute | solution.py:357
  55.3 1.8 %collective-permute-start.6 = (bf16[1040,128]{1,0:T(8,128)(2,1)S(1)}, bf16[1040,128]{1,0:T(8,128)(2,1)S(1)}, u32[]{:S(2)}, u32[]{:S(2)}) collective-permute-start(bf16[1040,128]{1,0:T(8,128)(2,1)S(1)} %get-tuple-element.21.refs_0_), channel_id=1, source_target_pairs={{0,1},{1,0},{2,3},{3,2},{4,5},{5,4},{6,7},{7,6},{8,9},{9,8},{10,11... | collective-permute-start | bytes 798728 | tf_op jit(solution)/shard_map/ppermute | solution.py:363
  57.3 3.9 %collective-permute-done.9.refs_4_ = bf16[1040,128]{1,0:T(8,128)(2,1)S(1)} collective-permute-done((bf16[1040,128]{1,0:T(8,128)(2,1)S(1)}, bf16[1040,128]{1,0:T(8,128)(2,1)S(1)}, u32[]{:S(2)}, u32[]{:S(2)}) %collective-permute-start.9) | collective-permute-done | bytes 266272 | tf_op jit(solution)/shard_map/ppermute | solution.py:357
  61.1 1.0 collective-permute-start.8
  62.1 7.6 %collective-permute-done.11.refs_6_ = bf16[1040,128]{1,0:T(8,128)(2,1)S(1)} collective-permute-done((bf16[1040,128]{1,0:T(8,128)(2,1)S(1)}, bf16[1040,128]{1,0:T(8,128)(2,1)S(1)}, u32[]{:S(2)}, u32[]{:S(2)}) %collective-permute-start.11) | collective-permute-done | bytes 266272 | tf_op jit(solution)/shard_map/ppermute | solution.py:357
  69.7 2.2 %collective-permute-start.10 = (bf16[1040,128]{1,0:T(8,128)(2,1)S(1)}, bf16[1040,128]{1,0:T(8,128)(2,1)S(1)}, u32[]{:S(2)}, u32[]{:S(2)}) collective-permute-start(bf16[1040,128]{1,0:T(8,128)(2,1)S(1)} %collective-permute-done.9.refs_4_), channel_id=1, source_target_pairs={{0,1},{1,0},{2,3},{3,2},{4,5},{5,4},{6,7},{7,6},{8,9},{9,8},{10,11... | collective-permute-start | bytes 798728 | tf_op jit(solution)/shard_map/ppermute | solution.py:363
  73.1 0.7 copy-done.15
  74.8 0.8 copy-done.1
  75.6 14.8 %shard_map.73 = (f32[8,128,256]{2,1,0:T(8,128)}, f32[8,8,256]{2,1,0:T(8,128)}) custom-call(s32[2]{0:T(128)} %pad_add_fusion.place_ref, bf16[1040,128]{1,0:T(8,128)(2,1)} %copy-done.3, bf16[1040,128]{1,0:T(8,128)(2,1)} %copy-done.13, bf16[1040,128]{1,0:T(8,128)(2,1)} %copy-done.10, bf16[1040,128]{1,0:T(8,128)(2,1)} %collective-permute-done.8.refs_3_, ...), custom_call_target="tpu_custom_call" | custom-call | tf_op jit(solution)/shard_map/pallas_call | solution.py:242
  90.5 0.6 copy-done.7
  91.4 10.4 %shard_map.74 = bf16[8,144,256]{2,1,0:T(8,128)(2,1)} custom-call(s32[2]{0:T(128)} %pad_add_fusion.place_ref, bf16[1040,128]{1,0:T(8,128)(2,1)} %copy-done.4, bf16[1040,128]{1,0:T(8,128)(2,1)} %copy-done.7, bf16[1040,128]{1,0:T(8,128)(2,1)} %copy-done.5, bf16[1040,128]{1,0:T(8,128)(2,1)} %copy-done.8, bf16[1040,128]{1,0:T(8,128)(2,1)} %copy-done.6, ...), custom_call_target="tpu_custom_call" | custom-call | tf_op jit(solution)/shard_map/pallas_call | solution.py:242
  101.8 9.9 %all-to-all-start.1 = ((bf16[8,144,256]{2,1,0:T(8,128)(2,1)}), bf16[8,144,256]{2,1,0:T(8,128)(2,1)S(1)}, u32[]{:S(2)}, u32[]{:S(2)}) async-start(bf16[8,144,256]{2,1,0:T(8,128)(2,1)} %shard_map.74), calls=%async_computation.1 | async-start | bytes 1179648 | tf_op jit(solution)/shard_map/all_to_all | solution.py:360
  111.8 0.8 copy.12.new_ref
  112.5 18.6 %all-to-all-done.1.in_ref = bf16[8,144,256]{2,1,0:T(8,128)(2,1)S(1)} async-done(((bf16[8,144,256]{2,1,0:T(8,128)(2,1)}), bf16[8,144,256]{2,1,0:T(8,128)(2,1)S(1)}, u32[]{:S(2)}, u32[]{:S(2)}) %all-to-all-start.1) | async-done | bytes 589856 | tf_op jit(solution)/shard_map/all_to_all | solution.py:360
  131.1 0.8 copy-done.2
  131.9 2.1 %combine.1.own_ref = bf16[64,512]{1,0:T(8,128)(2,1)} custom-call(bf16[8,144,256]{2,1,0:T(8,128)(2,1)} %copy-done.2, bf16[8,144,256]{2,1,0:T(8,128)(2,1)} %prepare.1.q_ref, bf16[2,128,256]{2,1,0:T(8,128)(2,1)} %copy.12.new_ref), custom_call_target="tpu_custom_call" | custom-call | tf_op jit(solution)/shard_map/combine/pallas_call | solution.py:285
  134.4 1.1 collective-permute-done.15.partner_ref
  135.6 0.6 copy-done.16
  136.2 6.3 %project.1 = bf16[8,64,512]{2,1,0:T(8,128)(2,1)} custom-call(s32[2]{0:T(128)} %pad_add_fusion.place_ref, bf16[64,512]{1,0:T(8,128)(2,1)} %combine.1.own_ref, bf16[64,512]{1,0:T(8,128)(2,1)} %copy-done.16, bf16[512,8192]{1,0:T(8,128)(2,1)} %w_own_ref.1, bf16[512,8192]{1,0:T(8,128)(2,1)} %collective-permute-done.16.w_partner_ref), custom_call_target="tpu_custom_call" | custom-call | tf_op jit(solution)/shard_map/project/pallas_call | solution.py:325
  142.5 21.4 %all_to_all.15 = bf16[8,64,512]{2,1,0:T(8,128)(2,1)S(1)} all-to-all(bf16[8,64,512]{2,1,0:T(8,128)(2,1)} %project.1), channel_id=1, replica_groups={{0,2,4,6,8,10,12,14},{1,3,5,7,9,11,13,15},{16,18,20,22,24,26,28,30},{17..., dimensions={0} | all-to-all | bytes 1048576 | tf_op jit(solution)/shard_map/all_to_all | solution.py:396
  163.9 0.7 reduce_sum.12
  (57 shorter events, 3.3 us)
Async XLA Ops:
  0.0 111.7 %copy-start = (bf16[64,2,1024]{2,1,0:T(2,128)(2,1)S(1)}, bf16[64,2,1024]{2,1,0:T(2,128)(2,1)}, u32[]{:S(2)}) copy-start(bf16[64,2,1024]{2,1,0:T(2,128)(2,1)} %param.8) | copy-start | bytes 786436
  0.0 135.6 %collective-permute-start.16 = (bf16[512,8192]{1,0:T(8,128)(2,1)}, bf16[512,8192]{1,0:T(8,128)(2,1)}, u32[]{:S(2)}, u32[]{:S(2)}) collective-permute-start(bf16[512,8192]{1,0:T(8,128)(2,1)} %w_own_ref.1), channel_id=1, source_target_pairs={{0,1},{1,0},{2,3},{3,2},{4,5},{5,4},{6,7},{7,6},{8,9},{9,8},{10,11... | collective-permute-start | bytes 25165832 | tf_op jit(solution)/shard_map/ppermute | solution.py:363
  4.1 70.7 %copy-start.3 = (bf16[1040,128]{1,0:T(8,128)(2,1)}, bf16[1040,128]{1,0:T(8,128)(2,1)S(1)}, u32[]{:S(2)}) copy-start(bf16[1040,128]{1,0:T(8,128)(2,1)S(1)} %get-tuple-element.21.refs_0_) | copy-start | bytes 798724
  4.1 26.3 %collective-permute-start.13 = (bf16[1040,128]{1,0:T(8,128)(2,1)}, bf16[1040,128]{1,0:T(8,128)(2,1)}, u32[]{:S(2)}, u32[]{:S(2)}) collective-permute-start(bf16[1040,128]{1,0:T(8,128)(2,1)} %get-tuple-element.17), channel_id=1, source_target_pairs={{0,12},{1,13},{2,14},{3,15},{4,0},{5,1},{6,2},{7,3},{8,4},{9,5},{1... | collective-permute-start | bytes 798728 | tf_op jit(solution)/shard_map/ppermute | solution.py:357
  15.3 19.0 %collective-permute-start = (bf16[1040,128]{1,0:T(8,128)(2,1)S(1)}, bf16[1040,128]{1,0:T(8,128)(2,1)S(1)}, u32[]{:S(2)}, u32[]{:S(2)}) collective-permute-start(bf16[1040,128]{1,0:T(8,128)(2,1)S(1)} %get-tuple-element.18), channel_id=1, source_target_pairs={{0,6},{1,7},{2,8},{3,9},{4,10},{5,11},{6,12},{7,13},{8,14},{9,15},... | collective-permute-start | bytes 798728 | tf_op jit(solution)/shard_map/ppermute | solution.py:357
  15.3 40.0 %collective-permute-start.2 = (bf16[1040,128]{1,0:T(8,128)(2,1)S(1)}, bf16[1040,128]{1,0:T(8,128)(2,1)S(1)}, u32[]{:S(2)}, u32[]{:S(2)}) collective-permute-start(bf16[1040,128]{1,0:T(8,128)(2,1)S(1)} %get-tuple-element.19), channel_id=1, source_target_pairs={{0,10},{1,11},{2,12},{3,13},{4,14},{5,15},{6,0},{7,1},{8,2},{9,3},... | collective-permute-start | bytes 798728 | tf_op jit(solution)/shard_map/ppermute | solution.py:357
  22.1 52.7 %all-to-all-start = ((bf16[8,144,256]{2,1,0:T(8,128)(2,1)}), bf16[8,144,256]{2,1,0:T(8,128)(2,1)S(1)}, u32[]{:S(2)}, u32[]{:S(2)}) async-start(bf16[8,144,256]{2,1,0:T(8,128)(2,1)} %prepare.1.q_ref), calls=%async_computation | async-start | bytes 1179648 | tf_op jit(solution)/shard_map/all_to_all | solution.py:360
  29.1 26.2 %collective-permute-start.4 = (bf16[1040,128]{1,0:T(8,128)(2,1)S(1)}, bf16[1040,128]{1,0:T(8,128)(2,1)S(1)}, u32[]{:S(2)}, u32[]{:S(2)}) collective-permute-start(bf16[1040,128]{1,0:T(8,128)(2,1)S(1)} %get-tuple-element.20), channel_id=1, source_target_pairs={{0,8},{1,9},{2,10},{3,11},{4,12},{5,13},{6,14},{7,15},{8,0},{9,1},... | collective-permute-start | bytes 798728 | tf_op jit(solution)/shard_map/ppermute | solution.py:357
  30.4 26.7 %collective-permute-start.7 = (bf16[1040,128]{1,0:T(8,128)(2,1)S(1)}, bf16[1040,128]{1,0:T(8,128)(2,1)S(1)}, u32[]{:S(2)}, u32[]{:S(2)}) collective-permute-start(bf16[1040,128]{1,0:T(8,128)(2,1)S(1)} %get-tuple-element.22), channel_id=1, source_target_pairs={{0,2},{1,3},{2,4},{3,5},{4,6},{5,7},{6,8},{7,9},{8,10},{9,11},{10,... | collective-permute-start | bytes 798728 | tf_op jit(solution)/shard_map/ppermute | solution.py:357
  34.2 56.3 %copy-start.4 = (bf16[1040,128]{1,0:T(8,128)(2,1)}, bf16[1040,128]{1,0:T(8,128)(2,1)S(1)}, u32[]{:S(2)}) copy-start(bf16[1040,128]{1,0:T(8,128)(2,1)S(1)} %collective-permute-done.refs_0_) | copy-start | bytes 798724
  34.2 26.9 %collective-permute-start.9 = (bf16[1040,128]{1,0:T(8,128)(2,1)S(1)}, bf16[1040,128]{1,0:T(8,128)(2,1)S(1)}, u32[]{:S(2)}, u32[]{:S(2)}) collective-permute-start(bf16[1040,128]{1,0:T(8,128)(2,1)S(1)} %get-tuple-element.23), channel_id=1, source_target_pairs={{0,14},{1,15},{2,0},{3,1},{4,2},{5,3},{6,4},{7,5},{8,6},{9,7},{10,... | collective-permute-start | bytes 798728 | tf_op jit(solution)/shard_map/ppermute | solution.py:357
  55.3 35.2 %copy-start.5 = (bf16[1040,128]{1,0:T(8,128)(2,1)}, bf16[1040,128]{1,0:T(8,128)(2,1)S(1)}, u32[]{:S(2)}) copy-start(bf16[1040,128]{1,0:T(8,128)(2,1)S(1)} %collective-permute-done.2.refs_2_) | copy-start | bytes 798724
  55.3 14.4 %collective-permute-start.11 = (bf16[1040,128]{1,0:T(8,128)(2,1)S(1)}, bf16[1040,128]{1,0:T(8,128)(2,1)S(1)}, u32[]{:S(2)}, u32[]{:S(2)}) collective-permute-start(bf16[1040,128]{1,0:T(8,128)(2,1)S(1)} %get-tuple-element.24), channel_id=1, source_target_pairs={{0,4},{1,5},{2,6},{3,7},{4,8},{5,9},{6,10},{7,11},{8,12},{9,13},{1... | collective-permute-start | bytes 798728 | tf_op jit(solution)/shard_map/ppermute | solution.py:357
  55.3 35.2 %copy-start.6 = (bf16[1040,128]{1,0:T(8,128)(2,1)}, bf16[1040,128]{1,0:T(8,128)(2,1)S(1)}, u32[]{:S(2)}) copy-start(bf16[1040,128]{1,0:T(8,128)(2,1)S(1)} %collective-permute-done.4.refs_4_) | copy-start | bytes 798724
  55.3 16.7 %collective-permute-start.6 = (bf16[1040,128]{1,0:T(8,128)(2,1)S(1)}, bf16[1040,128]{1,0:T(8,128)(2,1)S(1)}, u32[]{:S(2)}, u32[]{:S(2)}) collective-permute-start(bf16[1040,128]{1,0:T(8,128)(2,1)S(1)} %get-tuple-element.21.refs_0_), channel_id=1, source_target_pairs={{0,1},{1,0},{2,3},{3,2},{4,5},{5,4},{6,7},{7,6},{8,9},{9,8},{10,11... | collective-permute-start | bytes 798728 | tf_op jit(solution)/shard_map/ppermute | solution.py:363
  57.1 15.5 %copy-start.10 = (bf16[1040,128]{1,0:T(8,128)(2,1)}, bf16[1040,128]{1,0:T(8,128)(2,1)S(1)}, u32[]{:S(2)}) copy-start(bf16[1040,128]{1,0:T(8,128)(2,1)S(1)} %collective-permute-done.7.refs_2_) | copy-start | bytes 798724
  57.1 15.0 %collective-permute-start.14 = (bf16[1040,128]{1,0:T(8,128)(2,1)}, bf16[1040,128]{1,0:T(8,128)(2,1)S(1)}, u32[]{:S(2)}, u32[]{:S(2)}) collective-permute-start(bf16[1040,128]{1,0:T(8,128)(2,1)} %collective-permute-done.13.refs_8_), channel_id=1, source_target_pairs={{0,1},{1,0},{2,3},{3,2},{4,5},{5,4},{6,7},{7,6},{8,9},{9,8},{10,11... | collective-permute-start | bytes 798728 | tf_op jit(solution)/shard_map/ppermute | solution.py:363
  61.1 13.7 %copy-start.11 = (bf16[1040,128]{1,0:T(8,128)(2,1)}, bf16[1040,128]{1,0:T(8,128)(2,1)S(1)}, u32[]{:S(2)}) copy-start(bf16[1040,128]{1,0:T(8,128)(2,1)S(1)} %collective-permute-done.9.refs_4_) | copy-start | bytes 798724
  61.1 11.3 %collective-permute-start.8 = (bf16[1040,128]{1,0:T(8,128)(2,1)S(1)}, bf16[1040,128]{1,0:T(8,128)(2,1)}, u32[]{:S(2)}, u32[]{:S(2)}) collective-permute-start(bf16[1040,128]{1,0:T(8,128)(2,1)S(1)} %collective-permute-done.7.refs_2_), channel_id=1, source_target_pairs={{0,1},{1,0},{2,3},{3,2},{4,5},{5,4},{6,7},{7,6},{8,9},{9,8},{10,11... | collective-permute-start | bytes 798728 | tf_op jit(solution)/shard_map/ppermute | solution.py:363
  69.7 5.1 %copy-start.12 = (bf16[1040,128]{1,0:T(8,128)(2,1)}, bf16[1040,128]{1,0:T(8,128)(2,1)S(1)}, u32[]{:S(2)}) copy-start(bf16[1040,128]{1,0:T(8,128)(2,1)S(1)} %collective-permute-done.11.refs_6_) | copy-start | bytes 798724
  69.7 3.4 %collective-permute-start.10 = (bf16[1040,128]{1,0:T(8,128)(2,1)S(1)}, bf16[1040,128]{1,0:T(8,128)(2,1)S(1)}, u32[]{:S(2)}, u32[]{:S(2)}) collective-permute-start(bf16[1040,128]{1,0:T(8,128)(2,1)S(1)} %collective-permute-done.9.refs_4_), channel_id=1, source_target_pairs={{0,1},{1,0},{2,3},{3,2},{4,5},{5,4},{6,7},{7,6},{8,9},{9,8},{10,11... | collective-permute-start | bytes 798728 | tf_op jit(solution)/shard_map/ppermute | solution.py:363
  72.0 2.9 %copy-start.13 = (bf16[1040,128]{1,0:T(8,128)(2,1)}, bf16[1040,128]{1,0:T(8,128)(2,1)S(1)}, u32[]{:S(2)}) copy-start(bf16[1040,128]{1,0:T(8,128)(2,1)S(1)} %collective-permute-done.6.refs_1_) | copy-start | bytes 798724
  72.0 2.8 %collective-permute-start.12 = (bf16[1040,128]{1,0:T(8,128)(2,1)S(1)}, bf16[1040,128]{1,0:T(8,128)(2,1)}, u32[]{:S(2)}, u32[]{:S(2)}) collective-permute-start(bf16[1040,128]{1,0:T(8,128)(2,1)S(1)} %collective-permute-done.11.refs_6_), channel_id=1, source_target_pairs={{0,1},{1,0},{2,3},{3,2},{4,5},{5,4},{6,7},{7,6},{8,9},{9,8},{10,11... | collective-permute-start | bytes 798728 | tf_op jit(solution)/shard_map/ppermute | solution.py:363
  72.1 18.3 %collective-permute-start.1 = (bf16[1040,128]{1,0:T(8,128)(2,1)S(1)}, bf16[1040,128]{1,0:T(8,128)(2,1)S(1)}, u32[]{:S(2)}, u32[]{:S(2)}) collective-permute-start(bf16[1040,128]{1,0:T(8,128)(2,1)S(1)} %collective-permute-done.refs_0_), channel_id=1, source_target_pairs={{0,1},{1,0},{2,3},{3,2},{4,5},{5,4},{6,7},{7,6},{8,9},{9,8},{10,11... | collective-permute-start | bytes 798728 | tf_op jit(solution)/shard_map/ppermute | solution.py:363
  72.5 18.0 %collective-permute-start.3 = (bf16[1040,128]{1,0:T(8,128)(2,1)S(1)}, bf16[1040,128]{1,0:T(8,128)(2,1)S(1)}, u32[]{:S(2)}, u32[]{:S(2)}) collective-permute-start(bf16[1040,128]{1,0:T(8,128)(2,1)S(1)} %collective-permute-done.2.refs_2_), channel_id=1, source_target_pairs={{0,1},{1,0},{2,3},{3,2},{4,5},{5,4},{6,7},{7,6},{8,9},{9,8},{10,11... | collective-permute-start | bytes 798728 | tf_op jit(solution)/shard_map/ppermute | solution.py:363
  73.8 16.7 %collective-permute-start.5 = (bf16[1040,128]{1,0:T(8,128)(2,1)S(1)}, bf16[1040,128]{1,0:T(8,128)(2,1)S(1)}, u32[]{:S(2)}, u32[]{:S(2)}) collective-permute-start(bf16[1040,128]{1,0:T(8,128)(2,1)S(1)} %collective-permute-done.4.refs_4_), channel_id=1, source_target_pairs={{0,1},{1,0},{2,3},{3,2},{4,5},{5,4},{6,7},{7,6},{8,9},{9,8},{10,11... | collective-permute-start | bytes 798728 | tf_op jit(solution)/shard_map/ppermute | solution.py:363
  74.8 0.8 copy-start.1
  90.5 0.8 copy-start.8
  90.5 0.9 copy-start.9
  101.8 29.3 %all-to-all-start.1 = ((bf16[8,144,256]{2,1,0:T(8,128)(2,1)}), bf16[8,144,256]{2,1,0:T(8,128)(2,1)S(1)}, u32[]{:S(2)}, u32[]{:S(2)}) async-start(bf16[8,144,256]{2,1,0:T(8,128)(2,1)} %shard_map.74), calls=%async_computation.1 | async-start | bytes 1179648 | tf_op jit(solution)/shard_map/all_to_all | solution.py:360
  131.1 0.8 copy-start.2
  134.0 1.6 collective-permute-start.15
  (4 other events, 2.7 us)

commit v4 on v2

--- a/solution.py
+++ b/solution.py
@@ -15,6 +15,7 @@
 CHUNKS = ((0, 1, 7, 2, 6), (3, 5, 4))
 STAT_ROWS = 16
 INTERPRET = False
+GRANT = 24 * 1024 * 1024
 
 
 def split3(x):
@@ -58,7 +59,7 @@
     )(queries, block_table.T, prefix_len.reshape(1, -1))
 
 
-def attend_chunk(place, bufs, queries_t, state, shifts, y_count, group_count, per_batch, first, last):
+def attend_chunk(place, bufs, queries_t, state, shifts, y_count, group_count, per_batch, first, last, early):
     n_buf = len(bufs)
     buf_rows = bufs[0].shape[0]
     rows, cols = queries_t[0].shape
@@ -67,6 +68,7 @@
     int_rows = group_count + 8 * ((n_buf + 7) // 8)
 
     def kernel(place_ref, *refs):
+        refs = refs[len(early) :]
         buf_refs = refs[:n_buf]
         q_refs = refs[n_buf : n_buf + group_count]
         rest = list(refs[n_buf + group_count :])
@@ -229,7 +231,7 @@
         pltpu.SemaphoreType.DMA((group_count,)),
     ]
     anywhere = pl.BlockSpec(memory_space=pltpu.MemorySpace.HBM)
-    n_in = n_buf + group_count + (0 if first else 2)
+    n_in = len(early) + n_buf + group_count + (0 if first else 2)
     return pl.pallas_call(
         kernel,
         out_shape=out_shape,
@@ -241,7 +243,7 @@
             scratch_shapes=scratch,
         ),
         interpret=INTERPRET,
-    )(place, *bufs, *queries_t, *(() if first else state))
+    )(place, *early, *bufs, *queries_t, *(() if first else state))
 
 
 def combine(arrived, query_t, newest_t, heads_dev):
@@ -277,15 +279,16 @@
         kernel,
         out_shape=jax.ShapeDtypeStruct((req_rows, heads_dev * HEAD_SIZE), jnp.bfloat16),
         interpret=INTERPRET,
+        compiler_params=pltpu.CompilerParams(vmem_limit_bytes=GRANT),
         name="combine",
     )(arrived, query_t, newest_t)
 
 
-def project(place, mix_own, mix_partner, weight_own, weight_partner, y_count):
+def held_weights(place, weight_own, weight_partner, y_count):
     width = weight_own.shape[1] // (2 * y_count)
-    req_rows, depth = mix_own.shape
-
-    def kernel(place_ref, own_ref, partner_ref, w_own_ref, w_partner_ref, out_ref, w_all, sem):
+    depth = weight_own.shape[0]
+
+    def kernel(place_ref, w_own_ref, w_partner_ref, out_ref, sem):
         core = lax.rem(place_ref[0], 2)
         copies = []
         for n in range(y_count):
@@ -293,35 +296,50 @@
             for k, ref in enumerate((w_own_ref, w_partner_ref)):
                 copies.append(
                     pltpu.make_async_copy(
-                        ref.at[:, pl.ds(start, width)], w_all.at[n, pl.ds(k * depth, depth)], sem.at[2 * n + k]
+                        ref.at[:, pl.ds(start, width)], out_ref.at[n, pl.ds(k * depth, depth)], sem.at[2 * n + k]
                     )
                 )
         for one in copies:
             one.start()
-        mix = jnp.concatenate([own_ref[...], partner_ref[...]], axis=1)
-        for n in range(y_count):
-            copies[2 * n].wait()
-            copies[2 * n + 1].wait()
-            out_ref[n] = jnp.dot(mix, w_all[n], preferred_element_type=jnp.float32).astype(jnp.bfloat16)
-
-    vmem = pl.BlockSpec(memory_space=pltpu.MemorySpace.VMEM)
+        for one in copies:
+            one.wait()
+
     anywhere = pl.BlockSpec(memory_space=pltpu.MemorySpace.HBM)
     return pl.pallas_call(
         kernel,
-        out_shape=jax.ShapeDtypeStruct((y_count, req_rows, width), jnp.bfloat16),
+        out_shape=pltpu.VMEM((y_count, 2 * depth, width), jnp.bfloat16),
         grid_spec=pltpu.PrefetchScalarGridSpec(
             num_scalar_prefetch=1,
             grid=(),
-            in_specs=[vmem, vmem, anywhere, anywhere],
-            out_specs=vmem,
-            scratch_shapes=[
-                pltpu.VMEM((y_count, 2 * depth, width), jnp.bfloat16),
-                pltpu.SemaphoreType.DMA((2 * y_count,)),
-            ],
+            in_specs=[anywhere, anywhere],
+            out_specs=pl.BlockSpec(memory_space=pltpu.MemorySpace.VMEM),
+            scratch_shapes=[pltpu.SemaphoreType.DMA((2 * y_count,))],
         ),
         interpret=INTERPRET,
+        compiler_params=pltpu.CompilerParams(vmem_limit_bytes=GRANT),
+        name="held_weights",
+    )(place, weight_own, weight_partner)
+
+
+def project(mix_own, mix_partner, weights):
+    y_count, _, width = weights.shape
+    req_rows, _ = mix_own.shape
+
+    def kernel(own_ref, partner_ref, w_ref, out_ref):
+        mix = jnp.concatenate([own_ref[...], partner_ref[...]], axis=1)
+        for n in range(y_count):
+            out_ref[n] = jnp.dot(mix, w_ref[n], preferred_element_type=jnp.float32).astype(jnp.bfloat16)
+
+    vmem = pl.BlockSpec(memory_space=pltpu.MemorySpace.VMEM)
+    return pl.pallas_call(
+        kernel,
+        out_shape=jax.ShapeDtypeStruct((y_count, req_rows, width), jnp.bfloat16),
+        in_specs=[vmem, vmem, vmem],
+        out_specs=vmem,
+        interpret=INTERPRET,
+        compiler_params=pltpu.CompilerParams(vmem_limit_bytes=GRANT),
         name="project",
-    )(place, mix_own, mix_partner, weight_own, weight_partner)
+    )(mix_own, mix_partner, weights)
 
 
 def per_device_inner(
@@ -369,13 +387,14 @@
         bufs = [b for s in shifts for b in (own[s], partner[s])]
         last = n == len(CHUNKS) - 1
         state = attend_chunk(
-            place, bufs, queries_t, state, shifts, y_count, group_count, 4, n == 0, last
+            place, bufs, queries_t, state, shifts, y_count, group_count, 4, n == 0, last, (newest_t,) if last else ()
         )
     arrived = lax.all_to_all(state[0], "grp", split_axis=0, concat_axis=0, tiled=True)
+    weights = held_weights(place, out_weight, weight_partner, y_count)
 
     mix_own = combine(arrived, query_t, newest_t, heads_dev)
     mix_partner = to_other_core(mix_own)
-    partial = project(place, mix_own, mix_partner, out_weight, weight_partner, y_count)
+    partial = project(mix_own, mix_partner, weights)
     same_core = [[2 * i + c for i in range(y_count)] for c in range(2)]
     arrived = lax.all_to_all(partial, "tp", split_axis=0, concat_axis=0, axis_index_groups=same_core, tiled=True)
     return jnp.sum(arrived.astype(jnp.float32), axis=0).astype(jnp.bfloat16)

time: 180 us -> 177 us (0.983)
  blocking collectives: 21.4 us -> 46.8 us
  waiting for transfers between devices: 44.9 us -> 24.6 us
  starting transfers between devices: 68.6 us -> 62.3 us
  Pallas kernels: 35.8 us -> 32.5 us
  local copies, waits for them, and re-layouts: 6.16 us -> 8.14 us
    all_to_all x0 -> x1, blocking collectives: none -> 26.4 us  [per_device_inner(): lax.all_to_all(state[0], 'grp', split_axis=0, concat_axis=0, tiled=True)]
    all_to_all x1 -> x0, waiting for transfers between devices: 18.6 us -> none  [per_device_inner(): lax.all_to_all(state[0], 'grp', split_axis=0, concat_axis=0, tiled=True)]
    all_to_all x1 -> x0, starting transfers between devices: 6.8 us -> none  [per_device_inner(): lax.all_to_all(state[0], 'grp', split_axis=0, concat_axis=0, tiled=True)]
    pallas_call x1, Pallas kernels: 6.25 us -> 1.55 us  [project(): pl.pallas_call(kernel, out_shape=jax.ShapeDtypeStruct((y_count, req_rows,...]
    pallas_call x0 -> x1, Pallas kernels: none -> 3.07 us  [held_weights(): pl.pallas_call(kernel, out_shape=pltpu.VMEM((y_count, 2 * depth, width),...]
    unnamed x48 -> x52, local copies, waits for them, and re-layouts: 3.44 us -> 5.4 us
  transfers between devices with their start and end apart: 25 -> 24, of which waited for: 8 -> 6; matrix products, arithmetic and copies ran while one was open for 2% -> 2% of each run, Pallas kernels for 16% -> 17%
where the time goes in v4:
time: 177 us
  starting transfers between devices  62.3 us (35%)
  blocking collectives  46.8 us (26%)
  Pallas kernels  32.5 us (18%)
  waiting for transfers between devices  24.6 us (14%)
  local copies, waits for them, and re-layouts  8.14 us (5%)
  other arithmetic  2.19 us (1%)
    ppermute x10, starting transfers between devices, to_other_core(): return lax.ppermute(x, 'tp', swap)  42.7 us
    all_to_all x1, blocking collectives, per_device_inner(): lax.all_to_all(state[0], 'grp', split_axis=0, concat_axis=0, tiled=True)  26.4 us
    pallas_call x2, Pallas kernels, attend_chunk(): pl.pallas_call(kernel, out_shape=out_shape, grid_spec=pltpu.PrefetchScala...  25.4 us
    all_to_all x1, blocking collectives, per_device_inner(): lax.all_to_all(partial, 'tp', split_axis=0, concat_axis=0, axis_index_gro...  20.4 us
    ppermute x7, waiting for transfers between devices, along_x(): lax.ppermute(x, 'grp', [(i, (i + shift) % group_count) for i in range(gro...  15.4 us
    ppermute x7, starting transfers between devices, along_y(): lax.ppermute(x, 'tp', [(i, (i + 2 * shift) % tp_count) for i in range(tp_...  10.4 us
    ppermute x7, starting transfers between devices, along_x(): lax.ppermute(x, 'grp', [(i, (i + shift) % group_count) for i in range(gro...  9.25 us
    ppermute x7, waiting for transfers between devices, along_y(): lax.ppermute(x, 'tp', [(i, (i + 2 * shift) % tp_count) for i in range(tp_...  9.13 us
  transfers between devices with their start and end apart: 24, of which 6 were waited for; matrix products, arithmetic and copies ran while one was open for 2% of the time, Pallas kernels for 17%

profile of v4, /device:TPU:513, one launch (start us, length us, event | category | flops | bytes accessed | tf_op | source)
XLA Modules:
  0.0 176.8 jit_solution(12992361817920112656)
XLA Ops:
  0.0 20.4 %collective-permute-start.23 = (bf16[512,8192]{1,0:T(8,128)(2,1)}, bf16[512,8192]{1,0:T(8,128)(2,1)}, u32[]{:S(2)}, u32[]{:S(2)}) collective-permute-start(bf16[512,8192]{1,0:T(8,128)(2,1)} %w_own_ref.1), channel_id=1, source_target_pairs={{0,1},{1,0},{2,3},{3,2},{4,5},{5,4},{6,7},{7,6},{8,9},{9,8},{10,11... | collective-permute-start | bytes 25165832 | tf_op jit(solution)/shard_map/ppermute | solution.py:365
  20.4 2.2 %prepare.1.refs_10_.refs_7_.q_ref = bf16[144,256]{1,0:T(8,128)(2,1)} custom-call(bf16[64,512]{1,0:T(8,128)(2,1)} %q_ref.1, s32[8,64]{1,0:T(8,128)} %bitcast.26, s32[1,64]{1,0:T(1,128)} %bitcast.27), custom_call_target="tpu_custom_call" | custom-call | tf_op jit(solution)/shard_map/prepare/pallas_call | solution.py:54
  22.8 5.5 %collective-permute-start.9 = (bf16[144,256]{1,0:T(8,128)(2,1)}, bf16[144,256]{1,0:T(8,128)(2,1)S(1)}, u32[]{:S(2)}, u32[]{:S(2)}) collective-permute-start(bf16[144,256]{1,0:T(8,128)(2,1)} %prepare.1.refs_10_.refs_7_.q_ref), channel_id=1, source_target_pairs={{0,64},{16,80},{32,96},{48,112},{64,0},{80,16},{96,32},{112,48},{1... | collective-permute-start | bytes 221192 | tf_op jit(solution)/shard_map/ppermute | solution.py:362
  28.2 0.7 convert_element_type.18
  29.1 1.7 constant_dynamic-slice_fusion
  31.3 0.7 collective-permute-done.10.refs_15_.refs_12_
  32.0 3.8 %collective-permute-start.2 = (bf16[1040,128]{1,0:T(8,128)(2,1)S(1)}, bf16[1040,128]{1,0:T(8,128)(2,1)S(1)}, u32[]{:S(2)}, u32[]{:S(2)}) collective-permute-start(bf16[1040,128]{1,0:T(8,128)(2,1)S(1)} %get-tuple-element.19), channel_id=1, source_target_pairs={{0,10},{1,11},{2,12},{3,13},{4,14},{5,15},{6,0},{7,1},{8,2},{9,3},... | collective-permute-start | bytes 798728 | tf_op jit(solution)/shard_map/ppermute | solution.py:359
  35.9 8.1 %collective-permute-done.8.refs_13_.refs_10_ = bf16[144,256]{1,0:T(8,128)(2,1)S(1)} collective-permute-done((bf16[144,256]{1,0:T(8,128)(2,1)S(1)}, bf16[144,256]{1,0:T(8,128)(2,1)S(1)}, u32[]{:S(2)}, u32[]{:S(2)}) %collective-permute-start.8) | collective-permute-done | bytes 73760 | tf_op jit(solution)/shard_map/ppermute | solution.py:362
  44.0 3.3 %collective-permute-start.7 = (bf16[144,256]{1,0:T(8,128)(2,1)S(1)}, bf16[144,256]{1,0:T(8,128)(2,1)S(1)}, u32[]{:S(2)}, u32[]{:S(2)}) collective-permute-start(bf16[144,256]{1,0:T(8,128)(2,1)S(1)} %copy-done.3), channel_id=1, source_target_pairs={{0,32},{16,48},{32,64},{48,80},{64,96},{80,112},{96,0},{112,16},{1... | collective-permute-start | bytes 221192 | tf_op jit(solution)/shard_map/ppermute | solution.py:362
  47.3 2.3 %collective-permute-done.7.refs_12_.refs_9_ = bf16[144,256]{1,0:T(8,128)(2,1)S(1)} collective-permute-done((bf16[144,256]{1,0:T(8,128)(2,1)S(1)}, bf16[144,256]{1,0:T(8,128)(2,1)S(1)}, u32[]{:S(2)}, u32[]{:S(2)}) %collective-permute-start.7) | collective-permute-done | bytes 73760 | tf_op jit(solution)/shard_map/ppermute | solution.py:362
  49.8 4.3 %collective-permute-done.6.refs_11_.refs_8_ = bf16[144,256]{1,0:T(8,128)(2,1)S(1)} collective-permute-done((bf16[144,256]{1,0:T(8,128)(2,1)S(1)}, bf16[144,256]{1,0:T(8,128)(2,1)S(1)}, u32[]{:S(2)}, u32[]{:S(2)}) %collective-permute-start.6) | collective-permute-done | bytes 73760 | tf_op jit(solution)/shard_map/ppermute | solution.py:362
  54.2 2.5 %collective-permute-start.14 = (bf16[1040,128]{1,0:T(8,128)(2,1)S(1)}, bf16[1040,128]{1,0:T(8,128)(2,1)S(1)}, u32[]{:S(2)}, u32[]{:S(2)}) collective-permute-start(bf16[1040,128]{1,0:T(8,128)(2,1)S(1)} %get-tuple-element.22), channel_id=1, source_target_pairs={{0,2},{1,3},{2,4},{3,5},{4,6},{5,7},{6,8},{7,9},{8,10},{9,11},{10,... | collective-permute-start | bytes 798728 | tf_op jit(solution)/shard_map/ppermute | solution.py:359
  56.7 1.3 collective-permute-start.16
  58.0 2.6 %collective-permute-start.18 = (bf16[1040,128]{1,0:T(8,128)(2,1)S(1)}, bf16[1040,128]{1,0:T(8,128)(2,1)}, u32[]{:S(2)}, u32[]{:S(2)}) collective-permute-start(bf16[1040,128]{1,0:T(8,128)(2,1)S(1)} %get-tuple-element.24), channel_id=1, source_target_pairs={{0,4},{1,5},{2,6},{3,7},{4,8},{5,9},{6,10},{7,11},{8,12},{9,13},{1... | collective-permute-start | bytes 798728 | tf_op jit(solution)/shard_map/ppermute | solution.py:359
  60.5 5.7 %collective-permute-done.4.refs_5_ = bf16[1040,128]{1,0:T(8,128)(2,1)S(1)} collective-permute-done((bf16[1040,128]{1,0:T(8,128)(2,1)S(1)}, bf16[1040,128]{1,0:T(8,128)(2,1)S(1)}, u32[]{:S(2)}, u32[]{:S(2)}) %collective-permute-start.4) | collective-permute-done | bytes 266272 | tf_op jit(solution)/shard_map/ppermute | solution.py:359
  66.2 9.2 %collective-permute-start.13 = (bf16[1040,128]{1,0:T(8,128)(2,1)S(1)}, bf16[1040,128]{1,0:T(8,128)(2,1)}, u32[]{:S(2)}, u32[]{:S(2)}) collective-permute-start(bf16[1040,128]{1,0:T(8,128)(2,1)S(1)} %get-tuple-element.21.refs_0_), channel_id=1, source_target_pairs={{0,1},{1,0},{2,3},{3,2},{4,5},{5,4},{6,7},{7,6},{8,9},{9,8},{10,11... | collective-permute-start | bytes 798728 | tf_op jit(solution)/shard_map/ppermute | solution.py:365
  75.4 4.9 %collective-permute-start.21 = (bf16[1040,128]{1,0:T(8,128)(2,1)S(1)}, bf16[1040,128]{1,0:T(8,128)(2,1)S(1)}, u32[]{:S(2)}, u32[]{:S(2)}) collective-permute-start(bf16[1040,128]{1,0:T(8,128)(2,1)S(1)} %collective-permute-done.20.refs_8_), channel_id=1, source_target_pairs={{0,1},{1,0},{2,3},{3,2},{4,5},{5,4},{6,7},{7,6},{8,9},{9,8},{10,11... | collective-permute-start | bytes 798728 | tf_op jit(solution)/shard_map/ppermute | solution.py:365
  80.5 3.4 %collective-permute-done.18.refs_6_ = bf16[1040,128]{1,0:T(8,128)(2,1)} collective-permute-done((bf16[1040,128]{1,0:T(8,128)(2,1)S(1)}, bf16[1040,128]{1,0:T(8,128)(2,1)}, u32[]{:S(2)}, u32[]{:S(2)}) %collective-permute-start.18) | collective-permute-done | bytes 266272 | tf_op jit(solution)/shard_map/ppermute | solution.py:359
  83.9 5.9 %collective-permute-start.17 = (bf16[1040,128]{1,0:T(8,128)(2,1)S(1)}, bf16[1040,128]{1,0:T(8,128)(2,1)S(1)}, u32[]{:S(2)}, u32[]{:S(2)}) collective-permute-start(bf16[1040,128]{1,0:T(8,128)(2,1)S(1)} %collective-permute-done.16.refs_4_), channel_id=1, source_target_pairs={{0,1},{1,0},{2,3},{3,2},{4,5},{5,4},{6,7},{7,6},{8,9},{9,8},{10,11... | collective-permute-start | bytes 798728 | tf_op jit(solution)/shard_map/ppermute | solution.py:365
  91.3 0.7 copy-done.25
  92.5 0.8 copy.12.refs_0_.new_ref
  93.3 0.7 pad_add_fusion.place_ref
  94.1 13.1 %shard_map.73 = (f32[8,128,256]{2,1,0:T(8,128)}, f32[8,8,256]{2,1,0:T(8,128)}) custom-call(s32[2]{0:T(128)} %pad_add_fusion.place_ref, bf16[1040,128]{1,0:T(8,128)(2,1)} %copy-done.6, bf16[1040,128]{1,0:T(8,128)(2,1)} %collective-permute-done.13.refs_1_, bf16[1040,128]{1,0:T(8,128)(2,1)} %copy-done.21, bf16[1040,128]{1,0:T(8,128)(2,1)} %copy-done.24, ...), custom_call_target="tpu_custom_call" | custom-call | tf_op jit(solution)/shard_map/pallas_call | solution.py:235
  107.3 0.6 copy-done.17
  108.1 12.2 %shard_map.74 = bf16[8,144,256]{2,1,0:T(8,128)(2,1)} custom-call(s32[2]{0:T(128)} %pad_add_fusion.place_ref, bf16[2,128,256]{2,1,0:T(8,128)(2,1)} %copy.12.refs_0_.new_ref, bf16[1040,128]{1,0:T(8,128)(2,1)} %copy-done.14, bf16[1040,128]{1,0:T(8,128)(2,1)} %copy-done.17, bf16[1040,128]{1,0:T(8,128)(2,1)} %copy-done.15, bf16[1040,128]{1,0:T(8,128)(2,1)} %copy-done.18, ...), custom_call_target="tpu_custom_call" | custom-call | tf_op jit(solution)/shard_map/pallas_call | solution.py:235
  120.4 26.4 %all_to_all.10.in_ref = bf16[8,144,256]{2,1,0:T(8,128)(2,1)S(1)} all-to-all(bf16[8,144,256]{2,1,0:T(8,128)(2,1)} %shard_map.74), channel_id=1, replica_groups=mesh['rep'=2,'grp'=8,'tp'=16] {'grp'}, dimensions={0} | all-to-all | bytes 1179648 | tf_op jit(solution)/shard_map/all_to_all | solution.py:392
  147.1 0.6 collective-permute-start.22
  147.7 3.4 %copy-done.1 = bf16[512,8192]{1,0:T(8,128)(2,1)S(1)} copy-done((bf16[512,8192]{1,0:T(8,128)(2,1)S(1)}, bf16[512,8192]{1,0:T(8,128)(2,1)}, u32[]{:S(2)}) %copy-start.1) | copy-done | bytes 8388632
  151.1 3.1 %held_weights.1.w_ref = bf16[8,1024,512]{2,1,0:T(8,128)(2,1)S(1)} custom-call(s32[2]{0:T(128)S(1)} %copy-done.5, bf16[512,8192]{1,0:T(8,128)(2,1)S(1)} %copy-done.1, bf16[512,8192]{1,0:T(8,128)(2,1)} %collective-permute-done.23.w_partner_ref), custom_call_target="tpu_custom_call" | custom-call | tf_op jit(solution)/shard_map/held_weights/pallas_call | solution.py:308
  154.2 1.6 project.1
  155.7 20.4 %all_to_all.11 = bf16[8,64,512]{2,1,0:T(8,128)(2,1)S(1)} all-to-all(bf16[8,64,512]{2,1,0:T(8,128)(2,1)S(1)} %project.1), channel_id=1, replica_groups={{0,2,4,6,8,10,12,14},{1,3,5,7,9,11,13,15},{16,18,20,22,24,26,28,30},{17..., dimensions={0} | all-to-all | bytes 1048576 | tf_op jit(solution)/shard_map/all_to_all | solution.py:399
  176.1 0.7 reduce_sum.12
  (87 shorter events, 3.8 us)
Async XLA Ops:
  0.0 92.5 %copy-start = (bf16[64,2,1024]{2,1,0:T(2,128)(2,1)S(1)}, bf16[64,2,1024]{2,1,0:T(2,128)(2,1)}, u32[]{:S(2)}) copy-start(bf16[64,2,1024]{2,1,0:T(2,128)(2,1)} %param.8) | copy-start | bytes 786436
  0.0 147.7 %collective-permute-start.23 = (bf16[512,8192]{1,0:T(8,128)(2,1)}, bf16[512,8192]{1,0:T(8,128)(2,1)}, u32[]{:S(2)}, u32[]{:S(2)}) collective-permute-start(bf16[512,8192]{1,0:T(8,128)(2,1)} %w_own_ref.1), channel_id=1, source_target_pairs={{0,1},{1,0},{2,3},{3,2},{4,5},{5,4},{6,7},{7,6},{8,9},{9,8},{10,11... | collective-permute-start | bytes 25165832 | tf_op jit(solution)/shard_map/ppermute | solution.py:365
  22.6 8.4 %collective-permute-start.12 = (bf16[144,256]{1,0:T(8,128)(2,1)}, bf16[144,256]{1,0:T(8,128)(2,1)S(1)}, u32[]{:S(2)}, u32[]{:S(2)}) collective-permute-start(bf16[144,256]{1,0:T(8,128)(2,1)} %prepare.1.refs_10_.refs_7_.q_ref), channel_id=1, source_target_pairs={{0,112},{16,0},{32,16},{48,32},{64,48},{80,64},{96,80},{112,96},{1... | collective-permute-start | bytes 221192 | tf_op jit(solution)/shard_map/ppermute | solution.py:362
  22.6 8.6 %collective-permute-start.11 = (bf16[144,256]{1,0:T(8,128)(2,1)}, bf16[144,256]{1,0:T(8,128)(2,1)S(1)}, u32[]{:S(2)}, u32[]{:S(2)}) collective-permute-start(bf16[144,256]{1,0:T(8,128)(2,1)} %prepare.1.refs_10_.refs_7_.q_ref), channel_id=1, source_target_pairs={{0,96},{16,112},{32,0},{48,16},{64,32},{80,48},{96,64},{112,80},{1... | collective-permute-start | bytes 221192 | tf_op jit(solution)/shard_map/ppermute | solution.py:362
  22.6 9.4 %collective-permute-start.10 = (bf16[144,256]{1,0:T(8,128)(2,1)}, bf16[144,256]{1,0:T(8,128)(2,1)S(1)}, u32[]{:S(2)}, u32[]{:S(2)}) collective-permute-start(bf16[144,256]{1,0:T(8,128)(2,1)} %prepare.1.refs_10_.refs_7_.q_ref), channel_id=1, source_target_pairs={{0,80},{16,96},{32,112},{48,0},{64,16},{80,32},{96,48},{112,64},{1... | collective-permute-start | bytes 221192 | tf_op jit(solution)/shard_map/ppermute | solution.py:362
  22.8 13.1 %collective-permute-start.9 = (bf16[144,256]{1,0:T(8,128)(2,1)}, bf16[144,256]{1,0:T(8,128)(2,1)S(1)}, u32[]{:S(2)}, u32[]{:S(2)}) collective-permute-start(bf16[144,256]{1,0:T(8,128)(2,1)} %prepare.1.refs_10_.refs_7_.q_ref), channel_id=1, source_target_pairs={{0,64},{16,80},{32,96},{48,112},{64,0},{80,16},{96,32},{112,48},{1... | collective-permute-start | bytes 221192 | tf_op jit(solution)/shard_map/ppermute | solution.py:362
  29.1 117.7 %copy-start.4 = (bf16[144,256]{1,0:T(8,128)(2,1)S(1)}, bf16[144,256]{1,0:T(8,128)(2,1)}, u32[]{:S(2)}) copy-start(bf16[144,256]{1,0:T(8,128)(2,1)} %prepare.1.refs_10_.refs_7_.q_ref) | copy-start | bytes 221188
  31.0 63.0 %copy-start.6 = (bf16[1040,128]{1,0:T(8,128)(2,1)}, bf16[1040,128]{1,0:T(8,128)(2,1)S(1)}, u32[]{:S(2)}) copy-start(bf16[1040,128]{1,0:T(8,128)(2,1)S(1)} %get-tuple-element.21.refs_0_) | copy-start | bytes 798724
  31.0 62.9 %copy-start.7 = (bf16[144,256]{1,0:T(8,128)(2,1)}, bf16[144,256]{1,0:T(8,128)(2,1)S(1)}, u32[]{:S(2)}) copy-start(bf16[144,256]{1,0:T(8,128)(2,1)S(1)} %collective-permute-done.12.refs_17_.refs_14_) | copy-start | bytes 221188
  31.0 23.1 %collective-permute-start.20 = (bf16[1040,128]{1,0:T(8,128)(2,1)S(1)}, bf16[1040,128]{1,0:T(8,128)(2,1)S(1)}, u32[]{:S(2)}, u32[]{:S(2)}) collective-permute-start(bf16[1040,128]{1,0:T(8,128)(2,1)S(1)} %get-tuple-element.17), channel_id=1, source_target_pairs={{0,12},{1,13},{2,14},{3,15},{4,0},{5,1},{6,2},{7,3},{8,4},{9,5},{1... | collective-permute-start | bytes 798728 | tf_op jit(solution)/shard_map/ppermute | solution.py:359
  31.2 62.8 %copy-start.8 = (bf16[144,256]{1,0:T(8,128)(2,1)}, bf16[144,256]{1,0:T(8,128)(2,1)S(1)}, u32[]{:S(2)}) copy-start(bf16[144,256]{1,0:T(8,128)(2,1)S(1)} %collective-permute-done.11.refs_16_.refs_13_) | copy-start | bytes 221188
  31.2 25.5 %collective-permute-start = (bf16[1040,128]{1,0:T(8,128)(2,1)S(1)}, bf16[1040,128]{1,0:T(8,128)(2,1)S(1)}, u32[]{:S(2)}, u32[]{:S(2)}) collective-permute-start(bf16[1040,128]{1,0:T(8,128)(2,1)S(1)} %get-tuple-element.18), channel_id=1, source_target_pairs={{0,6},{1,7},{2,8},{3,9},{4,10},{5,11},{6,12},{7,13},{8,14},{9,15},... | collective-permute-start | bytes 798728 | tf_op jit(solution)/shard_map/ppermute | solution.py:359
  32.0 61.9 %copy-start.9 = (bf16[144,256]{1,0:T(8,128)(2,1)}, bf16[144,256]{1,0:T(8,128)(2,1)S(1)}, u32[]{:S(2)}) copy-start(bf16[144,256]{1,0:T(8,128)(2,1)S(1)} %collective-permute-done.10.refs_15_.refs_12_) | copy-start | bytes 221188
  32.0 25.9 %collective-permute-start.2 = (bf16[1040,128]{1,0:T(8,128)(2,1)S(1)}, bf16[1040,128]{1,0:T(8,128)(2,1)S(1)}, u32[]{:S(2)}, u32[]{:S(2)}) collective-permute-start(bf16[1040,128]{1,0:T(8,128)(2,1)S(1)} %get-tuple-element.19), channel_id=1, source_target_pairs={{0,10},{1,11},{2,12},{3,13},{4,14},{5,15},{6,0},{7,1},{8,2},{9,3},... | collective-permute-start | bytes 798728 | tf_op jit(solution)/shard_map/ppermute | solution.py:359
  35.8 58.2 %copy-start.10 = (bf16[144,256]{1,0:T(8,128)(2,1)}, bf16[144,256]{1,0:T(8,128)(2,1)S(1)}, u32[]{:S(2)}) copy-start(bf16[144,256]{1,0:T(8,128)(2,1)S(1)} %collective-permute-done.9.refs_14_.refs_11_) | copy-start | bytes 221188
  35.8 8.2 %collective-permute-start.8 = (bf16[144,256]{1,0:T(8,128)(2,1)S(1)}, bf16[144,256]{1,0:T(8,128)(2,1)S(1)}, u32[]{:S(2)}, u32[]{:S(2)}) collective-permute-start(bf16[144,256]{1,0:T(8,128)(2,1)S(1)} %copy-done.3), channel_id=1, source_target_pairs={{0,48},{16,64},{32,80},{48,96},{64,112},{80,0},{96,16},{112,32},{1... | collective-permute-start | bytes 221192 | tf_op jit(solution)/shard_map/ppermute | solution.py:362
  44.0 5.6 %collective-permute-start.7 = (bf16[144,256]{1,0:T(8,128)(2,1)S(1)}, bf16[144,256]{1,0:T(8,128)(2,1)S(1)}, u32[]{:S(2)}, u32[]{:S(2)}) collective-permute-start(bf16[144,256]{1,0:T(8,128)(2,1)S(1)} %copy-done.3), channel_id=1, source_target_pairs={{0,32},{16,48},{32,64},{48,80},{64,96},{80,112},{96,0},{112,16},{1... | collective-permute-start | bytes 221192 | tf_op jit(solution)/shard_map/ppermute | solution.py:362
  49.7 4.5 %collective-permute-start.6 = (bf16[144,256]{1,0:T(8,128)(2,1)S(1)}, bf16[144,256]{1,0:T(8,128)(2,1)S(1)}, u32[]{:S(2)}, u32[]{:S(2)}) collective-permute-start(bf16[144,256]{1,0:T(8,128)(2,1)S(1)} %copy-done.3), channel_id=1, source_target_pairs={{0,16},{16,32},{32,48},{48,64},{64,80},{80,96},{96,112},{112,0},{1... | collective-permute-start | bytes 221192 | tf_op jit(solution)/shard_map/ppermute | solution.py:362
  54.1 12.1 %collective-permute-start.4 = (bf16[1040,128]{1,0:T(8,128)(2,1)S(1)}, bf16[1040,128]{1,0:T(8,128)(2,1)S(1)}, u32[]{:S(2)}, u32[]{:S(2)}) collective-permute-start(bf16[1040,128]{1,0:T(8,128)(2,1)S(1)} %get-tuple-element.20), channel_id=1, source_target_pairs={{0,8},{1,9},{2,10},{3,11},{4,12},{5,13},{6,14},{7,15},{8,0},{9,1},... | collective-permute-start | bytes 798728 | tf_op jit(solution)/shard_map/ppermute | solution.py:359
  54.2 21.3 %collective-permute-start.14 = (bf16[1040,128]{1,0:T(8,128)(2,1)S(1)}, bf16[1040,128]{1,0:T(8,128)(2,1)S(1)}, u32[]{:S(2)}, u32[]{:S(2)}) collective-permute-start(bf16[1040,128]{1,0:T(8,128)(2,1)S(1)} %get-tuple-element.22), channel_id=1, source_target_pairs={{0,2},{1,3},{2,4},{3,5},{4,6},{5,7},{6,8},{7,9},{8,10},{9,11},{10,... | collective-permute-start | bytes 798728 | tf_op jit(solution)/shard_map/ppermute | solution.py:359
  56.7 23.6 %collective-permute-start.16 = (bf16[1040,128]{1,0:T(8,128)(2,1)S(1)}, bf16[1040,128]{1,0:T(8,128)(2,1)S(1)}, u32[]{:S(2)}, u32[]{:S(2)}) collective-permute-start(bf16[1040,128]{1,0:T(8,128)(2,1)S(1)} %get-tuple-element.23), channel_id=1, source_target_pairs={{0,14},{1,15},{2,0},{3,1},{4,2},{5,3},{6,4},{7,5},{8,6},{9,7},{10,... | collective-permute-start | bytes 798728 | tf_op jit(solution)/shard_map/ppermute | solution.py:359
  58.0 25.9 %collective-permute-start.18 = (bf16[1040,128]{1,0:T(8,128)(2,1)S(1)}, bf16[1040,128]{1,0:T(8,128)(2,1)}, u32[]{:S(2)}, u32[]{:S(2)}) collective-permute-start(bf16[1040,128]{1,0:T(8,128)(2,1)S(1)} %get-tuple-element.24), channel_id=1, source_target_pairs={{0,4},{1,5},{2,6},{3,7},{4,8},{5,9},{6,10},{7,11},{8,12},{9,13},{1... | collective-permute-start | bytes 798728 | tf_op jit(solution)/shard_map/ppermute | solution.py:359
  66.2 23.6 %collective-permute-start.13 = (bf16[1040,128]{1,0:T(8,128)(2,1)S(1)}, bf16[1040,128]{1,0:T(8,128)(2,1)}, u32[]{:S(2)}, u32[]{:S(2)}) collective-permute-start(bf16[1040,128]{1,0:T(8,128)(2,1)S(1)} %get-tuple-element.21.refs_0_), channel_id=1, source_target_pairs={{0,1},{1,0},{2,3},{3,2},{4,5},{5,4},{6,7},{7,6},{8,9},{9,8},{10,11... | collective-permute-start | bytes 798728 | tf_op jit(solution)/shard_map/ppermute | solution.py:365
  75.4 14.4 %collective-permute-start.21 = (bf16[1040,128]{1,0:T(8,128)(2,1)S(1)}, bf16[1040,128]{1,0:T(8,128)(2,1)S(1)}, u32[]{:S(2)}, u32[]{:S(2)}) collective-permute-start(bf16[1040,128]{1,0:T(8,128)(2,1)S(1)} %collective-permute-done.20.refs_8_), channel_id=1, source_target_pairs={{0,1},{1,0},{2,3},{3,2},{4,5},{5,4},{6,7},{7,6},{8,9},{9,8},{10,11... | collective-permute-start | bytes 798728 | tf_op jit(solution)/shard_map/ppermute | solution.py:365
  80.3 10.2 %collective-permute-start.15 = (bf16[1040,128]{1,0:T(8,128)(2,1)S(1)}, bf16[1040,128]{1,0:T(8,128)(2,1)S(1)}, u32[]{:S(2)}, u32[]{:S(2)}) collective-permute-start(bf16[1040,128]{1,0:T(8,128)(2,1)S(1)} %collective-permute-done.14.refs_2_), channel_id=1, source_target_pairs={{0,1},{1,0},{2,3},{3,2},{4,5},{5,4},{6,7},{7,6},{8,9},{9,8},{10,11... | collective-permute-start | bytes 798728 | tf_op jit(solution)/shard_map/ppermute | solution.py:365
  83.9 7.2 %collective-permute-start.17 = (bf16[1040,128]{1,0:T(8,128)(2,1)S(1)}, bf16[1040,128]{1,0:T(8,128)(2,1)S(1)}, u32[]{:S(2)}, u32[]{:S(2)}) collective-permute-start(bf16[1040,128]{1,0:T(8,128)(2,1)S(1)} %collective-permute-done.16.refs_4_), channel_id=1, source_target_pairs={{0,1},{1,0},{2,3},{3,2},{4,5},{5,4},{6,7},{7,6},{8,9},{9,8},{10,11... | collective-permute-start | bytes 798728 | tf_op jit(solution)/shard_map/ppermute | solution.py:365
  89.8 17.4 %collective-permute-start.1 = (bf16[1040,128]{1,0:T(8,128)(2,1)S(1)}, bf16[1040,128]{1,0:T(8,128)(2,1)S(1)}, u32[]{:S(2)}, u32[]{:S(2)}) collective-permute-start(bf16[1040,128]{1,0:T(8,128)(2,1)S(1)} %collective-permute-done.refs_1_), channel_id=1, source_target_pairs={{0,1},{1,0},{2,3},{3,2},{4,5},{5,4},{6,7},{7,6},{8,9},{9,8},{10,11... | collective-permute-start | bytes 798728 | tf_op jit(solution)/shard_map/ppermute | solution.py:365
  89.9 4.1 %collective-permute-start.19 = (bf16[1040,128]{1,0:T(8,128)(2,1)}, bf16[1040,128]{1,0:T(8,128)(2,1)}, u32[]{:S(2)}, u32[]{:S(2)}) collective-permute-start(bf16[1040,128]{1,0:T(8,128)(2,1)} %collective-permute-done.18.refs_6_), channel_id=1, source_target_pairs={{0,1},{1,0},{2,3},{3,2},{4,5},{5,4},{6,7},{7,6},{8,9},{9,8},{10,11... | collective-permute-start | bytes 798728 | tf_op jit(solution)/shard_map/ppermute | solution.py:365
  90.6 16.7 %collective-permute-start.3 = (bf16[1040,128]{1,0:T(8,128)(2,1)S(1)}, bf16[1040,128]{1,0:T(8,128)(2,1)S(1)}, u32[]{:S(2)}, u32[]{:S(2)}) collective-permute-start(bf16[1040,128]{1,0:T(8,128)(2,1)S(1)} %collective-permute-done.2.refs_3_), channel_id=1, source_target_pairs={{0,1},{1,0},{2,3},{3,2},{4,5},{5,4},{6,7},{7,6},{8,9},{9,8},{10,11... | collective-permute-start | bytes 798728 | tf_op jit(solution)/shard_map/ppermute | solution.py:365
  92.0 15.3 %collective-permute-start.5 = (bf16[1040,128]{1,0:T(8,128)(2,1)S(1)}, bf16[1040,128]{1,0:T(8,128)(2,1)S(1)}, u32[]{:S(2)}, u32[]{:S(2)}) collective-permute-start(bf16[1040,128]{1,0:T(8,128)(2,1)S(1)} %collective-permute-done.4.refs_5_), channel_id=1, source_target_pairs={{0,1},{1,0},{2,3},{3,2},{4,5},{5,4},{6,7},{7,6},{8,9},{9,8},{10,11... | collective-permute-start | bytes 798728 | tf_op jit(solution)/shard_map/ppermute | solution.py:365
  94.0 53.7 %copy-start.5 = (s32[2]{0:T(128)S(1)}, s32[2]{0:T(128)}, u32[]{:S(2)}) copy-start(s32[2]{0:T(128)} %pad_add_fusion.place_ref) | copy-start | bytes 28
  147.1 7.1 %collective-permute-start.22 = (bf16[64,512]{1,0:T(8,128)(2,1)S(1)}, bf16[64,512]{1,0:T(8,128)(2,1)S(1)}, u32[]{:S(2)}, u32[]{:S(2)}) collective-permute-start(bf16[64,512]{1,0:T(8,128)(2,1)S(1)} %combine.1.own_ref), channel_id=1, source_target_pairs={{0,1},{1,0},{2,3},{3,2},{4,5},{5,4},{6,7},{7,6},{8,9},{9,8},{10,11... | collective-permute-start | bytes 196616 | tf_op jit(solution)/shard_map/ppermute | solution.py:365
  (18 other events, 419.1 us)

commit v5 on v4

--- a/solution.py
+++ b/solution.py
@@ -246,12 +246,26 @@
     )(place, *early, *bufs, *queries_t, *(() if first else state))
 
 
-def combine(arrived, query_t, newest_t, heads_dev):
+def combine(place, arrived, query_t, newest_t, weight_own, weight_partner, heads_dev, y_count):
+    width = weight_own.shape[1] // (2 * y_count)
+    depth = weight_own.shape[0]
     parts, _, cols = arrived.shape
     req_rows = cols // heads_dev
     factor = math.log2(math.e) / math.sqrt(HEAD_SIZE)
 
-    def kernel(in_ref, q_ref, new_ref, out_ref):
+    def kernel(place_ref, in_ref, q_ref, new_ref, w_own_ref, w_partner_ref, out_ref, held_ref, sem):
+        core = lax.rem(place_ref[0], 2)
+        copies = []
+        for n in range(y_count):
+            start = pl.multiple_of((2 * n + core) * width, width)
+            for k, ref in enumerate((w_own_ref, w_partner_ref)):
+                copies.append(
+                    pltpu.make_async_copy(
+                        ref.at[:, pl.ds(start, width)], held_ref.at[n, pl.ds(k * depth, depth)], sem.at[2 * n + k]
+                    )
+                )
+        for one in copies:
+            one.start()
         query = q_ref[0:HEAD_SIZE].astype(jnp.float32)
         own = jnp.sum(query * new_ref[0].astype(jnp.float32), axis=0, keepdims=True) * factor
         top = own
@@ -274,51 +288,28 @@
         for h in range(heads_dev):
             one = mix[:, h * req_rows : (h + 1) * req_rows]
             out_ref[:, h * HEAD_SIZE : (h + 1) * HEAD_SIZE] = one.T.astype(jnp.bfloat16)
-
-    return pl.pallas_call(
-        kernel,
-        out_shape=jax.ShapeDtypeStruct((req_rows, heads_dev * HEAD_SIZE), jnp.bfloat16),
-        interpret=INTERPRET,
-        compiler_params=pltpu.CompilerParams(vmem_limit_bytes=GRANT),
-        name="combine",
-    )(arrived, query_t, newest_t)
-
-
-def held_weights(place, weight_own, weight_partner, y_count):
-    width = weight_own.shape[1] // (2 * y_count)
-    depth = weight_own.shape[0]
-
-    def kernel(place_ref, w_own_ref, w_partner_ref, out_ref, sem):
-        core = lax.rem(place_ref[0], 2)
-        copies = []
-        for n in range(y_count):
-            start = pl.multiple_of((2 * n + core) * width, width)
-            for k, ref in enumerate((w_own_ref, w_partner_ref)):
-                copies.append(
-                    pltpu.make_async_copy(
-                        ref.at[:, pl.ds(start, width)], out_ref.at[n, pl.ds(k * depth, depth)], sem.at[2 * n + k]
-                    )
-                )
-        for one in copies:
-            one.start()
         for one in copies:
             one.wait()
 
+    vmem = pl.BlockSpec(memory_space=pltpu.MemorySpace.VMEM)
     anywhere = pl.BlockSpec(memory_space=pltpu.MemorySpace.HBM)
     return pl.pallas_call(
         kernel,
-        out_shape=pltpu.VMEM((y_count, 2 * depth, width), jnp.bfloat16),
+        out_shape=[
+            jax.ShapeDtypeStruct((req_rows, heads_dev * HEAD_SIZE), jnp.bfloat16),
+            pltpu.VMEM((y_count, 2 * depth, width), jnp.bfloat16),
+        ],
         grid_spec=pltpu.PrefetchScalarGridSpec(
             num_scalar_prefetch=1,
             grid=(),
-            in_specs=[anywhere, anywhere],
-            out_specs=pl.BlockSpec(memory_space=pltpu.MemorySpace.VMEM),
+            in_specs=[vmem, vmem, vmem, anywhere, anywhere],
+            out_specs=[vmem, vmem],
             scratch_shapes=[pltpu.SemaphoreType.DMA((2 * y_count,))],
         ),
         interpret=INTERPRET,
         compiler_params=pltpu.CompilerParams(vmem_limit_bytes=GRANT),
-        name="held_weights",
-    )(place, weight_own, weight_partner)
+        name="combine",
+    )(place, arrived, query_t, newest_t, weight_own, weight_partner)
 
 
 def project(mix_own, mix_partner, weights):
@@ -390,9 +381,8 @@
             place, bufs, queries_t, state, shifts, y_count, group_count, 4, n == 0, last, (newest_t,) if last else ()
         )
     arrived = lax.all_to_all(state[0], "grp", split_axis=0, concat_axis=0, tiled=True)
-    weights = held_weights(place, out_weight, weight_partner, y_count)
-
-    mix_own = combine(arrived, query_t, newest_t, heads_dev)
+
+    mix_own, weights = combine(place, arrived, query_t, newest_t, out_weight, weight_partner, heads_dev, y_count)
     mix_partner = to_other_core(mix_own)
     partial = project(mix_own, mix_partner, weights)
     same_core = [[2 * i + c for i in range(y_count)] for c in range(2)]

time: 177 us -> 178 us (level)
  transfers between devices with their start and end apart: 24 -> 24, of which waited for: 6 -> 7; matrix products, arithmetic and copies ran while one was open for 2% -> 2% of each run, Pallas kernels for 17% -> 16%
where the time goes in v5:
time: 178 us; the launch traced here: 177 us
  starting transfers between devices  62.3 us (35%)
  blocking collectives  46.8 us (26%)
  Pallas kernels  32.2 us (18%)
  waiting for transfers between devices  25.5 us (14%)
  local copies, waits for them, and re-layouts  8.17 us (5%)
  other arithmetic  2.17 us (1%)
    ppermute x10, starting transfers between devices, to_other_core(): return lax.ppermute(x, 'tp', swap)  42.7 us
    all_to_all x1, blocking collectives, per_device_inner(): lax.all_to_all(state[0], 'grp', split_axis=0, concat_axis=0, tiled=True)  26.4 us
    pallas_call x2, Pallas kernels, attend_chunk(): pl.pallas_call(kernel, out_shape=out_shape, grid_spec=pltpu.PrefetchScala...  25.4 us
    all_to_all x1, blocking collectives, per_device_inner(): lax.all_to_all(partial, 'tp', split_axis=0, concat_axis=0, axis_index_gro...  20.4 us
    ppermute x7, waiting for transfers between devices, along_x(): lax.ppermute(x, 'grp', [(i, (i + shift) % group_count) for i in range(gro...  15.4 us
    ppermute x7, starting transfers between devices, along_y(): lax.ppermute(x, 'tp', [(i, (i + 2 * shift) % tp_count) for i in range(tp_...  10.4 us
    ppermute x7, starting transfers between devices, along_x(): lax.ppermute(x, 'grp', [(i, (i + shift) % group_count) for i in range(gro...  9.25 us
    ppermute x7, waiting for transfers between devices, along_y(): lax.ppermute(x, 'tp', [(i, (i + 2 * shift) % tp_count) for i in range(tp_...  9.13 us
  transfers between devices with their start and end apart: 24, of which 7 were waited for; matrix products, arithmetic and copies ran while one was open for 2% of the time, Pallas kernels for 16%

profile of v5, /device:TPU:513, one launch (start us, length us, event | category | flops | bytes accessed | tf_op | source)
XLA Modules:
  0.0 177.4 jit_solution(3793402950864131679)
XLA Ops:
  0.0 20.4 %collective-permute-start.22 = (bf16[512,8192]{1,0:T(8,128)(2,1)}, bf16[512,8192]{1,0:T(8,128)(2,1)}, u32[]{:S(2)}, u32[]{:S(2)}) collective-permute-start(bf16[512,8192]{1,0:T(8,128)(2,1)} %w_own_ref.1), channel_id=1, source_target_pairs={{0,1},{1,0},{2,3},{3,2},{4,5},{5,4},{6,7},{7,6},{8,9},{9,8},{10,11... | collective-permute-start | bytes 25165832 | tf_op jit(solution)/shard_map/ppermute | solution.py:356
  20.4 2.2 %prepare.1.refs_10_.refs_7_.q_ref = bf16[144,256]{1,0:T(8,128)(2,1)} custom-call(bf16[64,512]{1,0:T(8,128)(2,1)} %q_ref.1, s32[8,64]{1,0:T(8,128)} %bitcast.26, s32[1,64]{1,0:T(1,128)} %bitcast.27), custom_call_target="tpu_custom_call" | custom-call | tf_op jit(solution)/shard_map/prepare/pallas_call | solution.py:54
  22.8 5.5 %collective-permute-start.9 = (bf16[144,256]{1,0:T(8,128)(2,1)}, bf16[144,256]{1,0:T(8,128)(2,1)S(1)}, u32[]{:S(2)}, u32[]{:S(2)}) collective-permute-start(bf16[144,256]{1,0:T(8,128)(2,1)} %prepare.1.refs_10_.refs_7_.q_ref), channel_id=1, source_target_pairs={{0,64},{16,80},{32,96},{48,112},{64,0},{80,16},{96,32},{112,48},{1... | collective-permute-start | bytes 221192 | tf_op jit(solution)/shard_map/ppermute | solution.py:353
  28.2 0.7 convert_element_type.18
  29.1 1.7 constant_dynamic-slice_fusion
  31.3 0.7 collective-permute-done.10.refs_15_.refs_12_
  32.0 3.8 %collective-permute-start.2 = (bf16[1040,128]{1,0:T(8,128)(2,1)S(1)}, bf16[1040,128]{1,0:T(8,128)(2,1)S(1)}, u32[]{:S(2)}, u32[]{:S(2)}) collective-permute-start(bf16[1040,128]{1,0:T(8,128)(2,1)S(1)} %get-tuple-element.23), channel_id=1, source_target_pairs={{0,10},{1,11},{2,12},{3,13},{4,14},{5,15},{6,0},{7,1},{8,2},{9,3},... | collective-permute-start | bytes 798728 | tf_op jit(solution)/shard_map/ppermute | solution.py:350
  35.9 8.1 %collective-permute-done.8.refs_13_.refs_10_ = bf16[144,256]{1,0:T(8,128)(2,1)S(1)} collective-permute-done((bf16[144,256]{1,0:T(8,128)(2,1)S(1)}, bf16[144,256]{1,0:T(8,128)(2,1)S(1)}, u32[]{:S(2)}, u32[]{:S(2)}) %collective-permute-start.8) | collective-permute-done | bytes 73760 | tf_op jit(solution)/shard_map/ppermute | solution.py:353
  44.0 3.3 %collective-permute-start.7 = (bf16[144,256]{1,0:T(8,128)(2,1)S(1)}, bf16[144,256]{1,0:T(8,128)(2,1)S(1)}, u32[]{:S(2)}, u32[]{:S(2)}) collective-permute-start(bf16[144,256]{1,0:T(8,128)(2,1)S(1)} %copy-done.3), channel_id=1, source_target_pairs={{0,32},{16,48},{32,64},{48,80},{64,96},{80,112},{96,0},{112,16},{1... | collective-permute-start | bytes 221192 | tf_op jit(solution)/shard_map/ppermute | solution.py:353
  47.3 2.3 %collective-permute-done.7.refs_12_.refs_9_ = bf16[144,256]{1,0:T(8,128)(2,1)S(1)} collective-permute-done((bf16[144,256]{1,0:T(8,128)(2,1)S(1)}, bf16[144,256]{1,0:T(8,128)(2,1)S(1)}, u32[]{:S(2)}, u32[]{:S(2)}) %collective-permute-start.7) | collective-permute-done | bytes 73760 | tf_op jit(solution)/shard_map/ppermute | solution.py:353
  49.8 4.3 %collective-permute-done.6.refs_11_.refs_8_ = bf16[144,256]{1,0:T(8,128)(2,1)S(1)} collective-permute-done((bf16[144,256]{1,0:T(8,128)(2,1)S(1)}, bf16[144,256]{1,0:T(8,128)(2,1)S(1)}, u32[]{:S(2)}, u32[]{:S(2)}) %collective-permute-start.6) | collective-permute-done | bytes 73760 | tf_op jit(solution)/shard_map/ppermute | solution.py:353
  54.2 2.5 %collective-permute-start.14 = (bf16[1040,128]{1,0:T(8,128)(2,1)S(1)}, bf16[1040,128]{1,0:T(8,128)(2,1)S(1)}, u32[]{:S(2)}, u32[]{:S(2)}) collective-permute-start(bf16[1040,128]{1,0:T(8,128)(2,1)S(1)} %get-tuple-element.26), channel_id=1, source_target_pairs={{0,2},{1,3},{2,4},{3,5},{4,6},{5,7},{6,8},{7,9},{8,10},{9,11},{10,... | collective-permute-start | bytes 798728 | tf_op jit(solution)/shard_map/ppermute | solution.py:350
  56.7 1.3 collective-permute-start.16
  58.0 2.6 %collective-permute-start.18 = (bf16[1040,128]{1,0:T(8,128)(2,1)S(1)}, bf16[1040,128]{1,0:T(8,128)(2,1)}, u32[]{:S(2)}, u32[]{:S(2)}) collective-permute-start(bf16[1040,128]{1,0:T(8,128)(2,1)S(1)} %get-tuple-element.28), channel_id=1, source_target_pairs={{0,4},{1,5},{2,6},{3,7},{4,8},{5,9},{6,10},{7,11},{8,12},{9,13},{1... | collective-permute-start | bytes 798728 | tf_op jit(solution)/shard_map/ppermute | solution.py:350
  60.5 5.7 %collective-permute-done.4.refs_5_ = bf16[1040,128]{1,0:T(8,128)(2,1)S(1)} collective-permute-done((bf16[1040,128]{1,0:T(8,128)(2,1)S(1)}, bf16[1040,128]{1,0:T(8,128)(2,1)S(1)}, u32[]{:S(2)}, u32[]{:S(2)}) %collective-permute-start.4) | collective-permute-done | bytes 266272 | tf_op jit(solution)/shard_map/ppermute | solution.py:350
  66.2 9.2 %collective-permute-start.13 = (bf16[1040,128]{1,0:T(8,128)(2,1)S(1)}, bf16[1040,128]{1,0:T(8,128)(2,1)}, u32[]{:S(2)}, u32[]{:S(2)}) collective-permute-start(bf16[1040,128]{1,0:T(8,128)(2,1)S(1)} %get-tuple-element.25.refs_0_), channel_id=1, source_target_pairs={{0,1},{1,0},{2,3},{3,2},{4,5},{5,4},{6,7},{7,6},{8,9},{9,8},{10,11... | collective-permute-start | bytes 798728 | tf_op jit(solution)/shard_map/ppermute | solution.py:356
  75.4 4.9 %collective-permute-start.21 = (bf16[1040,128]{1,0:T(8,128)(2,1)S(1)}, bf16[1040,128]{1,0:T(8,128)(2,1)S(1)}, u32[]{:S(2)}, u32[]{:S(2)}) collective-permute-start(bf16[1040,128]{1,0:T(8,128)(2,1)S(1)} %collective-permute-done.20.refs_8_), channel_id=1, source_target_pairs={{0,1},{1,0},{2,3},{3,2},{4,5},{5,4},{6,7},{7,6},{8,9},{9,8},{10,11... | collective-permute-start | bytes 798728 | tf_op jit(solution)/shard_map/ppermute | solution.py:356
  80.5 3.4 %collective-permute-done.18.refs_6_ = bf16[1040,128]{1,0:T(8,128)(2,1)} collective-permute-done((bf16[1040,128]{1,0:T(8,128)(2,1)S(1)}, bf16[1040,128]{1,0:T(8,128)(2,1)}, u32[]{:S(2)}, u32[]{:S(2)}) %collective-permute-start.18) | collective-permute-done | bytes 266272 | tf_op jit(solution)/shard_map/ppermute | solution.py:350
  83.9 5.9 %collective-permute-start.17 = (bf16[1040,128]{1,0:T(8,128)(2,1)S(1)}, bf16[1040,128]{1,0:T(8,128)(2,1)S(1)}, u32[]{:S(2)}, u32[]{:S(2)}) collective-permute-start(bf16[1040,128]{1,0:T(8,128)(2,1)S(1)} %collective-permute-done.16.refs_4_), channel_id=1, source_target_pairs={{0,1},{1,0},{2,3},{3,2},{4,5},{5,4},{6,7},{7,6},{8,9},{9,8},{10,11... | collective-permute-start | bytes 798728 | tf_op jit(solution)/shard_map/ppermute | solution.py:356
  91.3 0.7 copy-done.25
  92.6 0.8 copy.12.refs_0_.new_ref
  93.3 0.6 pad_add_fusion.place_ref
  94.1 13.1 %shard_map.73 = (f32[8,128,256]{2,1,0:T(8,128)}, f32[8,8,256]{2,1,0:T(8,128)}) custom-call(s32[2]{0:T(128)} %pad_add_fusion.place_ref, bf16[1040,128]{1,0:T(8,128)(2,1)} %copy-done.6, bf16[1040,128]{1,0:T(8,128)(2,1)} %collective-permute-done.13.refs_1_, bf16[1040,128]{1,0:T(8,128)(2,1)} %copy-done.21, bf16[1040,128]{1,0:T(8,128)(2,1)} %copy-done.24, ...), custom_call_target="tpu_custom_call" | custom-call | tf_op jit(solution)/shard_map/pallas_call | solution.py:235
  107.3 0.6 copy-done.17
  108.1 12.2 %shard_map.74 = bf16[8,144,256]{2,1,0:T(8,128)(2,1)} custom-call(s32[2]{0:T(128)} %pad_add_fusion.place_ref, bf16[2,128,256]{2,1,0:T(8,128)(2,1)} %copy.12.refs_0_.new_ref, bf16[1040,128]{1,0:T(8,128)(2,1)} %copy-done.14, bf16[1040,128]{1,0:T(8,128)(2,1)} %copy-done.17, bf16[1040,128]{1,0:T(8,128)(2,1)} %copy-done.15, bf16[1040,128]{1,0:T(8,128)(2,1)} %copy-done.18, ...), custom_call_target="tpu_custom_call" | custom-call | tf_op jit(solution)/shard_map/pallas_call | solution.py:235
  120.4 26.4 %all_to_all.10.in_ref = bf16[8,144,256]{2,1,0:T(8,128)(2,1)S(1)} all-to-all(bf16[8,144,256]{2,1,0:T(8,128)(2,1)} %shard_map.74), channel_id=1, replica_groups=mesh['rep'=2,'grp'=8,'tp'=16] {'grp'}, dimensions={0} | all-to-all | bytes 1179648 | tf_op jit(solution)/shard_map/all_to_all | solution.py:383
  146.8 3.4 %copy-done.1 = bf16[512,8192]{1,0:T(8,128)(2,1)S(1)} copy-done((bf16[512,8192]{1,0:T(8,128)(2,1)S(1)}, bf16[512,8192]{1,0:T(8,128)(2,1)}, u32[]{:S(2)}) %copy-start.1) | copy-done | bytes 8388632
  150.2 3.1 %combine.1 = (bf16[64,512]{1,0:T(8,128)(2,1)S(1)}, bf16[8,1024,512]{2,1,0:T(8,128)(2,1)S(1)}) custom-call(s32[2]{0:T(128)S(1)} %copy-done.5, bf16[8,144,256]{2,1,0:T(8,128)(2,1)S(1)} %all_to_all.10.in_ref, bf16[144,256]{1,0:T(8,128)(2,1)S(1)} %copy-done.4, bf16[2,128,256]{2,1,0:T(8,128)(2,1)S(1)} %copy-done.2, bf16[512,8192]{1,0:T(8,128)(2,1)S(1)} %copy-done.1, ...), custom_call_target="tpu_custom_call" | custom-call | tf_op jit(solution)/shard_map/combine/pallas_call | solution.py:296
  153.9 0.9 collective-permute-done.23.partner_ref
  154.8 1.6 project.1
  156.3 20.4 %all_to_all.11 = bf16[8,64,512]{2,1,0:T(8,128)(2,1)S(1)} all-to-all(bf16[8,64,512]{2,1,0:T(8,128)(2,1)S(1)} %project.1), channel_id=1, replica_groups={{0,2,4,6,8,10,12,14},{1,3,5,7,9,11,13,15},{16,18,20,22,24,26,28,30},{17..., dimensions={0} | all-to-all | bytes 1048576 | tf_op jit(solution)/shard_map/all_to_all | solution.py:389
  176.7 0.7 reduce_sum.12
  (86 shorter events, 4.1 us)
Async XLA Ops:
  0.0 92.5 %copy-start = (bf16[64,2,1024]{2,1,0:T(2,128)(2,1)S(1)}, bf16[64,2,1024]{2,1,0:T(2,128)(2,1)}, u32[]{:S(2)}) copy-start(bf16[64,2,1024]{2,1,0:T(2,128)(2,1)} %param.8) | copy-start | bytes 786436
  0.0 146.8 %collective-permute-start.22 = (bf16[512,8192]{1,0:T(8,128)(2,1)}, bf16[512,8192]{1,0:T(8,128)(2,1)}, u32[]{:S(2)}, u32[]{:S(2)}) collective-permute-start(bf16[512,8192]{1,0:T(8,128)(2,1)} %w_own_ref.1), channel_id=1, source_target_pairs={{0,1},{1,0},{2,3},{3,2},{4,5},{5,4},{6,7},{7,6},{8,9},{9,8},{10,11... | collective-permute-start | bytes 25165832 | tf_op jit(solution)/shard_map/ppermute | solution.py:356
  22.6 8.4 %collective-permute-start.12 = (bf16[144,256]{1,0:T(8,128)(2,1)}, bf16[144,256]{1,0:T(8,128)(2,1)S(1)}, u32[]{:S(2)}, u32[]{:S(2)}) collective-permute-start(bf16[144,256]{1,0:T(8,128)(2,1)} %prepare.1.refs_10_.refs_7_.q_ref), channel_id=1, source_target_pairs={{0,112},{16,0},{32,16},{48,32},{64,48},{80,64},{96,80},{112,96},{1... | collective-permute-start | bytes 221192 | tf_op jit(solution)/shard_map/ppermute | solution.py:353
  22.6 8.6 %collective-permute-start.11 = (bf16[144,256]{1,0:T(8,128)(2,1)}, bf16[144,256]{1,0:T(8,128)(2,1)S(1)}, u32[]{:S(2)}, u32[]{:S(2)}) collective-permute-start(bf16[144,256]{1,0:T(8,128)(2,1)} %prepare.1.refs_10_.refs_7_.q_ref), channel_id=1, source_target_pairs={{0,96},{16,112},{32,0},{48,16},{64,32},{80,48},{96,64},{112,80},{1... | collective-permute-start | bytes 221192 | tf_op jit(solution)/shard_map/ppermute | solution.py:353
  22.6 9.4 %collective-permute-start.10 = (bf16[144,256]{1,0:T(8,128)(2,1)}, bf16[144,256]{1,0:T(8,128)(2,1)S(1)}, u32[]{:S(2)}, u32[]{:S(2)}) collective-permute-start(bf16[144,256]{1,0:T(8,128)(2,1)} %prepare.1.refs_10_.refs_7_.q_ref), channel_id=1, source_target_pairs={{0,80},{16,96},{32,112},{48,0},{64,16},{80,32},{96,48},{112,64},{1... | collective-permute-start | bytes 221192 | tf_op jit(solution)/shard_map/ppermute | solution.py:353
  22.8 13.1 %collective-permute-start.9 = (bf16[144,256]{1,0:T(8,128)(2,1)}, bf16[144,256]{1,0:T(8,128)(2,1)S(1)}, u32[]{:S(2)}, u32[]{:S(2)}) collective-permute-start(bf16[144,256]{1,0:T(8,128)(2,1)} %prepare.1.refs_10_.refs_7_.q_ref), channel_id=1, source_target_pairs={{0,64},{16,80},{32,96},{48,112},{64,0},{80,16},{96,32},{112,48},{1... | collective-permute-start | bytes 221192 | tf_op jit(solution)/shard_map/ppermute | solution.py:353
  29.1 117.7 %copy-start.4 = (bf16[144,256]{1,0:T(8,128)(2,1)S(1)}, bf16[144,256]{1,0:T(8,128)(2,1)}, u32[]{:S(2)}) copy-start(bf16[144,256]{1,0:T(8,128)(2,1)} %prepare.1.refs_10_.refs_7_.q_ref) | copy-start | bytes 221188
  31.0 63.0 %copy-start.6 = (bf16[1040,128]{1,0:T(8,128)(2,1)}, bf16[1040,128]{1,0:T(8,128)(2,1)S(1)}, u32[]{:S(2)}) copy-start(bf16[1040,128]{1,0:T(8,128)(2,1)S(1)} %get-tuple-element.25.refs_0_) | copy-start | bytes 798724
  31.0 62.9 %copy-start.7 = (bf16[144,256]{1,0:T(8,128)(2,1)}, bf16[144,256]{1,0:T(8,128)(2,1)S(1)}, u32[]{:S(2)}) copy-start(bf16[144,256]{1,0:T(8,128)(2,1)S(1)} %collective-permute-done.12.refs_17_.refs_14_) | copy-start | bytes 221188
  31.0 23.1 %collective-permute-start.20 = (bf16[1040,128]{1,0:T(8,128)(2,1)S(1)}, bf16[1040,128]{1,0:T(8,128)(2,1)S(1)}, u32[]{:S(2)}, u32[]{:S(2)}) collective-permute-start(bf16[1040,128]{1,0:T(8,128)(2,1)S(1)} %get-tuple-element.21), channel_id=1, source_target_pairs={{0,12},{1,13},{2,14},{3,15},{4,0},{5,1},{6,2},{7,3},{8,4},{9,5},{1... | collective-permute-start | bytes 798728 | tf_op jit(solution)/shard_map/ppermute | solution.py:350
  31.2 62.8 %copy-start.8 = (bf16[144,256]{1,0:T(8,128)(2,1)}, bf16[144,256]{1,0:T(8,128)(2,1)S(1)}, u32[]{:S(2)}) copy-start(bf16[144,256]{1,0:T(8,128)(2,1)S(1)} %collective-permute-done.11.refs_16_.refs_13_) | copy-start | bytes 221188
  31.2 25.5 %collective-permute-start = (bf16[1040,128]{1,0:T(8,128)(2,1)S(1)}, bf16[1040,128]{1,0:T(8,128)(2,1)S(1)}, u32[]{:S(2)}, u32[]{:S(2)}) collective-permute-start(bf16[1040,128]{1,0:T(8,128)(2,1)S(1)} %get-tuple-element.22), channel_id=1, source_target_pairs={{0,6},{1,7},{2,8},{3,9},{4,10},{5,11},{6,12},{7,13},{8,14},{9,15},... | collective-permute-start | bytes 798728 | tf_op jit(solution)/shard_map/ppermute | solution.py:350
  32.0 62.0 %copy-start.9 = (bf16[144,256]{1,0:T(8,128)(2,1)}, bf16[144,256]{1,0:T(8,128)(2,1)S(1)}, u32[]{:S(2)}) copy-start(bf16[144,256]{1,0:T(8,128)(2,1)S(1)} %collective-permute-done.10.refs_15_.refs_12_) | copy-start | bytes 221188
  32.0 25.9 %collective-permute-start.2 = (bf16[1040,128]{1,0:T(8,128)(2,1)S(1)}, bf16[1040,128]{1,0:T(8,128)(2,1)S(1)}, u32[]{:S(2)}, u32[]{:S(2)}) collective-permute-start(bf16[1040,128]{1,0:T(8,128)(2,1)S(1)} %get-tuple-element.23), channel_id=1, source_target_pairs={{0,10},{1,11},{2,12},{3,13},{4,14},{5,15},{6,0},{7,1},{8,2},{9,3},... | collective-permute-start | bytes 798728 | tf_op jit(solution)/shard_map/ppermute | solution.py:350
  35.8 58.2 %copy-start.10 = (bf16[144,256]{1,0:T(8,128)(2,1)}, bf16[144,256]{1,0:T(8,128)(2,1)S(1)}, u32[]{:S(2)}) copy-start(bf16[144,256]{1,0:T(8,128)(2,1)S(1)} %collective-permute-done.9.refs_14_.refs_11_) | copy-start | bytes 221188
  35.8 8.2 %collective-permute-start.8 = (bf16[144,256]{1,0:T(8,128)(2,1)S(1)}, bf16[144,256]{1,0:T(8,128)(2,1)S(1)}, u32[]{:S(2)}, u32[]{:S(2)}) collective-permute-start(bf16[144,256]{1,0:T(8,128)(2,1)S(1)} %copy-done.3), channel_id=1, source_target_pairs={{0,48},{16,64},{32,80},{48,96},{64,112},{80,0},{96,16},{112,32},{1... | collective-permute-start | bytes 221192 | tf_op jit(solution)/shard_map/ppermute | solution.py:353
  44.0 5.6 %collective-permute-start.7 = (bf16[144,256]{1,0:T(8,128)(2,1)S(1)}, bf16[144,256]{1,0:T(8,128)(2,1)S(1)}, u32[]{:S(2)}, u32[]{:S(2)}) collective-permute-start(bf16[144,256]{1,0:T(8,128)(2,1)S(1)} %copy-done.3), channel_id=1, source_target_pairs={{0,32},{16,48},{32,64},{48,80},{64,96},{80,112},{96,0},{112,16},{1... | collective-permute-start | bytes 221192 | tf_op jit(solution)/shard_map/ppermute | solution.py:353
  49.7 4.5 %collective-permute-start.6 = (bf16[144,256]{1,0:T(8,128)(2,1)S(1)}, bf16[144,256]{1,0:T(8,128)(2,1)S(1)}, u32[]{:S(2)}, u32[]{:S(2)}) collective-permute-start(bf16[144,256]{1,0:T(8,128)(2,1)S(1)} %copy-done.3), channel_id=1, source_target_pairs={{0,16},{16,32},{32,48},{48,64},{64,80},{80,96},{96,112},{112,0},{1... | collective-permute-start | bytes 221192 | tf_op jit(solution)/shard_map/ppermute | solution.py:353
  54.1 12.1 %collective-permute-start.4 = (bf16[1040,128]{1,0:T(8,128)(2,1)S(1)}, bf16[1040,128]{1,0:T(8,128)(2,1)S(1)}, u32[]{:S(2)}, u32[]{:S(2)}) collective-permute-start(bf16[1040,128]{1,0:T(8,128)(2,1)S(1)} %get-tuple-element.24), channel_id=1, source_target_pairs={{0,8},{1,9},{2,10},{3,11},{4,12},{5,13},{6,14},{7,15},{8,0},{9,1},... | collective-permute-start | bytes 798728 | tf_op jit(solution)/shard_map/ppermute | solution.py:350
  54.2 21.3 %collective-permute-start.14 = (bf16[1040,128]{1,0:T(8,128)(2,1)S(1)}, bf16[1040,128]{1,0:T(8,128)(2,1)S(1)}, u32[]{:S(2)}, u32[]{:S(2)}) collective-permute-start(bf16[1040,128]{1,0:T(8,128)(2,1)S(1)} %get-tuple-element.26), channel_id=1, source_target_pairs={{0,2},{1,3},{2,4},{3,5},{4,6},{5,7},{6,8},{7,9},{8,10},{9,11},{10,... | collective-permute-start | bytes 798728 | tf_op jit(solution)/shard_map/ppermute | solution.py:350
  56.7 23.6 %collective-permute-start.16 = (bf16[1040,128]{1,0:T(8,128)(2,1)S(1)}, bf16[1040,128]{1,0:T(8,128)(2,1)S(1)}, u32[]{:S(2)}, u32[]{:S(2)}) collective-permute-start(bf16[1040,128]{1,0:T(8,128)(2,1)S(1)} %get-tuple-element.27), channel_id=1, source_target_pairs={{0,14},{1,15},{2,0},{3,1},{4,2},{5,3},{6,4},{7,5},{8,6},{9,7},{10,... | collective-permute-start | bytes 798728 | tf_op jit(solution)/shard_map/ppermute | solution.py:350
  58.0 25.9 %collective-permute-start.18 = (bf16[1040,128]{1,0:T(8,128)(2,1)S(1)}, bf16[1040,128]{1,0:T(8,128)(2,1)}, u32[]{:S(2)}, u32[]{:S(2)}) collective-permute-start(bf16[1040,128]{1,0:T(8,128)(2,1)S(1)} %get-tuple-element.28), channel_id=1, source_target_pairs={{0,4},{1,5},{2,6},{3,7},{4,8},{5,9},{6,10},{7,11},{8,12},{9,13},{1... | collective-permute-start | bytes 798728 | tf_op jit(solution)/shard_map/ppermute | solution.py:350
  66.2 23.6 %collective-permute-start.13 = (bf16[1040,128]{1,0:T(8,128)(2,1)S(1)}, bf16[1040,128]{1,0:T(8,128)(2,1)}, u32[]{:S(2)}, u32[]{:S(2)}) collective-permute-start(bf16[1040,128]{1,0:T(8,128)(2,1)S(1)} %get-tuple-element.25.refs_0_), channel_id=1, source_target_pairs={{0,1},{1,0},{2,3},{3,2},{4,5},{5,4},{6,7},{7,6},{8,9},{9,8},{10,11... | collective-permute-start | bytes 798728 | tf_op jit(solution)/shard_map/ppermute | solution.py:356
  75.4 14.4 %collective-permute-start.21 = (bf16[1040,128]{1,0:T(8,128)(2,1)S(1)}, bf16[1040,128]{1,0:T(8,128)(2,1)S(1)}, u32[]{:S(2)}, u32[]{:S(2)}) collective-permute-start(bf16[1040,128]{1,0:T(8,128)(2,1)S(1)} %collective-permute-done.20.refs_8_), channel_id=1, source_target_pairs={{0,1},{1,0},{2,3},{3,2},{4,5},{5,4},{6,7},{7,6},{8,9},{9,8},{10,11... | collective-permute-start | bytes 798728 | tf_op jit(solution)/shard_map/ppermute | solution.py:356
  80.3 10.2 %collective-permute-start.15 = (bf16[1040,128]{1,0:T(8,128)(2,1)S(1)}, bf16[1040,128]{1,0:T(8,128)(2,1)S(1)}, u32[]{:S(2)}, u32[]{:S(2)}) collective-permute-start(bf16[1040,128]{1,0:T(8,128)(2,1)S(1)} %collective-permute-done.14.refs_2_), channel_id=1, source_target_pairs={{0,1},{1,0},{2,3},{3,2},{4,5},{5,4},{6,7},{7,6},{8,9},{9,8},{10,11... | collective-permute-start | bytes 798728 | tf_op jit(solution)/shard_map/ppermute | solution.py:356
  83.9 7.2 %collective-permute-start.17 = (bf16[1040,128]{1,0:T(8,128)(2,1)S(1)}, bf16[1040,128]{1,0:T(8,128)(2,1)S(1)}, u32[]{:S(2)}, u32[]{:S(2)}) collective-permute-start(bf16[1040,128]{1,0:T(8,128)(2,1)S(1)} %collective-permute-done.16.refs_4_), channel_id=1, source_target_pairs={{0,1},{1,0},{2,3},{3,2},{4,5},{5,4},{6,7},{7,6},{8,9},{9,8},{10,11... | collective-permute-start | bytes 798728 | tf_op jit(solution)/shard_map/ppermute | solution.py:356
  89.8 17.4 %collective-permute-start.1 = (bf16[1040,128]{1,0:T(8,128)(2,1)S(1)}, bf16[1040,128]{1,0:T(8,128)(2,1)S(1)}, u32[]{:S(2)}, u32[]{:S(2)}) collective-permute-start(bf16[1040,128]{1,0:T(8,128)(2,1)S(1)} %collective-permute-done.refs_1_), channel_id=1, source_target_pairs={{0,1},{1,0},{2,3},{3,2},{4,5},{5,4},{6,7},{7,6},{8,9},{9,8},{10,11... | collective-permute-start | bytes 798728 | tf_op jit(solution)/shard_map/ppermute | solution.py:356
  89.9 4.1 %collective-permute-start.19 = (bf16[1040,128]{1,0:T(8,128)(2,1)}, bf16[1040,128]{1,0:T(8,128)(2,1)}, u32[]{:S(2)}, u32[]{:S(2)}) collective-permute-start(bf16[1040,128]{1,0:T(8,128)(2,1)} %collective-permute-done.18.refs_6_), channel_id=1, source_target_pairs={{0,1},{1,0},{2,3},{3,2},{4,5},{5,4},{6,7},{7,6},{8,9},{9,8},{10,11... | collective-permute-start | bytes 798728 | tf_op jit(solution)/shard_map/ppermute | solution.py:356
  90.6 16.7 %collective-permute-start.3 = (bf16[1040,128]{1,0:T(8,128)(2,1)S(1)}, bf16[1040,128]{1,0:T(8,128)(2,1)S(1)}, u32[]{:S(2)}, u32[]{:S(2)}) collective-permute-start(bf16[1040,128]{1,0:T(8,128)(2,1)S(1)} %collective-permute-done.2.refs_3_), channel_id=1, source_target_pairs={{0,1},{1,0},{2,3},{3,2},{4,5},{5,4},{6,7},{7,6},{8,9},{9,8},{10,11... | collective-permute-start | bytes 798728 | tf_op jit(solution)/shard_map/ppermute | solution.py:356
  92.0 15.3 %collective-permute-start.5 = (bf16[1040,128]{1,0:T(8,128)(2,1)S(1)}, bf16[1040,128]{1,0:T(8,128)(2,1)S(1)}, u32[]{:S(2)}, u32[]{:S(2)}) collective-permute-start(bf16[1040,128]{1,0:T(8,128)(2,1)S(1)} %collective-permute-done.4.refs_5_), channel_id=1, source_target_pairs={{0,1},{1,0},{2,3},{3,2},{4,5},{5,4},{6,7},{7,6},{8,9},{9,8},{10,11... | collective-permute-start | bytes 798728 | tf_op jit(solution)/shard_map/ppermute | solution.py:356
  93.3 53.5 %copy-start.2 = (bf16[2,128,256]{2,1,0:T(8,128)(2,1)S(1)}, bf16[2,128,256]{2,1,0:T(8,128)(2,1)}, u32[]{:S(2)}) copy-start(bf16[2,128,256]{2,1,0:T(8,128)(2,1)} %copy.12.refs_0_.new_ref) | copy-start | bytes 393220
  153.3 1.5 collective-permute-start.23
  (18 other events, 418.5 us)
